TPU v7x, 32 devices: a whole 2x2x4 slice. The times are simulated.
32 devices in a mesh: tm: 16 (over z, x, core), space: 2 (over y).
Axes of the slice: x: 2, y: 2, z: 4, core: 2. Of those that a mesh axis runs over, the one named last changes fastest.
Arguments:
- fine_nodes: float32 [16, 3, 3, 32, 4096], P('tm', None, None, 'space'), may hold values from -6 to 6
- init_state: float32 [3, 32, 4096], P(None, 'space'), may hold values from -6 to 6
- mean_depth: float32 [32, 4096], P('space'), may hold values from 0.5 to 2
Outputs:
- new_nodes: float32 [16, 3, 3, 32, 4096], P('tm', None, None, 'space')
All inputs are finite; a program needn't handle non-finite values.
Results may differ from a plain program's by a relative error of at most 0.00002.
Values sent between devices are 32-bit elements; how exact they have to be, the bound alone decides.
No kernel may reach another device: no remote copies, remote signals or barrier semaphores. Data moves between devices by JAX's collectives and lax.ppermute only.
A program may use at most 64 MiB of HBM per device.

v0:
```python
import jax
import jax.numpy as jnp
from jax import lax
from jax.sharding import PartitionSpec as P

step_size = 0.3
viscosity = 1.0 / 3.0
coriolis = 0.5
quad_near = 5.0 / 24.0
quad_mid = 1.0 / 3.0
quad_far = -1.0 / 24.0


def from_behind(value, axis, by):
    peers = lax.axis_size(axis)
    pairs = [(i, i + by) for i in range(peers) if 0 <= i + by < peers]
    return lax.ppermute(value, axis, pairs)


def extended(cells, sides, width):
    for axis, dim in sides:
        count = lax.axis_size(axis)
        head = lax.slice_in_dim(cells, 0, width, axis=dim)
        tail = lax.slice_in_dim(cells, cells.shape[dim] - width, cells.shape[dim], axis=dim)
        cells = jnp.concatenate(
            [
                lax.ppermute(tail, axis, [(i, (i + 1) % count) for i in range(count)]),
                cells,
                lax.ppermute(head, axis, [((i + 1) % count, i) for i in range(count)]),
            ],
            axis=dim,
        )
    return cells


def column_slope(values):
    return (jnp.roll(values, -1, -1) - jnp.roll(values, 1, -1)) * 0.5


def row_slope(values):
    return (values[..., 2:, :] - values[..., :-2, :]) * 0.5


def diffuse(values, centre):
    return (
        values[..., 2:, :]
        + values[..., :-2, :]
        + jnp.roll(centre, -1, -1)
        + jnp.roll(centre, 1, -1)
        - 4.0 * centre
    )


def tendency(padded, depth_rows):
    height = padded[..., 0, :, :]
    east_flow = padded[..., 1, :, :]
    north_flow = padded[..., 2, :, :]
    centre = padded[..., 1:-1, :]
    height_c = centre[..., 0, :, :]
    east_c = centre[..., 1, :, :]
    north_c = centre[..., 2, :, :]
    depth_c = depth_rows[1:-1]
    height_rate = (
        -column_slope(depth_c * east_c)
        - row_slope(depth_rows * north_flow)
        + viscosity * diffuse(height, height_c)
    )
    east_rate = (
        -column_slope(height_c) + coriolis * north_c + viscosity * diffuse(east_flow, east_c)
    )
    north_rate = -row_slope(height) - coriolis * east_c + viscosity * diffuse(north_flow, north_c)
    return jnp.stack([height_rate, east_rate, north_rate], axis=-3)


def per_device(fine_nodes, init_state, mean_depth):
    points = fine_nodes[0]
    row_count = points.shape[-2]
    col_count = points.shape[-1]
    half_step = step_size * 0.5
    is_first = lax.axis_index("tm") == 0
    previous = from_behind(points[2], "tm", 1)
    section_zero = jnp.where(is_first, init_state, previous)
    stacked = jnp.concatenate([points.reshape(9, row_count, col_count), mean_depth[None]], axis=0)
    widened_old = extended(stacked, (("space", 1),), 1)
    depth_rows = widened_old[9]
    old_rates = tendency(widened_old[:9].reshape(3, 3, row_count + 2, col_count), depth_rows)

    def fresh_rate(values):
        return tendency(extended(values, (("space", 1),), 1), depth_rows)

    rate_zero = fresh_rate(section_zero)
    section_one = (
        section_zero
        + half_step * (rate_zero - old_rates[0])
        + step_size * (quad_near * old_rates[0] + quad_mid * old_rates[1] + quad_far * old_rates[2])
    )
    rate_one = fresh_rate(section_one)
    section_two = (
        section_one
        + half_step * (rate_one - old_rates[1])
        + step_size * (quad_far * old_rates[0] + quad_mid * old_rates[1] + quad_near * old_rates[2])
    )
    rate_two = fresh_rate(section_two)
    fas_term = -(step_size / 3.0) * (rate_zero - 2.0 * rate_one + rate_two)
    drift_total = half_step * (rate_two - rate_zero) + fas_term
    boosted = drift_total + jnp.where(is_first, section_zero + step_size * rate_zero, 0.0)
    coarse_end = boosted
    offset = 1
    while offset < lax.axis_size("tm"):

        def one_layer(turn_index, values):
            padded = extended(values, (("space", 1),), 1)
            return values + step_size * tendency(padded, depth_rows)

        powered = lax.fori_loop(0, offset, one_layer, coarse_end)
        coarse_end = coarse_end + from_behind(powered, "tm", offset)
        offset = offset * 2
    previous_end = from_behind(coarse_end, "tm", 1)
    coarse_begin = jnp.where(is_first, init_state, previous_end)
    middle = section_one + 0.5 * (coarse_begin - section_zero + (coarse_end - section_two))
    return jnp.stack([coarse_begin, middle, coarse_end], axis=0)[None]


def solution(mesh):
    placed = (P("tm", None, None, "space", None), P(None, "space", None), P("space", None))
    return jax.shard_map(
        per_device,
        mesh=mesh,
        in_specs=placed,
        out_specs=P("tm", None, None, "space", None),
        check_vma=False,
    )
```

profile of v0, /device:TPU:26, one launch (start us, length us, event | category | flops | bytes accessed | tf_op | source)
XLA Modules:
  0.0 359.5 jit_solution(11264127611526048754)
XLA Ops:
  0.0 2.0 pad_maximum_fusion.46
  4.1 2.1 slice_bitcast_fusion.53
  6.2 1.9 collective-permute-start.6
  9.2 2.4 collective-permute-done.7
  11.6 2.3 pad_maximum_fusion.12
  17.2 2.5 collective-permute-done.6
  22.6 1.9 collective-permute-done.10
  32.6 1.9 collective-permute-done.11
  39.9 2.0 collective-permute-done.13
  47.6 1.9 collective-permute-done.15
  52.8 1.9 collective-permute-start.17
  54.7 11.7 %collective-permute-done.17 = f32[3,16,4096]{2,1,0:T(8,128)} collective-permute-done((f32[3,16,4096]{2,1,0:T(8,128)}, f32[3,16,4096]{2,1,0:T(8,128)}, u32[]{:S(2)}, u32[]{:S(2)}) %collective-permute-start.17) | collective-permute-done | bytes 786464 | tf_op jit(solution)/shard_map/ppermute | solution.py:17
  66.4 2.0 fusion.250
  69.4 29.0 %while.34 = (s32[]{:T(128)}, f32[3,16,4096]{2,1,0:T(8,128)S(1)}, f32[18,4096]{1,0:T(8,128)S(1)}, s32[]{:T(128)}, s32[]{}, /*index=5*/s32[]{}) while((s32[]{:T(128)}, f32[3,16,4096]{2,1,0:T(8,128)S(1)}, f32[18,4096]{1,0:T(8,128)S(1)}, s32[]{:T(128)}, s32[]{}, /*index=5*/s32[]{}) %tuple.247), condition=%wide.region_1.2_spmd, body=%wide.region_0.1_spmd.sunk | while | flops 4415490 | bytes 29294428 | solution.py:115
  76.7 1.8 dynamic-update-slice.16
  78.5 1.6 fusion.278
  91.2 1.8 dynamic-update-slice.16
  93.0 1.6 fusion.278
  99.7 17.0 %collective-permute-done.18 = f32[3,16,4096]{2,1,0:T(8,128)} collective-permute-done((f32[3,16,4096]{2,1,0:T(8,128)S(1)}, f32[3,16,4096]{2,1,0:T(8,128)}, u32[]{:S(2)}, u32[]{:S(2)}) %collective-permute-start.18) | collective-permute-done | bytes 786464 | tf_op jit(solution)/shard_map/ppermute | solution.py:17
  119.1 58.1 %while.35 = (s32[]{:T(128)}, f32[3,16,4096]{2,1,0:T(8,128)S(1)}, f32[18,4096]{1,0:T(8,128)S(1)}, s32[]{:T(128)}, s32[]{}, /*index=5*/s32[]{}) while((s32[]{:T(128)}, f32[3,16,4096]{2,1,0:T(8,128)S(1)}, f32[18,4096]{1,0:T(8,128)S(1)}, s32[]{:T(128)}, s32[]{}, /*index=5*/s32[]{}) %tuple.256), condition=%wide.region_3.4_spmd, body=%wide.region_2.3_spmd.sunk | while | flops 4415490 | bytes 29294428 | solution.py:115
  126.4 1.8 dynamic-update-slice.18
  128.2 1.6 fusion.286
  140.9 1.8 dynamic-update-slice.18
  142.7 1.6 fusion.286
  155.4 1.8 dynamic-update-slice.18
  157.2 1.6 fusion.286
  169.9 1.8 dynamic-update-slice.18
  171.8 1.6 fusion.286
  178.4 16.6 %collective-permute-done.19 = f32[3,16,4096]{2,1,0:T(8,128)S(1)} collective-permute-done((f32[3,16,4096]{2,1,0:T(8,128)S(1)}, f32[3,16,4096]{2,1,0:T(8,128)S(1)}, u32[]{:S(2)}, u32[]{:S(2)}) %collective-permute-start.19) | collective-permute-done | bytes 786464 | tf_op jit(solution)/shard_map/ppermute | solution.py:17
  197.2 116.1 %while.36 = (s32[]{:T(128)}, f32[3,16,4096]{2,1,0:T(8,128)S(1)}, f32[18,4096]{1,0:T(8,128)S(1)}, s32[]{:T(128)}, s32[]{}, /*index=5*/s32[]{}) while((s32[]{:T(128)}, f32[3,16,4096]{2,1,0:T(8,128)S(1)}, f32[18,4096]{1,0:T(8,128)S(1)}, s32[]{:T(128)}, s32[]{}, /*index=5*/s32[]{}) %tuple.257), condition=%wide.region_5.6_spmd, body=%wide.region_4.5_spmd.sunk | while | flops 4415490 | bytes 29294428 | solution.py:115
  204.5 1.8 dynamic-update-slice.20
  206.4 1.6 fusion.294
  219.1 1.8 dynamic-update-slice.20
  220.9 1.6 fusion.294
  233.6 1.8 dynamic-update-slice.20
  235.4 1.6 fusion.294
  248.1 1.8 dynamic-update-slice.20
  249.9 1.6 fusion.294
  262.6 1.8 dynamic-update-slice.20
  264.4 1.6 fusion.294
  277.1 1.8 dynamic-update-slice.20
  278.9 1.6 fusion.294
  291.6 1.8 dynamic-update-slice.20
  293.5 1.6 fusion.294
  306.1 1.8 dynamic-update-slice.20
  314.8 28.3 %collective-permute-done.20 = f32[3,16,4096]{2,1,0:T(8,128)S(1)} collective-permute-done((f32[3,16,4096]{2,1,0:T(8,128)S(1)}, f32[3,16,4096]{2,1,0:T(8,128)S(1)}, u32[]{:S(2)}, u32[]{:S(2)}) %collective-permute-start.20) | collective-permute-done | bytes 786464 | tf_op jit(solution)/shard_map/ppermute | solution.py:17
  344.3 1.9 collective-permute-start.21
  346.2 11.4 %collective-permute-done.21 = f32[3,16,4096]{2,1,0:T(8,128)S(1)} collective-permute-done((f32[3,16,4096]{2,1,0:T(8,128)S(1)}, f32[3,16,4096]{2,1,0:T(8,128)S(1)}, u32[]{:S(2)}, u32[]{:S(2)}) %collective-permute-start.21) | collective-permute-done | bytes 786464 | tf_op jit(solution)/shard_map/ppermute | solution.py:17
  (583 shorter events, 199.5 us)
Async XLA Ops:
  2.1 7.1 %collective-permute-start.8 = (f32[10,1,4096]{2,1,0:T(1,128)S(1)}, f32[10,1,4096]{2,1,0:T(1,128)S(1)}, u32[]{:S(2)}, u32[]{:S(2)}) collective-permute-start(f32[10,1,4096]{2,1,0:T(1,128)S(1)} %get-tuple-element.205), channel_id=1, source_target_pairs={{1,0},{0,1},{3,2},{2,3},{5,4},{4,5},{7,6},{6,7},{9,8},{8,9},{11,10... | collective-permute-start | bytes 491528 | tf_op jit(solution)/shard_map/ppermute | solution.py:29
  3.6 7.9 %collective-permute-start.7 = (f32[10,1,4096]{2,1,0:T(1,128)S(1)}, f32[10,1,4096]{2,1,0:T(1,128)S(1)}, u32[]{:S(2)}, u32[]{:S(2)}) collective-permute-start(f32[10,1,4096]{2,1,0:T(1,128)S(1)} %get-tuple-element.204), channel_id=1, source_target_pairs={{0,1},{1,0},{2,3},{3,2},{4,5},{5,4},{6,7},{7,6},{8,9},{9,8},{10,11... | collective-permute-start | bytes 491528 | tf_op jit(solution)/shard_map/ppermute | solution.py:27
  6.2 13.5 %collective-permute-start.6 = (f32[3,16,4096]{2,1,0:T(8,128)}, f32[3,16,4096]{2,1,0:T(8,128)S(1)}, u32[]{:S(2)}, u32[]{:S(2)}) collective-permute-start(f32[3,16,4096]{2,1,0:T(8,128)} %slice_bitcast_fusion.53), channel_id=1, source_target_pairs={{0,2},{2,4},{4,6},{6,8},{8,10},{10,12},{12,14},{14,16},{16,18},{18... | collective-permute-start | bytes 2359304 | tf_op jit(solution)/shard_map/ppermute | solution.py:17
  20.3 4.2 %collective-permute-start.10 = (f32[3,1,4096]{2,1,0:T(1,128)S(1)}, f32[3,1,4096]{2,1,0:T(1,128)S(1)}, u32[]{:S(2)}, u32[]{:S(2)}) collective-permute-start(f32[3,1,4096]{2,1,0:T(1,128)S(1)} %get-tuple-element.235), channel_id=1, source_target_pairs={{1,0},{0,1},{3,2},{2,3},{5,4},{4,5},{7,6},{6,7},{9,8},{8,9},{11,10... | collective-permute-start | bytes 147464 | tf_op jit(solution)/shard_map/ppermute | solution.py:29
  21.8 4.1 %collective-permute-start.9 = (f32[3,1,4096]{2,1,0:T(1,128)S(1)}, f32[3,1,4096]{2,1,0:T(1,128)S(1)}, u32[]{:S(2)}, u32[]{:S(2)}) collective-permute-start(f32[3,1,4096]{2,1,0:T(1,128)S(1)} %get-tuple-element.234), channel_id=1, source_target_pairs={{0,1},{1,0},{2,3},{3,2},{4,5},{5,4},{6,7},{7,6},{8,9},{9,8},{10,11... | collective-permute-start | bytes 147464 | tf_op jit(solution)/shard_map/ppermute | solution.py:27
  29.4 21.9 %copy-start.20 = (f32[1,16,4096]{2,1,0:T(8,128)}, f32[1,16,4096]{2,1,0:T(8,128)S(1)}, u32[]{:S(2)}) copy-start(f32[1,16,4096]{2,1,0:T(8,128)S(1)} %fusion.170) | copy-start | bytes 786436
  30.3 4.2 %collective-permute-start.11 = (f32[3,1,4096]{2,1,0:T(1,128)S(1)}, f32[3,1,4096]{2,1,0:T(1,128)S(1)}, u32[]{:S(2)}, u32[]{:S(2)}) collective-permute-start(f32[3,1,4096]{2,1,0:T(1,128)S(1)} %get-tuple-element.225), channel_id=1, source_target_pairs={{0,1},{1,0},{2,3},{3,2},{4,5},{5,4},{6,7},{7,6},{8,9},{9,8},{10,11... | collective-permute-start | bytes 147464 | tf_op jit(solution)/shard_map/ppermute | solution.py:27
  30.9 4.7 %collective-permute-start.12 = (f32[3,1,4096]{2,1,0:T(1,128)S(1)}, f32[3,1,4096]{2,1,0:T(1,128)S(1)}, u32[]{:S(2)}, u32[]{:S(2)}) collective-permute-start(f32[3,1,4096]{2,1,0:T(1,128)S(1)} %get-tuple-element.224), channel_id=1, source_target_pairs={{1,0},{0,1},{3,2},{2,3},{5,4},{4,5},{7,6},{6,7},{9,8},{8,9},{11,10... | collective-permute-start | bytes 147464 | tf_op jit(solution)/shard_map/ppermute | solution.py:29
  35.9 15.5 %copy-start.21 = (f32[1,16,4096]{2,1,0:T(8,128)}, f32[1,16,4096]{2,1,0:T(8,128)S(1)}, u32[]{:S(2)}) copy-start(f32[1,16,4096]{2,1,0:T(8,128)S(1)} %get-tuple-element.220) | copy-start | bytes 786436
  36.4 14.9 %copy-start.22 = (f32[1,16,4096]{2,1,0:T(8,128)}, f32[1,16,4096]{2,1,0:T(8,128)S(1)}, u32[]{:S(2)}) copy-start(f32[1,16,4096]{2,1,0:T(8,128)S(1)} %fusion.146) | copy-start | bytes 786436
  37.6 4.3 %collective-permute-start.13 = (f32[3,1,4096]{2,1,0:T(1,128)S(1)}, f32[3,1,4096]{2,1,0:T(1,128)S(1)}, u32[]{:S(2)}, u32[]{:S(2)}) collective-permute-start(f32[3,1,4096]{2,1,0:T(1,128)S(1)} %get-tuple-element.219), channel_id=1, source_target_pairs={{0,1},{1,0},{2,3},{3,2},{4,5},{5,4},{6,7},{7,6},{8,9},{9,8},{10,11... | collective-permute-start | bytes 147464 | tf_op jit(solution)/shard_map/ppermute | solution.py:27
  39.1 4.1 %collective-permute-start.14 = (f32[3,1,4096]{2,1,0:T(1,128)S(1)}, f32[3,1,4096]{2,1,0:T(1,128)S(1)}, u32[]{:S(2)}, u32[]{:S(2)}) collective-permute-start(f32[3,1,4096]{2,1,0:T(1,128)S(1)} %get-tuple-element.218), channel_id=1, source_target_pairs={{1,0},{0,1},{3,2},{2,3},{5,4},{4,5},{7,6},{6,7},{9,8},{8,9},{11,10... | collective-permute-start | bytes 147464 | tf_op jit(solution)/shard_map/ppermute | solution.py:29
  45.3 4.2 %collective-permute-start.15 = (f32[3,1,4096]{2,1,0:T(1,128)S(1)}, f32[3,1,4096]{2,1,0:T(1,128)S(1)}, u32[]{:S(2)}, u32[]{:S(2)}) collective-permute-start(f32[3,1,4096]{2,1,0:T(1,128)S(1)} %get-tuple-element.213), channel_id=1, source_target_pairs={{0,1},{1,0},{2,3},{3,2},{4,5},{5,4},{6,7},{7,6},{8,9},{9,8},{10,11... | collective-permute-start | bytes 147464 | tf_op jit(solution)/shard_map/while/body/eval_jaxpr/ppermute | solution.py:27
  46.1 4.1 %collective-permute-start.16 = (f32[3,1,4096]{2,1,0:T(1,128)S(1)}, f32[3,1,4096]{2,1,0:T(1,128)S(1)}, u32[]{:S(2)}, u32[]{:S(2)}) collective-permute-start(f32[3,1,4096]{2,1,0:T(1,128)S(1)} %get-tuple-element.212), channel_id=1, source_target_pairs={{1,0},{0,1},{3,2},{2,3},{5,4},{4,5},{7,6},{6,7},{9,8},{8,9},{11,10... | collective-permute-start | bytes 147464 | tf_op jit(solution)/shard_map/while/body/eval_jaxpr/ppermute | solution.py:29
  52.8 13.6 %collective-permute-start.17 = (f32[3,16,4096]{2,1,0:T(8,128)}, f32[3,16,4096]{2,1,0:T(8,128)}, u32[]{:S(2)}, u32[]{:S(2)}) collective-permute-start(f32[3,16,4096]{2,1,0:T(8,128)} %fusion.96), channel_id=1, source_target_pairs={{0,2},{2,4},{4,6},{6,8},{8,10},{10,12},{12,14},{14,16},{16,18},{18... | collective-permute-start | bytes 2359304 | tf_op jit(solution)/shard_map/ppermute | solution.py:17
  70.1 8.4 %collective-permute-start = (f32[3,1,4096]{2,1,0:T(1,128)}, f32[3,1,4096]{2,1,0:T(1,128)}, u32[]{:S(2)}, u32[]{:S(2)}) collective-permute-start(f32[3,1,4096]{2,1,0:T(1,128)} %get-tuple-element.465), channel_id=1, source_target_pairs={{0,1},{1,0},{2,3},{3,2},{4,5},{5,4},{6,7},{7,6},{8,9},{9,8},{10,11... | collective-permute-start | bytes 147464 | tf_op jit(solution)/shard_map/while/body/eval_jaxpr/ppermute | solution.py:27
  71.3 5.3 %collective-permute-start.1 = (f32[3,1,4096]{2,1,0:T(1,128)}, f32[3,1,4096]{2,1,0:T(1,128)}, u32[]{:S(2)}, u32[]{:S(2)}) collective-permute-start(f32[3,1,4096]{2,1,0:T(1,128)} %get-tuple-element.466), channel_id=1, source_target_pairs={{1,0},{0,1},{3,2},{2,3},{5,4},{4,5},{7,6},{6,7},{9,8},{8,9},{11,10... | collective-permute-start | bytes 147464 | tf_op jit(solution)/shard_map/while/body/eval_jaxpr/ppermute | solution.py:29
  84.6 8.4 %collective-permute-start = (f32[3,1,4096]{2,1,0:T(1,128)}, f32[3,1,4096]{2,1,0:T(1,128)}, u32[]{:S(2)}, u32[]{:S(2)}) collective-permute-start(f32[3,1,4096]{2,1,0:T(1,128)} %get-tuple-element.465), channel_id=1, source_target_pairs={{0,1},{1,0},{2,3},{3,2},{4,5},{5,4},{6,7},{7,6},{8,9},{9,8},{10,11... | collective-permute-start | bytes 147464 | tf_op jit(solution)/shard_map/while/body/eval_jaxpr/ppermute | solution.py:27
  85.8 5.3 %collective-permute-start.1 = (f32[3,1,4096]{2,1,0:T(1,128)}, f32[3,1,4096]{2,1,0:T(1,128)}, u32[]{:S(2)}, u32[]{:S(2)}) collective-permute-start(f32[3,1,4096]{2,1,0:T(1,128)} %get-tuple-element.466), channel_id=1, source_target_pairs={{1,0},{0,1},{3,2},{2,3},{5,4},{4,5},{7,6},{6,7},{9,8},{8,9},{11,10... | collective-permute-start | bytes 147464 | tf_op jit(solution)/shard_map/while/body/eval_jaxpr/ppermute | solution.py:29
  98.4 18.3 %collective-permute-start.18 = (f32[3,16,4096]{2,1,0:T(8,128)S(1)}, f32[3,16,4096]{2,1,0:T(8,128)}, u32[]{:S(2)}, u32[]{:S(2)}) collective-permute-start(f32[3,16,4096]{2,1,0:T(8,128)S(1)} %get-tuple-element.65), channel_id=1, source_target_pairs={{0,4},{2,6},{4,8},{6,10},{8,12},{10,14},{12,16},{14,18},{16,20},{1... | collective-permute-start | bytes 2359304 | tf_op jit(solution)/shard_map/ppermute | solution.py:17
  119.8 8.4 %collective-permute-start.2 = (f32[3,1,4096]{2,1,0:T(1,128)}, f32[3,1,4096]{2,1,0:T(1,128)}, u32[]{:S(2)}, u32[]{:S(2)}) collective-permute-start(f32[3,1,4096]{2,1,0:T(1,128)} %get-tuple-element.494), channel_id=1, source_target_pairs={{0,1},{1,0},{2,3},{3,2},{4,5},{5,4},{6,7},{7,6},{8,9},{9,8},{10,11... | collective-permute-start | bytes 147464 | tf_op jit(solution)/shard_map/while/body/eval_jaxpr/ppermute | solution.py:27
  121.0 5.3 %collective-permute-start.3 = (f32[3,1,4096]{2,1,0:T(1,128)}, f32[3,1,4096]{2,1,0:T(1,128)}, u32[]{:S(2)}, u32[]{:S(2)}) collective-permute-start(f32[3,1,4096]{2,1,0:T(1,128)} %get-tuple-element.495), channel_id=1, source_target_pairs={{1,0},{0,1},{3,2},{2,3},{5,4},{4,5},{7,6},{6,7},{9,8},{8,9},{11,10... | collective-permute-start | bytes 147464 | tf_op jit(solution)/shard_map/while/body/eval_jaxpr/ppermute | solution.py:29
  134.3 8.4 %collective-permute-start.2 = (f32[3,1,4096]{2,1,0:T(1,128)}, f32[3,1,4096]{2,1,0:T(1,128)}, u32[]{:S(2)}, u32[]{:S(2)}) collective-permute-start(f32[3,1,4096]{2,1,0:T(1,128)} %get-tuple-element.494), channel_id=1, source_target_pairs={{0,1},{1,0},{2,3},{3,2},{4,5},{5,4},{6,7},{7,6},{8,9},{9,8},{10,11... | collective-permute-start | bytes 147464 | tf_op jit(solution)/shard_map/while/body/eval_jaxpr/ppermute | solution.py:27
  135.5 5.3 %collective-permute-start.3 = (f32[3,1,4096]{2,1,0:T(1,128)}, f32[3,1,4096]{2,1,0:T(1,128)}, u32[]{:S(2)}, u32[]{:S(2)}) collective-permute-start(f32[3,1,4096]{2,1,0:T(1,128)} %get-tuple-element.495), channel_id=1, source_target_pairs={{1,0},{0,1},{3,2},{2,3},{5,4},{4,5},{7,6},{6,7},{9,8},{8,9},{11,10... | collective-permute-start | bytes 147464 | tf_op jit(solution)/shard_map/while/body/eval_jaxpr/ppermute | solution.py:29
  148.8 8.4 %collective-permute-start.2 = (f32[3,1,4096]{2,1,0:T(1,128)}, f32[3,1,4096]{2,1,0:T(1,128)}, u32[]{:S(2)}, u32[]{:S(2)}) collective-permute-start(f32[3,1,4096]{2,1,0:T(1,128)} %get-tuple-element.494), channel_id=1, source_target_pairs={{0,1},{1,0},{2,3},{3,2},{4,5},{5,4},{6,7},{7,6},{8,9},{9,8},{10,11... | collective-permute-start | bytes 147464 | tf_op jit(solution)/shard_map/while/body/eval_jaxpr/ppermute | solution.py:27
  150.1 5.3 %collective-permute-start.3 = (f32[3,1,4096]{2,1,0:T(1,128)}, f32[3,1,4096]{2,1,0:T(1,128)}, u32[]{:S(2)}, u32[]{:S(2)}) collective-permute-start(f32[3,1,4096]{2,1,0:T(1,128)} %get-tuple-element.495), channel_id=1, source_target_pairs={{1,0},{0,1},{3,2},{2,3},{5,4},{4,5},{7,6},{6,7},{9,8},{8,9},{11,10... | collective-permute-start | bytes 147464 | tf_op jit(solution)/shard_map/while/body/eval_jaxpr/ppermute | solution.py:29
  163.3 8.4 %collective-permute-start.2 = (f32[3,1,4096]{2,1,0:T(1,128)}, f32[3,1,4096]{2,1,0:T(1,128)}, u32[]{:S(2)}, u32[]{:S(2)}) collective-permute-start(f32[3,1,4096]{2,1,0:T(1,128)} %get-tuple-element.494), channel_id=1, source_target_pairs={{0,1},{1,0},{2,3},{3,2},{4,5},{5,4},{6,7},{7,6},{8,9},{9,8},{10,11... | collective-permute-start | bytes 147464 | tf_op jit(solution)/shard_map/while/body/eval_jaxpr/ppermute | solution.py:27
  164.6 5.3 %collective-permute-start.3 = (f32[3,1,4096]{2,1,0:T(1,128)}, f32[3,1,4096]{2,1,0:T(1,128)}, u32[]{:S(2)}, u32[]{:S(2)}) collective-permute-start(f32[3,1,4096]{2,1,0:T(1,128)} %get-tuple-element.495), channel_id=1, source_target_pairs={{1,0},{0,1},{3,2},{2,3},{5,4},{4,5},{7,6},{6,7},{9,8},{8,9},{11,10... | collective-permute-start | bytes 147464 | tf_op jit(solution)/shard_map/while/body/eval_jaxpr/ppermute | solution.py:29
  177.1 17.9 %collective-permute-start.19 = (f32[3,16,4096]{2,1,0:T(8,128)S(1)}, f32[3,16,4096]{2,1,0:T(8,128)S(1)}, u32[]{:S(2)}, u32[]{:S(2)}) collective-permute-start(f32[3,16,4096]{2,1,0:T(8,128)S(1)} %get-tuple-element.66), channel_id=1, source_target_pairs={{0,8},{2,10},{4,12},{6,14},{8,16},{10,18},{12,20},{14,22},{16,24},... | collective-permute-start | bytes 2359304 | tf_op jit(solution)/shard_map/ppermute | solution.py:17
  197.9 8.4 %collective-permute-start.4 = (f32[3,1,4096]{2,1,0:T(1,128)}, f32[3,1,4096]{2,1,0:T(1,128)}, u32[]{:S(2)}, u32[]{:S(2)}) collective-permute-start(f32[3,1,4096]{2,1,0:T(1,128)} %get-tuple-element.523), channel_id=1, source_target_pairs={{0,1},{1,0},{2,3},{3,2},{4,5},{5,4},{6,7},{7,6},{8,9},{9,8},{10,11... | collective-permute-start | bytes 147464 | tf_op jit(solution)/shard_map/while/body/eval_jaxpr/ppermute | solution.py:27
  198.9 5.7 %collective-permute-start.5 = (f32[3,1,4096]{2,1,0:T(1,128)}, f32[3,1,4096]{2,1,0:T(1,128)}, u32[]{:S(2)}, u32[]{:S(2)}) collective-permute-start(f32[3,1,4096]{2,1,0:T(1,128)} %get-tuple-element.524), channel_id=1, source_target_pairs={{1,0},{0,1},{3,2},{2,3},{5,4},{4,5},{7,6},{6,7},{9,8},{8,9},{11,10... | collective-permute-start | bytes 147464 | tf_op jit(solution)/shard_map/while/body/eval_jaxpr/ppermute | solution.py:29
  212.5 8.4 %collective-permute-start.4 = (f32[3,1,4096]{2,1,0:T(1,128)}, f32[3,1,4096]{2,1,0:T(1,128)}, u32[]{:S(2)}, u32[]{:S(2)}) collective-permute-start(f32[3,1,4096]{2,1,0:T(1,128)} %get-tuple-element.523), channel_id=1, source_target_pairs={{0,1},{1,0},{2,3},{3,2},{4,5},{5,4},{6,7},{7,6},{8,9},{9,8},{10,11... | collective-permute-start | bytes 147464 | tf_op jit(solution)/shard_map/while/body/eval_jaxpr/ppermute | solution.py:27
  213.4 5.7 %collective-permute-start.5 = (f32[3,1,4096]{2,1,0:T(1,128)}, f32[3,1,4096]{2,1,0:T(1,128)}, u32[]{:S(2)}, u32[]{:S(2)}) collective-permute-start(f32[3,1,4096]{2,1,0:T(1,128)} %get-tuple-element.524), channel_id=1, source_target_pairs={{1,0},{0,1},{3,2},{2,3},{5,4},{4,5},{7,6},{6,7},{9,8},{8,9},{11,10... | collective-permute-start | bytes 147464 | tf_op jit(solution)/shard_map/while/body/eval_jaxpr/ppermute | solution.py:29
  227.0 8.4 %collective-permute-start.4 = (f32[3,1,4096]{2,1,0:T(1,128)}, f32[3,1,4096]{2,1,0:T(1,128)}, u32[]{:S(2)}, u32[]{:S(2)}) collective-permute-start(f32[3,1,4096]{2,1,0:T(1,128)} %get-tuple-element.523), channel_id=1, source_target_pairs={{0,1},{1,0},{2,3},{3,2},{4,5},{5,4},{6,7},{7,6},{8,9},{9,8},{10,11... | collective-permute-start | bytes 147464 | tf_op jit(solution)/shard_map/while/body/eval_jaxpr/ppermute | solution.py:27
  227.9 5.7 %collective-permute-start.5 = (f32[3,1,4096]{2,1,0:T(1,128)}, f32[3,1,4096]{2,1,0:T(1,128)}, u32[]{:S(2)}, u32[]{:S(2)}) collective-permute-start(f32[3,1,4096]{2,1,0:T(1,128)} %get-tuple-element.524), channel_id=1, source_target_pairs={{1,0},{0,1},{3,2},{2,3},{5,4},{4,5},{7,6},{6,7},{9,8},{8,9},{11,10... | collective-permute-start | bytes 147464 | tf_op jit(solution)/shard_map/while/body/eval_jaxpr/ppermute | solution.py:29
  241.5 8.4 %collective-permute-start.4 = (f32[3,1,4096]{2,1,0:T(1,128)}, f32[3,1,4096]{2,1,0:T(1,128)}, u32[]{:S(2)}, u32[]{:S(2)}) collective-permute-start(f32[3,1,4096]{2,1,0:T(1,128)} %get-tuple-element.523), channel_id=1, source_target_pairs={{0,1},{1,0},{2,3},{3,2},{4,5},{5,4},{6,7},{7,6},{8,9},{9,8},{10,11... | collective-permute-start | bytes 147464 | tf_op jit(solution)/shard_map/while/body/eval_jaxpr/ppermute | solution.py:27
  242.4 5.7 %collective-permute-start.5 = (f32[3,1,4096]{2,1,0:T(1,128)}, f32[3,1,4096]{2,1,0:T(1,128)}, u32[]{:S(2)}, u32[]{:S(2)}) collective-permute-start(f32[3,1,4096]{2,1,0:T(1,128)} %get-tuple-element.524), channel_id=1, source_target_pairs={{1,0},{0,1},{3,2},{2,3},{5,4},{4,5},{7,6},{6,7},{9,8},{8,9},{11,10... | collective-permute-start | bytes 147464 | tf_op jit(solution)/shard_map/while/body/eval_jaxpr/ppermute | solution.py:29
  256.0 8.4 %collective-permute-start.4 = (f32[3,1,4096]{2,1,0:T(1,128)}, f32[3,1,4096]{2,1,0:T(1,128)}, u32[]{:S(2)}, u32[]{:S(2)}) collective-permute-start(f32[3,1,4096]{2,1,0:T(1,128)} %get-tuple-element.523), channel_id=1, source_target_pairs={{0,1},{1,0},{2,3},{3,2},{4,5},{5,4},{6,7},{7,6},{8,9},{9,8},{10,11... | collective-permute-start | bytes 147464 | tf_op jit(solution)/shard_map/while/body/eval_jaxpr/ppermute | solution.py:27
  256.9 5.7 %collective-permute-start.5 = (f32[3,1,4096]{2,1,0:T(1,128)}, f32[3,1,4096]{2,1,0:T(1,128)}, u32[]{:S(2)}, u32[]{:S(2)}) collective-permute-start(f32[3,1,4096]{2,1,0:T(1,128)} %get-tuple-element.524), channel_id=1, source_target_pairs={{1,0},{0,1},{3,2},{2,3},{5,4},{4,5},{7,6},{6,7},{9,8},{8,9},{11,10... | collective-permute-start | bytes 147464 | tf_op jit(solution)/shard_map/while/body/eval_jaxpr/ppermute | solution.py:29
  270.5 8.4 %collective-permute-start.4 = (f32[3,1,4096]{2,1,0:T(1,128)}, f32[3,1,4096]{2,1,0:T(1,128)}, u32[]{:S(2)}, u32[]{:S(2)}) collective-permute-start(f32[3,1,4096]{2,1,0:T(1,128)} %get-tuple-element.523), channel_id=1, source_target_pairs={{0,1},{1,0},{2,3},{3,2},{4,5},{5,4},{6,7},{7,6},{8,9},{9,8},{10,11... | collective-permute-start | bytes 147464 | tf_op jit(solution)/shard_map/while/body/eval_jaxpr/ppermute | solution.py:27
  271.4 5.7 %collective-permute-start.5 = (f32[3,1,4096]{2,1,0:T(1,128)}, f32[3,1,4096]{2,1,0:T(1,128)}, u32[]{:S(2)}, u32[]{:S(2)}) collective-permute-start(f32[3,1,4096]{2,1,0:T(1,128)} %get-tuple-element.524), channel_id=1, source_target_pairs={{1,0},{0,1},{3,2},{2,3},{5,4},{4,5},{7,6},{6,7},{9,8},{8,9},{11,10... | collective-permute-start | bytes 147464 | tf_op jit(solution)/shard_map/while/body/eval_jaxpr/ppermute | solution.py:29
  285.0 8.4 %collective-permute-start.4 = (f32[3,1,4096]{2,1,0:T(1,128)}, f32[3,1,4096]{2,1,0:T(1,128)}, u32[]{:S(2)}, u32[]{:S(2)}) collective-permute-start(f32[3,1,4096]{2,1,0:T(1,128)} %get-tuple-element.523), channel_id=1, source_target_pairs={{0,1},{1,0},{2,3},{3,2},{4,5},{5,4},{6,7},{7,6},{8,9},{9,8},{10,11... | collective-permute-start | bytes 147464 | tf_op jit(solution)/shard_map/while/body/eval_jaxpr/ppermute | solution.py:27
  285.9 5.7 %collective-permute-start.5 = (f32[3,1,4096]{2,1,0:T(1,128)}, f32[3,1,4096]{2,1,0:T(1,128)}, u32[]{:S(2)}, u32[]{:S(2)}) collective-permute-start(f32[3,1,4096]{2,1,0:T(1,128)} %get-tuple-element.524), channel_id=1, source_target_pairs={{1,0},{0,1},{3,2},{2,3},{5,4},{4,5},{7,6},{6,7},{9,8},{8,9},{11,10... | collective-permute-start | bytes 147464 | tf_op jit(solution)/shard_map/while/body/eval_jaxpr/ppermute | solution.py:29
  299.5 8.4 %collective-permute-start.4 = (f32[3,1,4096]{2,1,0:T(1,128)}, f32[3,1,4096]{2,1,0:T(1,128)}, u32[]{:S(2)}, u32[]{:S(2)}) collective-permute-start(f32[3,1,4096]{2,1,0:T(1,128)} %get-tuple-element.523), channel_id=1, source_target_pairs={{0,1},{1,0},{2,3},{3,2},{4,5},{5,4},{6,7},{7,6},{8,9},{9,8},{10,11... | collective-permute-start | bytes 147464 | tf_op jit(solution)/shard_map/while/body/eval_jaxpr/ppermute | solution.py:27
  300.5 5.7 %collective-permute-start.5 = (f32[3,1,4096]{2,1,0:T(1,128)}, f32[3,1,4096]{2,1,0:T(1,128)}, u32[]{:S(2)}, u32[]{:S(2)}) collective-permute-start(f32[3,1,4096]{2,1,0:T(1,128)} %get-tuple-element.524), channel_id=1, source_target_pairs={{1,0},{0,1},{3,2},{2,3},{5,4},{4,5},{7,6},{6,7},{9,8},{8,9},{11,10... | collective-permute-start | bytes 147464 | tf_op jit(solution)/shard_map/while/body/eval_jaxpr/ppermute | solution.py:29
  313.3 44.2 %copy-start.28 = (f32[3,16,4096]{2,1,0:T(8,128)S(1)}, f32[3,16,4096]{2,1,0:T(8,128)}, u32[]{:S(2)}) copy-start(f32[3,16,4096]{2,1,0:T(8,128)} %param.10) | copy-start | bytes 2359300
  313.4 29.7 %collective-permute-start.20 = (f32[3,16,4096]{2,1,0:T(8,128)S(1)}, f32[3,16,4096]{2,1,0:T(8,128)S(1)}, u32[]{:S(2)}, u32[]{:S(2)}) collective-permute-start(f32[3,16,4096]{2,1,0:T(8,128)S(1)} %get-tuple-element.67), channel_id=1, source_target_pairs={{0,16},{2,18},{4,20},{6,22},{8,24},{10,26},{12,28},{14,30},{1,17},... | collective-permute-start | bytes 2359304 | tf_op jit(solution)/shard_map/ppermute | solution.py:17
  344.3 13.3 %collective-permute-start.21 = (f32[3,16,4096]{2,1,0:T(8,128)S(1)}, f32[3,16,4096]{2,1,0:T(8,128)S(1)}, u32[]{:S(2)}, u32[]{:S(2)}) collective-permute-start(f32[3,16,4096]{2,1,0:T(8,128)S(1)} %add.572), channel_id=1, source_target_pairs={{0,2},{2,4},{4,6},{6,8},{8,10},{10,12},{12,14},{14,16},{16,18},{18... | collective-permute-start | bytes 2359304 | tf_op jit(solution)/shard_map/ppermute | solution.py:17
  (110 other events, 172.1 us)
where the time goes:
time: 365 us; the launch traced here: 359 us
  local copies, waits for them, and re-layouts  119 us (33%)
  waiting for transfers between devices  103 us (28%)
  other arithmetic  86.4 us (24%)
  starting transfers between devices  48.6 us (13%)
    ppermute x6, waiting for transfers between devices, from_behind(): return lax.ppermute(value, axis, pairs)  87.5 us
    slice x38, local copies, waits for them, and re-layouts, diffuse(): jnp.roll(centre, 1, -1)  29.3 us
    concatenate x72, local copies, waits for them, and re-layouts, diffuse(): jnp.roll(centre, 1, -1)  26.4 us
    concatenate x14, local copies, waits for them, and re-layouts, extended(): jnp.concatenate([lax.ppermute(tail, axis, [(i, (i + 1) % count) for i in...  25.6 us
    add x18, other arithmetic, tendency(): -column_slope(height_c) + coriolis * north_c  23.4 us
    ppermute x19, starting transfers between devices, extended(): lax.ppermute(head, axis, [((i + 1) % count, i) for i in range(count)])  20.1 us
    while x210, local copies, waits for them, and re-layouts  19.2 us
    ppermute x19, starting transfers between devices, extended(): lax.ppermute(tail, axis, [(i, (i + 1) % count) for i in range(count)])  18.7 us
  transfers between devices with their start and end apart: 44, of which 16 were waited for; matrix products, arithmetic and copies ran while one was open for 27% of the time, Pallas kernels for 0%

commit v1 on v0

v1 whole, which is shorter than its diff:
```python
import functools

import jax
import jax.numpy as jnp
from jax import lax
from jax.experimental import pallas as pl
from jax.experimental.pallas import tpu as pltpu
from jax.sharding import Mesh
from jax.sharding import PartitionSpec as P

DT = 0.3
HALF = 0.5 * DT
NU = 1.0 / 3.0
FC = 0.5
DEEP = 3
TILE = 8
LANES = 128


def rolled(x, by, axis):
    return pltpu.roll(x, by % x.shape[axis], axis)


def tendency(q, depth):
    height, east, north = q

    def near(x):
        up, down = rolled(x, 1, 0), rolled(x, -1, 0)
        left, right = rolled(x, 1, 1), rolled(x, -1, 1)
        lap = ((up + down) + (left + right)) - 4.0 * x
        return up, down, left, right, NU * lap

    h_up, h_down, h_left, h_right, h_lap = near(height)
    _, _, _, _, e_lap = near(east)
    _, _, _, _, n_lap = near(north)
    flux_e = depth * east
    flux_n = depth * north
    dh = (
        (rolled(flux_e, 1, 1) - rolled(flux_e, -1, 1))
        + (rolled(flux_n, 1, 0) - rolled(flux_n, -1, 0))
    ) * 0.5 + h_lap
    de = (h_left - h_right) * 0.5 + FC * north + e_lap
    dn = (h_up - h_down) * 0.5 - FC * east + n_lap
    return dh, de, dn


def stepped(q, depth):
    return tuple(x + DT * r for x, r in zip(q, tendency(q, depth)))


def combine_body(first_ref, nodes, prev, init, g_out, k_out, edge_out):
    rows = g_out.shape[1]
    first = first_ref[0] == 1
    edge_out[:, 15:, :] = jnp.zeros((2, 1, edge_out.shape[2]), jnp.float32)
    for f in range(3):
        n0, n1, n2 = nodes[0, f], nodes[1, f], nodes[2, f]
        start = jnp.where(first, init[f], prev[f])
        g = (DT / 24.0) * (12.0 * start - 7.0 * n0 + 8.0 * n1 - n2)
        k = (DT / 4.0) * (n0 - 2.0 * n1 + n2)
        g_out[f] = g
        k_out[f] = k
        edge_out[0, 3 * f : 3 * f + 3, :] = g[:3]
        edge_out[1, 3 * f : 3 * f + 3, :] = g[rows - 3 :]
        edge_out[0, 9 + 2 * f : 11 + 2 * f, :] = k[:2]
        edge_out[1, 9 + 2 * f : 11 + 2 * f, :] = k[rows - 2 :]


def fine_body(width, reach, g_ref, k_ref, below, above, depth_ref, msg_out, b_out, v_out):
    rows, cols = g_ref.shape[1:]
    depth = depth_ref[...]

    def with_halo(ref, f, base, deep):
        gap = jnp.zeros((TILE - 2 * deep, cols), jnp.float32)
        lo = base + deep * f
        return jnp.concatenate([ref[f], below[lo : lo + deep, :], gap, above[lo : lo + deep, :]], axis=0)

    g = tuple(with_halo(g_ref, f, 0, 3) for f in range(3))
    k = tuple(with_halo(k_ref, f, 9, 2) for f in range(3))
    fg = tendency(g, depth)
    u = tendency(fg, depth)
    v = tendency(tuple(a + HALF * b for a, b in zip(k, fg)), depth)
    fv = tendency(v, depth)
    span = msg_out.shape[2]
    lane = lax.broadcasted_iota(jnp.int32, (rows, LANES), 1)
    for f in range(3):
        b = DT * (u[f][:rows] + (1.0 / 6.0) * fv[f][:rows])
        v_out[f] = v[f][:rows]
        b_out[f] = b
        for j in range(msg_out.shape[0]):
            at = j * width
            if width % LANES == 0:
                parts = [b[:, (at + t) % cols : (at + t) % cols + LANES] for t in range(0, span, LANES)]
                tail = b[:, (at - LANES) % cols : (at - LANES) % cols + LANES]
            else:
                turned = rolled(b, -at, 1)
                parts = [turned[:, t : t + LANES] for t in range(0, span, LANES)]
                tail = turned[:, cols - LANES :]
            parts[-1] = jnp.where(lane < LANES - reach, parts[-1], tail)
            for t, part in enumerate(parts):
                msg_out[j, f * rows : (f + 1) * rows, t * LANES : (t + 1) * LANES] = part


def gathered(recv, slot, spaces, rows):
    return tuple(
        jnp.concatenate([recv[slot * spaces + y, f * rows : (f + 1) * rows, :] for y in range(spaces)], axis=0)
        for f in range(3)
    )


def total_body(spaces, recv, depth_ref, x0, total_out):
    rows = recv.shape[1] // 3
    slots = recv.shape[0] // spaces
    depth = depth_ref[...]
    q = tuple(x0[f] for f in range(3))
    for slot in range(slots):
        b = gathered(recv, slot, spaces, rows)
        q = tuple(x + y for x, y in zip(b, stepped(q, depth)))
    for f in range(3):
        total_out[f] = q[f]


def chain_body(spaces, lower_ref, recv, depth_ref, x0, carry, msg_out):
    rows = recv.shape[1] // 3
    slots = recv.shape[0] // spaces
    width = msg_out.shape[2]
    all_rows = rows * spaces
    depth = depth_ref[...]
    lower = lower_ref[0] == 1
    q = tuple(jnp.where(lower, x0[f], carry[f]) for f in range(3))
    for slot in range(slots):
        for y in range(spaces):
            at = slot * spaces + y
            for f in range(3):
                here = q[f][:, :width]
                lo, hi = y * rows, (y + 1) * rows
                msg_out[at, f * rows : (f + 1) * rows, :] = here[lo:hi]
                before, after = (lo - 1) % all_rows, hi % all_rows
                msg_out[at, 3 * rows + f : 3 * rows + f + 1, :] = here[before : before + 1]
                msg_out[at, 3 * rows + 3 + f : 3 * rows + 4 + f, :] = here[after : after + 1]
            msg_out[at, 3 * rows + 6 :, :] = jnp.zeros((2, width), jnp.float32)
        if slot + 1 < slots:
            b = gathered(recv, slot, spaces, rows)
            q = tuple(x + y for x, y in zip(b, stepped(q, depth)))


def finish_body(recv, b_ref, v_ref, depth_ref, out, state):
    rows = b_ref.shape[1]
    pieces, _, width = recv.shape
    for f in range(3):
        state[f, rows:, :] = jnp.zeros((TILE, state.shape[2]), jnp.float32)
        for j in range(pieces):
            cut = slice(j * width, (j + 1) * width)
            state[f, :rows, cut] = recv[j, f * rows : (f + 1) * rows, :]
            state[f, rows + TILE - 1 : rows + TILE, cut] = recv[j, 3 * rows + f : 3 * rows + f + 1, :]
            state[f, rows : rows + 1, cut] = recv[j, 3 * rows + 3 + f : 3 * rows + 4 + f, :]
    q = tuple(state[f] for f in range(3))
    after = stepped(q, depth_ref[...])
    for f in range(3):
        begin = q[f][:rows]
        end = b_ref[f] + after[f][:rows]
        out[0, f] = begin
        out[1, f] = 0.5 * ((begin + end) - v_ref[f])
        out[2, f] = end


def kernel(body, shapes, name, scalars=0, **more):
    vmem = pl.BlockSpec(memory_space=pltpu.VMEM)
    smem = pl.BlockSpec(memory_space=pltpu.SMEM)

    def call(*args):
        many = isinstance(shapes, list)
        outs = [jax.ShapeDtypeStruct(s, jnp.float32) for s in (shapes if many else [shapes])]
        return pl.pallas_call(
            body,
            out_shape=outs if many else outs[0],
            in_specs=[smem] * scalars + [vmem] * (len(args) - scalars),
            out_specs=[vmem] * len(outs) if many else vmem,
            compiler_params=pltpu.CompilerParams(vmem_limit_bytes=56 * 1024 * 1024),
            name=name,
            **more,
        )(*args)

    return call


def swap_rows(top, bottom):
    count = lax.axis_size("space")
    if count == 2:
        both = lax.ppermute(jnp.stack([top, bottom]), "space", [(0, 1), (1, 0)])
        return both[0], both[1]
    below = lax.ppermute(top, "space", [((i + 1) % count, i) for i in range(count)])
    above = lax.ppermute(bottom, "space", [(i, (i + 1) % count) for i in range(count)])
    return below, above


def per_device(fine_nodes, init_state, mean_depth):
    nodes = fine_nodes[0]
    rows, cols = nodes.shape[-2:]
    outer, inner, spaces = lax.axis_size("outer"), lax.axis_size("inner"), lax.axis_size("space")
    group = ("inner", "space")
    owners = inner * spaces
    width = cols // owners
    reach = outer * inner - 1
    span = -(-(width + 2 * reach) // LANES) * LANES
    at_outer, at_inner = lax.axis_index("outer"), lax.axis_index("inner")
    slice_index = at_outer * inner + at_inner
    first = (slice_index == 0).astype(jnp.int32).reshape(1)
    lower = (at_outer == 0).astype(jnp.int32).reshape(1)

    slices = outer * inner
    prev = lax.ppermute(nodes[2], ("outer", "inner"), [(i, i + 1) for i in range(slices - 1)])

    fixed = jnp.concatenate([mean_depth[None], init_state], axis=0)
    onward = jnp.concatenate([fixed, fixed[..., :span]], axis=-1)
    behind = jnp.concatenate([fixed[..., cols - span :], fixed], axis=-1)
    lane = lax.broadcasted_iota(jnp.int32, (4, rows, span), 2)
    windows = []
    for y in range(spaces):
        start = (at_inner * spaces + y) * width
        ahead = lax.dynamic_slice_in_dim(onward, start, span, axis=2)
        back = lax.dynamic_slice_in_dim(behind, start, span, axis=2)
        windows.append(jnp.where(lane < span - reach, ahead, back))
    windows = lax.all_to_all(jnp.stack(windows), "space", 0, 0, tiled=True)
    windows = windows.transpose(1, 0, 2, 3).reshape(4, spaces * rows, span)
    depth_block, init_block = windows[0], windows[1:]

    low, high = swap_rows(mean_depth[:DEEP], mean_depth[rows - DEEP :])
    gap = jnp.zeros((TILE - 2 * DEEP, cols), jnp.float32)
    depth = jnp.concatenate([mean_depth, low, gap, high], axis=0)

    state = (3, rows, cols)
    g, k, edges = kernel(combine_body, [state, state, (2, 16, cols)], "combine", scalars=1)(
        first, nodes, prev, init_state
    )
    below, above = swap_rows(edges[0], edges[1])
    msgs, drift, vee = kernel(
        functools.partial(fine_body, width, reach), [(owners, 3 * rows, span), state, state], "fine"
    )(g, k, below, above, depth)

    recv = lax.all_to_all(msgs, group, 0, 0, tiled=True)
    block = (3, spaces * rows, span)
    total = kernel(functools.partial(total_body, spaces), block, "total")(recv, depth_block, init_block)
    carry = lax.ppermute(total, "outer", [(i, i + 1) for i in range(outer - 1)])
    back = kernel(functools.partial(chain_body, spaces), (owners, 3 * rows + TILE, width), "chain", scalars=1)(
        lower, recv, depth_block, init_block, carry
    )
    mine = lax.all_to_all(back, group, 0, 0, tiled=True)
    if width % LANES:
        mine = mine.transpose(1, 0, 2).reshape(1, 3 * rows + TILE, cols)
    out = kernel(
        finish_body,
        (3,) + state,
        "finish",
        scratch_shapes=[pltpu.VMEM((3, rows + TILE, cols), jnp.float32)],
    )(mine, drift, vee, depth)
    return out[None]


def solution(mesh):
    slices, spaces = mesh.shape["tm"], mesh.shape["space"]
    split = Mesh(mesh.devices.reshape(2, slices // 2, spaces), ("outer", "inner", "space"))
    nodes = P(("outer", "inner"), None, None, "space", None)
    return jax.shard_map(
        per_device,
        mesh=split,
        in_specs=(nodes, P(None, "space", None), P("space", None)),
        out_specs=nodes,
        check_vma=False,
    )
```

time: 365 us -> 113 us (0.31)
  the two profiles are of different devices: /device:TPU:26 before, /device:TPU:0 now
where the time goes in v1:
time: 113 us; the launch traced here: 112 us
  waiting for transfers between devices  32.2 us (28%)
  starting transfers between devices  29.2 us (26%)
  Pallas kernels  21.4 us (19%)
  blocking collectives  20.2 us (18%)
  local copies, waits for them, and re-layouts  6 us (5%)
  other arithmetic  3.36 us (3%)
    pallas_call x5, Pallas kernels, call(): pl.pallas_call(body, out_shape=outs if many else outs[0], in_specs=[smem]...  21.4 us
    all_to_all x1, blocking collectives, per_device(): mine = lax.all_to_all(back, group, 0, 0, tiled=True)  20.2 us
    all_to_all x1, starting transfers between devices, per_device(): recv = lax.all_to_all(msgs, group, 0, 0, tiled=True)  17 us
    all_to_all x1, waiting for transfers between devices, per_device(): recv = lax.all_to_all(msgs, group, 0, 0, tiled=True)  16.4 us
    ppermute x2, waiting for transfers between devices, swap_rows(): both = lax.ppermute(jnp.stack([top, bottom]), 'space', [(0, 1), (1, 0)])  11.4 us
    ppermute x1, waiting for transfers between devices, per_device(): carry = lax.ppermute(total, 'outer', [(i, i + 1) for i in range(outer - 1)])  4.44 us
    all_to_all x1, starting transfers between devices, per_device(): windows = lax.all_to_all(jnp.stack(windows), 'space', 0, 0, tiled=True)  4.26 us
    ppermute x1, starting transfers between devices, per_device(): carry = lax.ppermute(total, 'outer', [(i, i + 1) for i in range(outer - 1)])  4.18 us
  transfers between devices with their start and end apart: 6, of which 4 were waited for; matrix products, arithmetic and copies ran while one was open for 4% of the time, Pallas kernels for 9%

profile of v1, /device:TPU:0, one launch (start us, length us, event | category | flops | bytes accessed | tf_op | source)
XLA Modules:
  0.0 112.4 jit_solution(12705030440619924009)
XLA Ops:
  0.0 1.7 %fusion.1 = (f32[4,16,4480]{2,1,0:T(8,128)S(1)}, f32[4,16,4480]{2,1,0:T(8,128)S(1)}) fusion(f32[3,16,4096]{2,1,0:T(8,128)} %init.1, f32[1,16,4096]{2,1,0:T(8,128)} %bitcast.27), kind=kLoop, calls=%fused_computation.3 | loop fusion | flops 1720320 | bytes 3342336 | tf_op jit(solution)/shard_map/concatenate | solution.py:214
  1.7 0.0 copy-start.1
  1.8 0.7 pad_maximum_fusion.3
  2.5 4.3 %all-to-all-start.1 = ((f32[2,4,16,384]{3,2,1,0:T(8,128)}), f32[2,4,16,384]{3,2,1,0:T(8,128)S(1)}, u32[]{:S(2)}, u32[]{:S(2)}) async-start(f32[2,4,16,384]{3,2,1,0:T(8,128)} %pad_maximum_fusion.3), calls=%async_computation.1 | async-start | bytes 393216 | tf_op jit(solution)/shard_map/all_to_all | solution.py:223
  6.8 0.0 copy-done.1
  6.8 2.2 %collective-permute-start.2 = (f32[2,3,4096]{2,1,0:T(4,128)S(1)}, f32[2,3,4096]{2,1,0:T(4,128)S(1)}, u32[]{:S(2)}, u32[]{:S(2)}) collective-permute-start(f32[2,3,4096]{2,1,0:T(4,128)S(1)} %pad_maximum_fusion.4), channel_id=1, source_target_pairs={{0,1},{1,0},{2,3},{3,2},{4,5},{5,4},{6,7},{7,6},{8,9},{9,8},{10,11... | collective-permute-start | bytes 294920 | tf_op jit(solution)/shard_map/ppermute | solution.py:189
  9.1 1.2 %slice_bitcast_fusion = f32[3,16,4096]{2,1,0:T(8,128)S(1)} fusion(f32[1,3,3,16,4096]{4,3,2,1,0:T(8,128)} %param.3), kind=kLoop, calls=%fused_computation.4 | loop fusion | bytes 1572864 | tf_op jit(solution)/shard_map/squeeze | solution.py:211
  10.3 1.5 %collective-permute-start = (f32[3,16,4096]{2,1,0:T(8,128)S(1)}, f32[3,16,4096]{2,1,0:T(8,128)S(1)}, u32[]{:S(2)}, u32[]{:S(2)}) collective-permute-start(f32[3,16,4096]{2,1,0:T(8,128)S(1)} %slice_bitcast_fusion), channel_id=1, source_target_pairs={{0,2},{2,4},{4,6},{6,8},{8,10},{10,12},{12,14},{14,16},{16,18},{18... | collective-permute-start | bytes 2359304 | tf_op jit(solution)/shard_map/ppermute | solution.py:211
  11.8 0.1 pad.12.clone
  11.9 2.9 %collective-permute-done.2 = f32[2,3,4096]{2,1,0:T(4,128)S(1)} collective-permute-done((f32[2,3,4096]{2,1,0:T(4,128)S(1)}, f32[2,3,4096]{2,1,0:T(4,128)S(1)}, u32[]{:S(2)}, u32[]{:S(2)}) %collective-permute-start.2) | collective-permute-done | bytes 98336 | tf_op jit(solution)/shard_map/ppermute | solution.py:189
  14.7 0.0 collective-permute-done.prev
  14.8 0.0 copy-start.2
  14.8 0.9 copy-done.2
  15.6 3.6 %combine.1 = (f32[3,16,4096]{2,1,0:T(8,128)}, f32[3,16,4096]{2,1,0:T(8,128)}, f32[2,16,4096]{2,1,0:T(8,128)}) custom-call(s32[1]{0:T(128)} %bitcast.1.first_ref, f32[3,3,16,4096]{3,2,1,0:T(8,128)} %bitcast.26, f32[3,16,4096]{2,1,0:T(8,128)} %copy-done.2, f32[3,16,4096]{2,1,0:T(8,128)} %init.1), custom_call_target="tpu_custom_call" | custom-call | tf_op jit(solution)/shard_map/combine/pallas_call | solution.py:173
  19.2 0.0 collective-permute-start.1
  19.2 0.9 pad_maximum_fusion.2.depth_ref
  20.1 8.5 %collective-permute-done.1 = f32[2,16,4096]{2,1,0:T(8,128)S(1)} collective-permute-done((f32[2,16,4096]{2,1,0:T(8,128)}, f32[2,16,4096]{2,1,0:T(8,128)S(1)}, u32[]{:S(2)}, u32[]{:S(2)}) %collective-permute-start.1) | collective-permute-done | bytes 524320 | tf_op jit(solution)/shard_map/ppermute | solution.py:189
  28.6 0.8 slice_bitcast_fusion.1
  29.4 6.8 %fine.1 = (f32[16,48,384]{2,1,0:T(8,128)}, f32[3,16,4096]{2,1,0:T(8,128)}, f32[3,16,4096]{2,1,0:T(8,128)}) custom-call(f32[3,16,4096]{2,1,0:T(8,128)} %get-tuple-element.11.g_ref, f32[3,16,4096]{2,1,0:T(8,128)} %get-tuple-element.12.k_ref, f32[16,4096]{1,0:T(8,128)} %get-tuple-element.22.below, f32[16,4096]{1,0:T(8,128)} %get-tuple-element.21.above, ...), custom_call_target="tpu_custom_call" | custom-call | tf_op jit(solution)/shard_map/fine/pallas_call | solution.py:173
  36.2 0.0 all-to-all-done.1
  36.2 17.0 %all-to-all-start = ((f32[16,48,384]{2,1,0:T(8,128)}), f32[16,48,384]{2,1,0:T(8,128)S(1)}, u32[]{:S(2)}, u32[]{:S(2)}) async-start(f32[16,48,384]{2,1,0:T(8,128)} %get-tuple-element.14), calls=%async_computation | async-start | bytes 2359296 | tf_op jit(solution)/shard_map/all_to_all | solution.py:240
  53.3 0.6 slice.57
  53.9 0.7 copy.4
  54.5 16.4 %all-to-all-done.recv = f32[16,48,384]{2,1,0:T(8,128)S(1)} async-done(((f32[16,48,384]{2,1,0:T(8,128)}), f32[16,48,384]{2,1,0:T(8,128)S(1)}, u32[]{:S(2)}, u32[]{:S(2)}) %all-to-all-start) | async-done | bytes 1179680 | tf_op jit(solution)/shard_map/all_to_all | solution.py:240
  70.9 0.0 copy-start
  70.9 1.0 copy-done
  71.9 3.4 %total.1 = f32[3,32,384]{2,1,0:T(8,128)} custom-call(f32[16,48,384]{2,1,0:T(8,128)} %copy-done, f32[32,384]{1,0:T(8,128)} %bitcast.32, f32[3,32,384]{2,1,0:T(8,128)} %bitcast.28), custom_call_target="tpu_custom_call" | custom-call | tf_op jit(solution)/shard_map/total/pallas_call | solution.py:173
  75.3 4.2 %collective-permute-start.3 = (f32[3,32,384]{2,1,0:T(8,128)}, f32[3,32,384]{2,1,0:T(8,128)S(1)}, u32[]{:S(2)}, u32[]{:S(2)}) collective-permute-start(f32[3,32,384]{2,1,0:T(8,128)} %total.1), channel_id=1, source_target_pairs={{0,16},{1,17},{2,18},{3,19},{4,20},{5,21},{6,22},{7,23},{8,24},{9,... | collective-permute-start | bytes 442376 | tf_op jit(solution)/shard_map/ppermute | solution.py:243
  79.5 4.4 %collective-permute-done.3.carry = f32[3,32,384]{2,1,0:T(8,128)S(1)} collective-permute-done((f32[3,32,384]{2,1,0:T(8,128)}, f32[3,32,384]{2,1,0:T(8,128)S(1)}, u32[]{:S(2)}, u32[]{:S(2)}) %collective-permute-start.3) | collective-permute-done | bytes 147488 | tf_op jit(solution)/shard_map/ppermute | solution.py:243
  84.0 0.0 copy-start.3
  84.0 0.7 copy-done.3
  84.6 3.5 %chain.1 = f32[16,56,256]{2,1,0:T(8,128)} custom-call(s32[1]{0:T(128)} %bitcast.lower_ref, f32[16,48,384]{2,1,0:T(8,128)} %copy-done, f32[32,384]{1,0:T(8,128)} %bitcast.33, f32[3,32,384]{2,1,0:T(8,128)} %bitcast.29, f32[3,32,384]{2,1,0:T(8,128)} %copy-done.3), custom_call_target="tpu_custom_call" | custom-call | tf_op jit(solution)/shard_map/chain/pallas_call | solution.py:173
  88.2 20.2 %all_to_all.15.recv = f32[16,56,256]{2,1,0:T(8,128)} all-to-all(f32[16,56,256]{2,1,0:T(8,128)} %chain.1), channel_id=1, replica_groups=mesh['outer'=2,'inner'=8,'space'=2] {'inner','space'}, dimensions={0} | all-to-all | bytes 1835008 | tf_op jit(solution)/shard_map/all_to_all | solution.py:247
  108.4 4.1 %finish.1 = f32[3,3,16,4096]{3,2,1,0:T(8,128)} custom-call(f32[16,56,256]{2,1,0:T(8,128)} %all_to_all.15.recv, f32[3,16,4096]{2,1,0:T(8,128)} %get-tuple-element.15.b_ref, f32[3,16,4096]{2,1,0:T(8,128)} %get-tuple-element.16.v_ref, f32[24,4096]{1,0:T(8,128)} %pad_maximum_fusion.2.depth_ref), custom_call_target="tpu_custom_call" | custom-call | tf_op jit(solution)/shard_map/finish/pallas_call | solution.py:173
  (7 shorter events, 0.1 us)
Async XLA Ops:
  1.7 5.0 %copy-start.1 = (f32[16,4096]{1,0:T(8,128)S(1)}, f32[16,4096]{1,0:T(8,128)}, u32[]{:S(2)}) copy-start(f32[16,4096]{1,0:T(8,128)} %param.5) | copy-start | bytes 786436
  2.5 33.7 %all-to-all-start.1 = ((f32[2,4,16,384]{3,2,1,0:T(8,128)}), f32[2,4,16,384]{3,2,1,0:T(8,128)S(1)}, u32[]{:S(2)}, u32[]{:S(2)}) async-start(f32[2,4,16,384]{3,2,1,0:T(8,128)} %pad_maximum_fusion.3), calls=%async_computation.1 | async-start | bytes 393216 | tf_op jit(solution)/shard_map/all_to_all | solution.py:223
  6.8 7.9 %collective-permute-start.2 = (f32[2,3,4096]{2,1,0:T(4,128)S(1)}, f32[2,3,4096]{2,1,0:T(4,128)S(1)}, u32[]{:S(2)}, u32[]{:S(2)}) collective-permute-start(f32[2,3,4096]{2,1,0:T(4,128)S(1)} %pad_maximum_fusion.4), channel_id=1, source_target_pairs={{0,1},{1,0},{2,3},{3,2},{4,5},{5,4},{6,7},{7,6},{8,9},{9,8},{10,11... | collective-permute-start | bytes 294920 | tf_op jit(solution)/shard_map/ppermute | solution.py:189
  10.3 4.5 %collective-permute-start = (f32[3,16,4096]{2,1,0:T(8,128)S(1)}, f32[3,16,4096]{2,1,0:T(8,128)S(1)}, u32[]{:S(2)}, u32[]{:S(2)}) collective-permute-start(f32[3,16,4096]{2,1,0:T(8,128)S(1)} %slice_bitcast_fusion), channel_id=1, source_target_pairs={{0,2},{2,4},{4,6},{6,8},{8,10},{10,12},{12,14},{14,16},{16,18},{18... | collective-permute-start | bytes 2359304 | tf_op jit(solution)/shard_map/ppermute | solution.py:211
  14.8 0.9 copy-start.2
  19.2 9.4 %collective-permute-start.1 = (f32[2,16,4096]{2,1,0:T(8,128)}, f32[2,16,4096]{2,1,0:T(8,128)S(1)}, u32[]{:S(2)}, u32[]{:S(2)}) collective-permute-start(f32[2,16,4096]{2,1,0:T(8,128)} %get-tuple-element.13), channel_id=1, source_target_pairs={{0,1},{1,0},{2,3},{3,2},{4,5},{5,4},{6,7},{7,6},{8,9},{9,8},{10,11... | collective-permute-start | bytes 1572872 | tf_op jit(solution)/shard_map/ppermute | solution.py:189
  36.2 34.7 %all-to-all-start = ((f32[16,48,384]{2,1,0:T(8,128)}), f32[16,48,384]{2,1,0:T(8,128)S(1)}, u32[]{:S(2)}, u32[]{:S(2)}) async-start(f32[16,48,384]{2,1,0:T(8,128)} %get-tuple-element.14), calls=%async_computation | async-start | bytes 2359296 | tf_op jit(solution)/shard_map/all_to_all | solution.py:240
  70.9 1.0 copy-start
  75.3 8.6 %collective-permute-start.3 = (f32[3,32,384]{2,1,0:T(8,128)}, f32[3,32,384]{2,1,0:T(8,128)S(1)}, u32[]{:S(2)}, u32[]{:S(2)}) collective-permute-start(f32[3,32,384]{2,1,0:T(8,128)} %total.1), channel_id=1, source_target_pairs={{0,16},{1,17},{2,18},{3,19},{4,20},{5,21},{6,22},{7,23},{8,24},{9,... | collective-permute-start | bytes 442376 | tf_op jit(solution)/shard_map/ppermute | solution.py:243
  84.0 0.7 copy-start.3

commit v2 on v1

v2 whole, which is shorter than its diff:
```python
import functools

import jax
import jax.numpy as jnp
from jax import lax
from jax.experimental import pallas as pl
from jax.experimental.pallas import tpu as pltpu
from jax.sharding import Mesh
from jax.sharding import PartitionSpec as P


DT = 0.3
HALF = 0.5 * DT
NU = 1.0 / 3.0
FC = 0.5
DEEP = 3
TILE = 8
LANES = 128
VMEM_BYTES = 20 * 1024 * 1024


def rolled(x, by, axis):
    return pltpu.roll(x, by % x.shape[axis], axis)


def advanced(q, flow, scale, keep):
    height, east, north = q
    soft, slope, turn = scale * NU, scale * 0.5, scale * FC
    stay = keep - 4.0 * soft
    h_soft, e_soft, n_soft = soft * height, soft * east, soft * north
    h_slope = slope * height
    flow_e, flow_n = flow * east, flow * north
    new_h = (
        (rolled(h_soft + flow_e, 1, 1) + rolled(h_soft - flow_e, -1, 1))
        + (rolled(h_soft + flow_n, 1, 0) + rolled(h_soft - flow_n, -1, 0))
        + stay * height
    )
    new_e = (
        (rolled(e_soft + h_slope, 1, 1) + rolled(e_soft - h_slope, -1, 1))
        + (rolled(e_soft, 1, 0) + rolled(e_soft, -1, 0))
        + (stay * east + turn * north)
    )
    new_n = (
        (rolled(n_soft, 1, 1) + rolled(n_soft, -1, 1))
        + (rolled(n_soft + h_slope, 1, 0) + rolled(n_soft - h_slope, -1, 0))
        + (stay * north - turn * east)
    )
    return new_h, new_e, new_n


def tendency(q, half_depth):
    return advanced(q, half_depth, 1.0, 0.0)


def stepped(q, step_depth):
    return advanced(q, step_depth, DT, 1.0)


def last_body(nodes, last_out, edge_out, sem):
    rows = last_out.shape[1]
    copy = pltpu.make_async_copy(nodes.at[2], last_out, sem)
    copy.start()
    copy.wait()
    for f in range(3):
        for r in range(DEEP):
            edge_out[0, DEEP * f + r] = last_out[f, r : r + 1, :]
            edge_out[1, DEEP * f + r] = last_out[f, rows - DEEP + r : rows - DEEP + r + 1, :]


def blend_body(nodes, depth, base_out, bend_out, edge_out):
    rows = depth.shape[0]
    for f in range(3):
        n0, n1, n2 = nodes[0, f], nodes[1, f], nodes[2, f]
        bend = (DT / 4.0) * (n0 - 2.0 * n1 + n2)
        base_out[f] = (DT / 24.0) * (8.0 * n1 - 7.0 * n0 - n2)
        bend_out[f] = bend
        for r in range(2):
            edge_out[0, 2 * f + r] = bend[r : r + 1]
            edge_out[1, 2 * f + r] = bend[rows - 2 + r : rows - 1 + r]
    for r in range(DEEP):
        edge_out[0, 6 + r] = depth[r : r + 1, :]
        edge_out[1, 6 + r] = depth[rows - DEEP + r : rows - DEEP + r + 1, :]


def edge_body(first_ref, base, prev_edge, init, edge_out):
    rows = base.shape[1]
    first = first_ref[0] == 1
    for f in range(3):
        for side, lo in ((0, 0), (1, rows - DEEP)):
            for r in range(DEEP):
                at = slice(lo + r, lo + r + 1)
                start = jnp.where(first, init[f, at, :], prev_edge[side, DEEP * f + r])
                edge_out[side, DEEP * f + r] = HALF * start + base[f, at, :]


def with_halo(own, low, high, first, deep, state):
    rows = own.shape[0]
    state[:rows, :] = own
    state[rows:, :] = jnp.zeros((TILE, own.shape[1]), jnp.float32)
    for r in range(deep):
        state[rows + r : rows + r + 1, :] = low[first + r]
        state[rows + TILE - deep + r : rows + TILE - deep + r + 1, :] = high[first + r]


def fine_body(
    width, reach, first_ref, base, bend, prev, init, depth, low, high, low_early, high_early,
    msg_out, b_out, v_out, depth_out, state,
):
    rows, _ = depth.shape
    first = first_ref[0] == 1
    with_halo(depth[...], low_early, high_early, 6, DEEP, depth_out)
    half_depth = 0.5 * depth_out[...]
    for f in range(3):
        start = jnp.where(first, init[f], prev[f])
        with_halo(HALF * start + base[f], low, high, DEEP * f, DEEP, state.at[f])
        with_halo(bend[f], low_early, high_early, 2 * f, 2, state.at[3 + f])
    g = tuple(state[f] for f in range(3))
    k = tuple(state[3 + f] for f in range(3))
    fg = tendency(g, half_depth)
    u = tendency(fg, half_depth)
    v = tendency(tuple(x + HALF * y for x, y in zip(k, fg)), half_depth)
    fv = tendency(v, half_depth)
    for f in range(3):
        b = DT * (u[f][:rows] + (1.0 / 6.0) * fv[f][:rows])
        v_out[f] = v[f][:rows]
        b_out[f] = b
        pack_blocks(b, f, width, reach, msg_out)


def dense(width, reach, rows):
    return width % LANES == 0 and 2 * reach <= 32 and rows % TILE == 0


def packed_rows(rows, width, reach):
    if not dense(width, reach, rows):
        return None
    tiles = 3 * rows // TILE
    return 3 * rows * (width // LANES) + TILE * -(-tiles // 4)


def pack_blocks(b, f, width, reach, msg_out):
    rows, cols = b.shape
    lane = lax.broadcasted_iota(jnp.int32, (rows, LANES), 1)
    if dense(width, reach, rows):
        small = lax.broadcasted_iota(jnp.int32, (TILE, LANES), 1)
        parts = width // LANES
        for j in range(msg_out.shape[0]):
            for t in range(parts):
                at = j * width + t * LANES
                msg_out[j, (f * parts + t) * rows : (f * parts + t + 1) * rows, :] = b[:, at : at + LANES]
            after = (j + 1) * width % cols
            before = (j * width - LANES) % cols
            halo = jnp.where(lane < LANES // 2, b[:, after : after + LANES], b[:, before : before + LANES])
            put_halo(halo, f * rows // TILE, 3 * parts * rows, small, msg_out.at[j])
        return
    span = msg_out.shape[2]
    for j in range(msg_out.shape[0]):
        turned = rolled(b, -j * width, 1)
        parts = [turned[:, t : t + LANES] for t in range(0, span, LANES)]
        parts[-1] = jnp.where(lane < LANES - reach, parts[-1], turned[:, cols - LANES :])
        for t, part in enumerate(parts):
            msg_out[j, f * rows : (f + 1) * rows, t * LANES : (t + 1) * LANES] = part


def put_halo(halo, tile, base, small, out):
    for i in range(halo.shape[0] // TILE):
        q = (tile + i) % 4
        at = base + (tile + i) // 4 * TILE
        moved = rolled(halo[i * TILE : (i + 1) * TILE], 16 + 32 * q, 1)
        if q:
            moved = jnp.where(small >= 32 * q, moved, out[at : at + TILE, :])
        out[at : at + TILE, :] = moved


def get_halo(source, tile, count, base):
    found = []
    for i in range(tile, tile + count):
        at = base + i // 4 * TILE
        found.append(rolled(source[at : at + TILE, :], -(16 + 32 * (i % 4)), 1))
    return jnp.concatenate(found, axis=0)


def block_of(message, f, rows, width, reach):
    if not dense(width, reach, rows):
        return message[f * rows : (f + 1) * rows, :]
    parts = width // LANES
    main = [message[(f * parts + t) * rows : (f * parts + t + 1) * rows, :] for t in range(parts)]
    return jnp.concatenate(main + [get_halo(message, f * rows // TILE, rows // TILE, 3 * parts * rows)], axis=1)


def gathered(recv, slot, spaces, rows, width, reach):
    return tuple(
        jnp.concatenate(
            [block_of(recv.at[slot * spaces + y], f, rows, width, reach) for y in range(spaces)], axis=0
        )
        for f in range(3)
    )


def total_body(spaces, rows, width, reach, recv, depth_ref, x0, total_out):
    slots = recv.shape[0] // spaces
    step_depth = HALF * depth_ref[...]
    q = tuple(x0[f] for f in range(3))
    for slot in range(slots):
        b = gathered(recv, slot, spaces, rows, width, reach)
        q = tuple(x + y for x, y in zip(b, stepped(q, step_depth)))
    all_rows = rows * spaces
    if not dense(width, reach, rows):
        for f in range(3):
            total_out[f * all_rows : (f + 1) * all_rows, :] = q[f]
        return
    small = lax.broadcasted_iota(jnp.int32, (TILE, LANES), 1)
    parts = width // LANES
    for f in range(3):
        for t in range(parts):
            total_out[(f * parts + t) * all_rows : (f * parts + t + 1) * all_rows, :] = q[f][
                :, t * LANES : (t + 1) * LANES
            ]
        put_halo(q[f][:, width:], f * all_rows // TILE, 3 * parts * all_rows, small, total_out)


def chain_body(spaces, rows, width, reach, lower_ref, recv, depth_ref, x0, carry, msg_out):
    slots = recv.shape[0] // spaces
    all_rows = rows * spaces
    step_depth = HALF * depth_ref[...]
    lower = lower_ref[0] == 1
    q = tuple(jnp.where(lower, x0[f], block_of(carry, f, all_rows, width, reach)) for f in range(3))
    for slot in range(slots):
        for y in range(spaces):
            at = slot * spaces + y
            for f in range(3):
                here = q[f][:, :width]
                lo, hi = y * rows, (y + 1) * rows
                msg_out[at, f * rows : (f + 1) * rows, :] = here[lo:hi]
                before, after = (lo - 1) % all_rows, hi % all_rows
                msg_out[at, 3 * rows + f : 3 * rows + f + 1, :] = here[before : before + 1]
                msg_out[at, 3 * rows + 3 + f : 3 * rows + 4 + f, :] = here[after : after + 1]
            msg_out[at, 3 * rows + 6 :, :] = jnp.zeros((2, width), jnp.float32)
        if slot + 1 < slots:
            b = gathered(recv, slot, spaces, rows, width, reach)
            q = tuple(x + y for x, y in zip(b, stepped(q, step_depth)))


def finish_body(recv, b_ref, v_ref, depth_ref, out, state, made, sems):
    rows = b_ref.shape[1]
    pieces, _, width = recv.shape
    for f in range(3):
        state[f, rows:, :] = jnp.zeros((TILE, state.shape[2]), jnp.float32)
        for j in range(pieces):
            cut = slice(j * width, (j + 1) * width)
            state[f, :rows, cut] = recv[j, f * rows : (f + 1) * rows, :]
            state[f, rows + TILE - 1 : rows + TILE, cut] = recv[j, 3 * rows + f : 3 * rows + f + 1, :]
            state[f, rows : rows + 1, cut] = recv[j, 3 * rows + 3 + f : 3 * rows + 4 + f, :]
    copies = [
        pltpu.make_async_copy(state.at[f, pl.ds(0, rows), :], out.at[0, f], sems.at[f]) for f in range(3)
    ]
    for copy in copies:
        copy.start()
    q = tuple(state[f] for f in range(3))
    after = stepped(q, HALF * depth_ref[...])
    for f in range(3):
        begin = q[f][:rows]
        end = b_ref[f] + after[f][:rows]
        made[0, f] = 0.5 * ((begin + end) - v_ref[f])
        made[1, f] = end
        for part in range(2):
            copy = pltpu.make_async_copy(made.at[part, f], out.at[part + 1, f], sems.at[3 + 2 * f + part])
            copy.start()
            copies.append(copy)
    for copy in copies:
        copy.wait()


def kernel(body, shapes, *args, scalars=0, far_in=(), far_out=False, **more):
    def spec(far):
        return pl.BlockSpec(memory_space=pltpu.HBM if far else pltpu.VMEM)

    smem = pl.BlockSpec(memory_space=pltpu.SMEM)
    many = isinstance(shapes, list)
    outs = [jax.ShapeDtypeStruct(s, jnp.float32) for s in (shapes if many else [shapes])]
    return pl.pallas_call(
        body,
        out_shape=outs if many else outs[0],
        in_specs=[smem if i < scalars else spec(i in far_in) for i in range(len(args))],
        out_specs=[spec(far_out)] * len(outs) if many else spec(far_out),
        compiler_params=pltpu.CompilerParams(vmem_limit_bytes=VMEM_BYTES),
        **more,
    )(*args)


def swap_rows(edges):
    count = lax.axis_size("space")
    if count == 2:
        both = lax.ppermute(edges, "space", [(0, 1), (1, 0)])
        return both[0], both[1]
    below = lax.ppermute(edges[0], "space", [((i + 1) % count, i) for i in range(count)])
    above = lax.ppermute(edges[1], "space", [(i, (i + 1) % count) for i in range(count)])
    return below, above


def per_device(fine_nodes, init_state, mean_depth):
    nodes = fine_nodes[0]
    rows, cols = nodes.shape[-2:]
    outer, inner, spaces = lax.axis_size("outer"), lax.axis_size("inner"), lax.axis_size("space")
    group = ("inner", "space")
    owners = inner * spaces
    width = cols // owners
    slices = outer * inner
    reach = slices - 1
    span = -(-(width + 2 * reach) // LANES) * LANES
    at_outer, at_inner = lax.axis_index("outer"), lax.axis_index("inner")
    first = (at_outer * inner + at_inner == 0).astype(jnp.int32).reshape(1)
    lower = (at_outer == 0).astype(jnp.int32).reshape(1)
    onward_pairs = [(i, i + 1) for i in range(slices - 1)]
    state = (3, rows, cols)

    last, last_edge = kernel(
        last_body, [state, (2, 3 * DEEP, 1, cols)], nodes, far_in=(0,),
        scratch_shapes=[pltpu.SemaphoreType.DMA],
    )
    prev_edge = lax.ppermute(last_edge, ("outer", "inner"), onward_pairs)
    prev = lax.ppermute(last, ("outer", "inner"), onward_pairs)

    base, bend, early = kernel(blend_body, [state, state, (2, 9, 1, cols)], nodes, mean_depth)
    low_early, high_early = swap_rows(early)

    edges = kernel(edge_body, (2, 3 * DEEP, 1, cols), first, base, prev_edge, init_state, scalars=1)
    low, high = swap_rows(edges)

    fixed = jnp.concatenate([mean_depth[None], init_state], axis=0)
    onward = jnp.concatenate([fixed, fixed[..., :span]], axis=-1)
    behind = jnp.concatenate([fixed[..., cols - span :], fixed], axis=-1)
    lane = lax.broadcasted_iota(jnp.int32, (4, rows, span), 2)
    windows = []
    for y in range(spaces):
        start = (at_inner * spaces + y) * width
        ahead = lax.dynamic_slice_in_dim(onward, start, span, axis=2)
        back = lax.dynamic_slice_in_dim(behind, start, span, axis=2)
        windows.append(jnp.where(lane < span - reach, ahead, back))
    windows = lax.all_to_all(jnp.stack(windows), "space", 0, 0, tiled=True)
    windows = windows.transpose(1, 0, 2, 3).reshape(4, spaces * rows, span)
    depth_block, init_block = windows[0], windows[1:]

    tight = packed_rows(rows, width, reach)
    msg_shape = (owners, tight, LANES) if tight else (owners, 3 * rows, span)
    tight = packed_rows(spaces * rows, width, reach)
    total_shape = (tight, LANES) if tight else (3 * spaces * rows, span)
    msgs, drift, vee, depth = kernel(
        functools.partial(fine_body, width, reach),
        [msg_shape, state, state, (rows + TILE, cols)],
        first, base, bend, prev, init_state, mean_depth, low, high, low_early, high_early,
        scalars=1,
        scratch_shapes=[pltpu.VMEM((6, rows + TILE, cols), jnp.float32)],
    )
    recv = lax.all_to_all(msgs, group, 0, 0, tiled=True)
    plan = (spaces, rows, width, reach)
    total = kernel(functools.partial(total_body, *plan), total_shape, recv, depth_block, init_block)
    carry = lax.ppermute(total, "outer", [(i, i + 1) for i in range(outer - 1)])
    back = kernel(
        functools.partial(chain_body, *plan), (owners, 3 * rows + TILE, width),
        lower, recv, depth_block, init_block, carry, scalars=1,
    )
    mine = lax.all_to_all(back, group, 0, 0, tiled=True)
    if width % LANES:
        mine = mine.transpose(1, 0, 2).reshape(1, 3 * rows + TILE, cols)
    out = kernel(
        finish_body, (3,) + state, mine, drift, vee, depth, far_out=True,
        scratch_shapes=[
            pltpu.VMEM((3, rows + TILE, cols), jnp.float32),
            pltpu.VMEM((2,) + state, jnp.float32),
            pltpu.SemaphoreType.DMA((9,)),
        ],
    )
    return out[None]


def solution(mesh):
    slices, spaces = mesh.shape["tm"], mesh.shape["space"]
    split = Mesh(mesh.devices.reshape(2, slices // 2, spaces), ("outer", "inner", "space"))
    nodes = P(("outer", "inner"), None, None, "space", None)
    return jax.shard_map(
        per_device,
        mesh=split,
        in_specs=(nodes, P(None, "space", None), P("space", None)),
        out_specs=nodes,
        check_vma=False,
    )
```

time: 113 us -> 88.1 us (0.78)
  Pallas kernels: 21.4 us -> 10.4 us
  waiting for transfers between devices: 32.2 us -> 23.6 us
  starting transfers between devices: 29.2 us -> 22.7 us
  local copies, waits for them, and re-layouts: 6 us -> 8.07 us
    all_to_all x1, starting transfers between devices: 17 us -> 3.94 us  [per_device(): recv = lax.all_to_all(msgs, group, 0, 0, tiled=True)]
    pallas_call x5 -> x7, Pallas kernels: 21.4 us -> 10.4 us  [kernel(): pl.pallas_call(body, out_shape=outs if many else outs[0], in_specs=[smem...]
    ppermute x3 -> x4, starting transfers between devices: 3.75 us -> 10.6 us  [the longest x1 4.6 us: per_device(): prev_edge = lax.ppermute(last_edge, ('outer', 'inner'), onward_pairs)]
    ppermute x3 -> x4, waiting for transfers between devices: 11.4 us -> 7.73 us  [the longest x2 7.72 us: swap_rows(): both = lax.ppermute(edges, 'space', [(0, 1), (1, 0)])]
    all_to_all x1, waiting for transfers between devices: 16.4 us -> 12.9 us  [per_device(): recv = lax.all_to_all(msgs, group, 0, 0, tiled=True)]
    unnamed x8 -> x18, local copies, waits for them, and re-layouts: 2.56 us -> 5.31 us
    ppermute x1, waiting for transfers between devices: 4.44 us -> 2.99 us  [per_device(): carry = lax.ppermute(total, 'outer', [(i, i + 1) for i in range(outer - 1)])]
    squeeze x1 -> x0, local copies, waits for them, and re-layouts: 1.18 us -> none  [per_device(): nodes[2]]
  transfers between devices with their start and end apart: 6 -> 7, of which waited for: 4 -> 3; matrix products, arithmetic and copies ran while one was open for 4% -> 7% of each run, Pallas kernels for 9% -> 6%
where the time goes in v2:
time: 88.1 us; the launch traced here: 87.5 us
  waiting for transfers between devices  23.6 us (27%)
  starting transfers between devices  22.7 us (26%)
  blocking collectives  19.2 us (22%)
  Pallas kernels  10.4 us (12%)
  local copies, waits for them, and re-layouts  8.07 us (9%)
  other arithmetic  3.28 us (4%)
    all_to_all x1, blocking collectives, per_device(): mine = lax.all_to_all(back, group, 0, 0, tiled=True)  19.2 us
    all_to_all x1, waiting for transfers between devices, per_device(): recv = lax.all_to_all(msgs, group, 0, 0, tiled=True)  12.9 us
    pallas_call x7, Pallas kernels, kernel(): pl.pallas_call(body, out_shape=outs if many else outs[0], in_specs=[smem...  10.4 us
    ppermute x2, waiting for transfers between devices, swap_rows(): both = lax.ppermute(edges, 'space', [(0, 1), (1, 0)])  7.72 us
    unnamed x18, local copies, waits for them, and re-layouts  5.31 us
    ppermute x1, starting transfers between devices, per_device(): prev_edge = lax.ppermute(last_edge, ('outer', 'inner'), onward_pairs)  4.6 us
    ppermute x1, starting transfers between devices, per_device(): carry = lax.ppermute(total, 'outer', [(i, i + 1) for i in range(outer - 1)])  4.13 us
    all_to_all x1, starting transfers between devices, per_device(): windows = lax.all_to_all(jnp.stack(windows), 'space', 0, 0, tiled=True)  4.08 us
  transfers between devices with their start and end apart: 7, of which 3 were waited for; matrix products, arithmetic and copies ran while one was open for 7% of the time, Pallas kernels for 6%

profile of v2, /device:TPU:0, one launch (start us, length us, event | category | flops | bytes accessed | tf_op | source)
XLA Modules:
  0.0 87.5 jit_solution(16913574796209288345)
XLA Ops:
  0.0 0.0 copy-start
  0.0 1.7 %copy-done = f32[1,3,3,16,4096]{4,3,2,1,0:T(8,128)S(1)} copy-done((f32[1,3,3,16,4096]{4,3,2,1,0:T(8,128)S(1)}, f32[1,3,3,16,4096]{4,3,2,1,0:T(8,128)}, u32[]{:S(2)}) %copy-start) | copy-done | bytes 2359320
  1.7 0.0 copy-start.2
  1.7 1.0 %shard_map.38 = (f32[3,16,4096]{2,1,0:T(8,128)}, f32[2,9,1,4096]{3,2,1,0:T(1,128)S(1)}) custom-call(f32[3,3,16,4096]{3,2,1,0:T(8,128)S(1)} %bitcast.20), custom_call_target="tpu_custom_call" | custom-call | tf_op jit(solution)/shard_map/pallas_call | solution.py:281
  2.6 2.4 %collective-permute-start = (f32[3,16,4096]{2,1,0:T(8,128)}, f32[3,16,4096]{2,1,0:T(8,128)S(1)}, u32[]{:S(2)}, u32[]{:S(2)}) collective-permute-start(f32[3,16,4096]{2,1,0:T(8,128)} %get-tuple-element.16), channel_id=1, source_target_pairs={{0,2},{2,4},{4,6},{6,8},{8,10},{10,12},{12,14},{14,16},{16,18},{18... | collective-permute-start | bytes 2359304 | tf_op jit(solution)/shard_map/ppermute | solution.py:322
  5.1 0.0 copy-start.1
  5.1 4.6 %collective-permute-start.1 = (f32[2,9,1,4096]{3,2,1,0:T(1,128)S(1)}, f32[2,9,1,4096]{3,2,1,0:T(1,128)S(1)}, u32[]{:S(2)}, u32[]{:S(2)}) collective-permute-start(f32[2,9,1,4096]{3,2,1,0:T(1,128)S(1)} %get-tuple-element.17), channel_id=1, source_target_pairs={{0,2},{2,4},{4,6},{6,8},{8,10},{10,12},{12,14},{14,16},{16,18},{18... | collective-permute-start | bytes 884744 | tf_op jit(solution)/shard_map/ppermute | solution.py:321
  9.7 0.0 copy-done.2
  9.7 0.3 shard_map.37
  10.1 0.0 copy-start.5
  10.1 0.9 copy-done.5
  10.9 1.5 %collective-permute-start.3 = (f32[2,9,1,4096]{3,2,1,0:T(1,128)S(1)}, f32[2,9,1,4096]{3,2,1,0:T(1,128)}, u32[]{:S(2)}, u32[]{:S(2)}) collective-permute-start(f32[2,9,1,4096]{3,2,1,0:T(1,128)S(1)} %get-tuple-element.18), channel_id=1, source_target_pairs={{0,1},{1,0},{2,3},{3,2},{4,5},{5,4},{6,7},{7,6},{8,9},{9,8},{10,11... | collective-permute-start | bytes 884744 | tf_op jit(solution)/shard_map/ppermute | solution.py:294
  12.5 0.0 copy-done.1
  12.5 1.5 %fusion.1 = (f32[4,16,4480]{2,1,0:T(8,128)}, f32[4,16,4480]{2,1,0:T(8,128)}) fusion(f32[3,16,4096]{2,1,0:T(8,128)S(1)} %copy-done.1, f32[1,16,4096]{2,1,0:T(8,128)S(1)} %bitcast.22), kind=kLoop, calls=%fused_computation.3 | loop fusion | flops 1720320 | bytes 3342336 | tf_op jit(solution)/shard_map/concatenate | solution.py:331
  14.0 1.1 %select_bitcast_fusion.1 = (f32[1,4,16,384]{3,2,1,0:T(8,128)S(1)}, f32[1,4,16,384]{3,2,1,0:T(8,128)S(1)}) fusion(f32[4,16,4480]{2,1,0:T(8,128)} %get-tuple-element.26, s32[]{:T(128)S(6)} %select_n.15, f32[4,16,4480]{2,1,0:T(8,128)} %get-tuple-element.25, pred[384]{0:T(512)(128)(4,1)S(1)} %iota_compare_fusion, s32[]{:T(128)S(6)} %select_n.17), kind=kLoop, calls=%fused_computation.10 | loop fusion | flops 49152 | bytes 590216 | tf_op jit(solution)/shard_map/stack | solution.py:340
  15.1 0.7 pad_maximum_fusion.2
  15.8 4.1 %all-to-all-start.1 = ((f32[2,4,16,384]{3,2,1,0:T(8,128)}), f32[2,4,16,384]{3,2,1,0:T(8,128)}, u32[]{:S(2)}, u32[]{:S(2)}) async-start(f32[2,4,16,384]{3,2,1,0:T(8,128)} %pad_maximum_fusion.2), calls=%async_computation.1 | async-start | bytes 393216 | tf_op jit(solution)/shard_map/all_to_all | solution.py:340
  19.9 0.0 collective-permute-done.1.prev_edge
  19.9 0.0 copy-start.6
  19.9 0.1 shard_map.39
  20.0 2.0 %collective-permute-start.2 = (f32[2,9,1,4096]{3,2,1,0:T(1,128)S(1)}, f32[2,9,1,4096]{3,2,1,0:T(1,128)S(1)}, u32[]{:S(2)}, u32[]{:S(2)}) collective-permute-start(f32[2,9,1,4096]{3,2,1,0:T(1,128)S(1)} %shard_map.39), channel_id=1, source_target_pairs={{0,1},{1,0},{2,3},{3,2},{4,5},{5,4},{6,7},{7,6},{8,9},{9,8},{10,11... | collective-permute-start | bytes 884744 | tf_op jit(solution)/shard_map/ppermute | solution.py:294
  22.0 0.0 collective-permute-done.3
  22.0 1.0 %slice_bitcast_fusion = (f32[9,1,4096]{2,1,0:T(1,128)S(1)}, f32[9,1,4096]{2,1,0:T(1,128)S(1)}) fusion(f32[2,9,1,4096]{3,2,1,0:T(1,128)} %collective-permute-done.3), kind=kLoop, calls=%fused_computation.5 | loop fusion | bytes 589824 | tf_op jit(solution)/shard_map/squeeze | solution.py:295
  23.0 7.7 %collective-permute-done.2 = f32[2,9,1,4096]{3,2,1,0:T(1,128)S(1)} collective-permute-done((f32[2,9,1,4096]{3,2,1,0:T(1,128)S(1)}, f32[2,9,1,4096]{3,2,1,0:T(1,128)S(1)}, u32[]{:S(2)}, u32[]{:S(2)}) %collective-permute-start.2) | collective-permute-done | bytes 294944 | tf_op jit(solution)/shard_map/ppermute | solution.py:294
  30.8 0.0 collective-permute-done.prev
  30.8 0.0 copy-start.3
  30.8 0.9 copy-done.3
  31.7 0.0 copy-done.6
  31.7 0.0 copy-start.4
  31.7 1.1 %copy-done.4 = f32[3,16,4096]{2,1,0:T(8,128)S(1)} copy-done((f32[3,16,4096]{2,1,0:T(8,128)S(1)}, f32[3,16,4096]{2,1,0:T(8,128)}, u32[]{:S(2)}) %copy-start.4) | copy-done | bytes 786456
  32.8 4.8 %shard_map.40 = (f32[16,112,128]{2,1,0:T(8,128)}, f32[3,16,4096]{2,1,0:T(8,128)S(1)}, f32[3,16,4096]{2,1,0:T(8,128)S(1)}, f32[24,4096]{1,0:T(8,128)S(1)}) custom-call(s32[1]{0:T(128)} %bitcast.1.first_ref, f32[3,16,4096]{2,1,0:T(8,128)S(1)} %get-tuple-element.14.base, f32[3,16,4096]{2,1,0:T(8,128)S(1)} %copy-done.6, f32[3,16,4096]{2,1,0:T(8,128)S(1)} %copy-done.4, ...), custom_call_target="tpu_custom_call" | custom-call | tf_op jit(solution)/shard_map/pallas_call | solution.py:281
  37.6 0.0 copy-start.7
  37.6 0.7 copy-done.7
  38.4 0.0 all-to-all-done.1
  38.4 3.9 %all-to-all-start = ((f32[16,112,128]{2,1,0:T(8,128)}), f32[16,112,128]{2,1,0:T(8,128)S(1)}, u32[]{:S(2)}, u32[]{:S(2)}) async-start(f32[16,112,128]{2,1,0:T(8,128)} %get-tuple-element.19), calls=%async_computation | async-start | bytes 1835008 | tf_op jit(solution)/shard_map/all_to_all | solution.py:355
  42.3 0.8 slice.41
  43.2 0.9 %slice.42 = f32[3,2,16,384]{3,2,0,1:T(8,128)S(1)} slice(f32[4,2,16,384]{3,2,0,1:T(8,128)} %bitcast.10), slice={[1:4], [0:2], [0:16], [0:384]} | slice | bytes 294912 | tf_op jit(solution)/shard_map/slice | solution.py:342
  44.1 12.9 %all-to-all-done.recv = f32[16,112,128]{2,1,0:T(8,128)S(1)} async-done(((f32[16,112,128]{2,1,0:T(8,128)}), f32[16,112,128]{2,1,0:T(8,128)S(1)}, u32[]{:S(2)}, u32[]{:S(2)}) %all-to-all-start) | async-done | bytes 917536 | tf_op jit(solution)/shard_map/all_to_all | solution.py:355
  57.0 1.2 %shard_map.41 = f32[216,128]{1,0:T(8,128)S(1)} custom-call(f32[16,112,128]{2,1,0:T(8,128)S(1)} %all-to-all-done.recv, f32[32,384]{1,0:T(8,128)S(1)} %bitcast.25, f32[3,32,384]{2,1,0:T(8,128)S(1)} %bitcast.23), custom_call_target="tpu_custom_call" | custom-call | tf_op jit(solution)/shard_map/pallas_call | solution.py:281
  58.2 4.1 %collective-permute-start.4 = (f32[216,128]{1,0:T(8,128)S(1)}, f32[216,128]{1,0:T(8,128)S(1)}, u32[]{:S(2)}, u32[]{:S(2)}) collective-permute-start(f32[216,128]{1,0:T(8,128)S(1)} %shard_map.41), channel_id=1, source_target_pairs={{0,16},{1,17},{2,18},{3,19},{4,20},{5,21},{6,22},{7,23},{8,24},{9,... | collective-permute-start | bytes 331784 | tf_op jit(solution)/shard_map/ppermute | solution.py:358
  62.3 3.0 %collective-permute-done.4.carry = f32[216,128]{1,0:T(8,128)S(1)} collective-permute-done((f32[216,128]{1,0:T(8,128)S(1)}, f32[216,128]{1,0:T(8,128)S(1)}, u32[]{:S(2)}, u32[]{:S(2)}) %collective-permute-start.4) | collective-permute-done | bytes 110624 | tf_op jit(solution)/shard_map/ppermute | solution.py:358
  65.3 1.0 %shard_map.42 = f32[16,56,256]{2,1,0:T(8,128)S(1)} custom-call(s32[1]{0:T(128)} %bitcast.lower_ref, f32[16,112,128]{2,1,0:T(8,128)S(1)} %all-to-all-done.recv, f32[32,384]{1,0:T(8,128)S(1)} %bitcast.26, f32[3,32,384]{2,1,0:T(8,128)S(1)} %bitcast.24, f32[216,128]{1,0:T(8,128)S(1)} %collective-permute-done.4.carry), custom_call_target="tpu_custom_call" | custom-call | tf_op jit(solution)/shard_map/pallas_call | solution.py:281
  66.3 0.0 copy-start.8
  66.4 19.2 %all_to_all.15.recv = f32[16,56,256]{2,1,0:T(8,128)S(1)} all-to-all(f32[16,56,256]{2,1,0:T(8,128)S(1)} %shard_map.42), channel_id=1, replica_groups=mesh['outer'=2,'inner'=8,'space'=2] {'inner','space'}, dimensions={0} | all-to-all | bytes 1835008 | tf_op jit(solution)/shard_map/all_to_all | solution.py:363
  85.6 0.0 copy-done.8
  85.6 2.0 %shard_map.43 = f32[3,3,16,4096]{3,2,1,0:T(8,128)} custom-call(f32[16,56,256]{2,1,0:T(8,128)S(1)} %all_to_all.15.recv, f32[3,16,4096]{2,1,0:T(8,128)S(1)} %get-tuple-element.20.b_ref, f32[3,16,4096]{2,1,0:T(8,128)S(1)} %get-tuple-element.21.v_ref, f32[24,4096]{1,0:T(8,128)S(1)} %copy-done.8), custom_call_target="tpu_custom_call" | custom-call | tf_op jit(solution)/shard_map/pallas_call | solution.py:281
  (3 shorter events, 0.0 us)
Async XLA Ops:
  0.0 1.7 %copy-start = (f32[1,3,3,16,4096]{4,3,2,1,0:T(8,128)S(1)}, f32[1,3,3,16,4096]{4,3,2,1,0:T(8,128)}, u32[]{:S(2)}) copy-start(f32[1,3,3,16,4096]{4,3,2,1,0:T(8,128)} %param.3) | copy-start | bytes 7077892
  1.7 8.0 %copy-start.2 = (f32[16,4096]{1,0:T(8,128)S(1)}, f32[16,4096]{1,0:T(8,128)}, u32[]{:S(2)}) copy-start(f32[16,4096]{1,0:T(8,128)} %depth.3) | copy-start | bytes 786436
  2.6 28.2 %collective-permute-start = (f32[3,16,4096]{2,1,0:T(8,128)}, f32[3,16,4096]{2,1,0:T(8,128)S(1)}, u32[]{:S(2)}, u32[]{:S(2)}) collective-permute-start(f32[3,16,4096]{2,1,0:T(8,128)} %get-tuple-element.16), channel_id=1, source_target_pairs={{0,2},{2,4},{4,6},{6,8},{8,10},{10,12},{12,14},{14,16},{16,18},{18... | collective-permute-start | bytes 2359304 | tf_op jit(solution)/shard_map/ppermute | solution.py:322
  5.1 7.4 %copy-start.1 = (f32[3,16,4096]{2,1,0:T(8,128)S(1)}, f32[3,16,4096]{2,1,0:T(8,128)}, u32[]{:S(2)}) copy-start(f32[3,16,4096]{2,1,0:T(8,128)} %init.3) | copy-start | bytes 2359300
  5.1 14.8 %collective-permute-start.1 = (f32[2,9,1,4096]{3,2,1,0:T(1,128)S(1)}, f32[2,9,1,4096]{3,2,1,0:T(1,128)S(1)}, u32[]{:S(2)}, u32[]{:S(2)}) collective-permute-start(f32[2,9,1,4096]{3,2,1,0:T(1,128)S(1)} %get-tuple-element.17), channel_id=1, source_target_pairs={{0,2},{2,4},{4,6},{6,8},{8,10},{10,12},{12,14},{14,16},{16,18},{18... | collective-permute-start | bytes 884744 | tf_op jit(solution)/shard_map/ppermute | solution.py:321
  10.1 0.9 %copy-start.5 = (f32[3,16,4096]{2,1,0:T(8,128)}, f32[3,16,4096]{2,1,0:T(8,128)S(1)}, u32[]{:S(2)}) copy-start(f32[3,16,4096]{2,1,0:T(8,128)S(1)} %get-tuple-element.15.bend) | copy-start | bytes 2359300
  10.9 11.1 %collective-permute-start.3 = (f32[2,9,1,4096]{3,2,1,0:T(1,128)S(1)}, f32[2,9,1,4096]{3,2,1,0:T(1,128)}, u32[]{:S(2)}, u32[]{:S(2)}) collective-permute-start(f32[2,9,1,4096]{3,2,1,0:T(1,128)S(1)} %get-tuple-element.18), channel_id=1, source_target_pairs={{0,1},{1,0},{2,3},{3,2},{4,5},{5,4},{6,7},{7,6},{8,9},{9,8},{10,11... | collective-permute-start | bytes 884744 | tf_op jit(solution)/shard_map/ppermute | solution.py:294
  15.8 22.6 %all-to-all-start.1 = ((f32[2,4,16,384]{3,2,1,0:T(8,128)}), f32[2,4,16,384]{3,2,1,0:T(8,128)}, u32[]{:S(2)}, u32[]{:S(2)}) async-start(f32[2,4,16,384]{3,2,1,0:T(8,128)} %pad_maximum_fusion.2), calls=%async_computation.1 | async-start | bytes 393216 | tf_op jit(solution)/shard_map/all_to_all | solution.py:340
  19.9 11.8 %copy-start.6 = (f32[3,16,4096]{2,1,0:T(8,128)S(1)}, f32[3,16,4096]{2,1,0:T(8,128)}, u32[]{:S(2)}) copy-start(f32[3,16,4096]{2,1,0:T(8,128)} %copy-done.5) | copy-start | bytes 2359300
  20.0 10.8 %collective-permute-start.2 = (f32[2,9,1,4096]{3,2,1,0:T(1,128)S(1)}, f32[2,9,1,4096]{3,2,1,0:T(1,128)S(1)}, u32[]{:S(2)}, u32[]{:S(2)}) collective-permute-start(f32[2,9,1,4096]{3,2,1,0:T(1,128)S(1)} %shard_map.39), channel_id=1, source_target_pairs={{0,1},{1,0},{2,3},{3,2},{4,5},{5,4},{6,7},{7,6},{8,9},{9,8},{10,11... | collective-permute-start | bytes 884744 | tf_op jit(solution)/shard_map/ppermute | solution.py:294
  30.8 0.9 %copy-start.3 = (f32[3,16,4096]{2,1,0:T(8,128)}, f32[3,16,4096]{2,1,0:T(8,128)S(1)}, u32[]{:S(2)}) copy-start(f32[3,16,4096]{2,1,0:T(8,128)S(1)} %collective-permute-done.prev) | copy-start | bytes 2359300
  31.7 1.1 %copy-start.4 = (f32[3,16,4096]{2,1,0:T(8,128)S(1)}, f32[3,16,4096]{2,1,0:T(8,128)}, u32[]{:S(2)}) copy-start(f32[3,16,4096]{2,1,0:T(8,128)} %copy-done.3) | copy-start | bytes 2359300
  37.6 0.7 copy-start.7
  38.4 18.6 %all-to-all-start = ((f32[16,112,128]{2,1,0:T(8,128)}), f32[16,112,128]{2,1,0:T(8,128)S(1)}, u32[]{:S(2)}, u32[]{:S(2)}) async-start(f32[16,112,128]{2,1,0:T(8,128)} %get-tuple-element.19), calls=%async_computation | async-start | bytes 1835008 | tf_op jit(solution)/shard_map/all_to_all | solution.py:355
  58.2 7.1 %collective-permute-start.4 = (f32[216,128]{1,0:T(8,128)S(1)}, f32[216,128]{1,0:T(8,128)S(1)}, u32[]{:S(2)}, u32[]{:S(2)}) collective-permute-start(f32[216,128]{1,0:T(8,128)S(1)} %shard_map.41), channel_id=1, source_target_pairs={{0,16},{1,17},{2,18},{3,19},{4,20},{5,21},{6,22},{7,23},{8,24},{9,... | collective-permute-start | bytes 331784 | tf_op jit(solution)/shard_map/ppermute | solution.py:358
  66.3 19.2 %copy-start.8 = (f32[24,4096]{1,0:T(8,128)S(1)}, f32[24,4096]{1,0:T(8,128)}, u32[]{:S(2)}) copy-start(f32[24,4096]{1,0:T(8,128)} %copy-done.7) | copy-start | bytes 1179652

commit v3 on v2

v3 whole, which is shorter than its diff:
```python
import functools

import jax
import jax.numpy as jnp
from jax import lax
from jax.experimental import pallas as pl
from jax.experimental.pallas import tpu as pltpu
from jax.sharding import Mesh
from jax.sharding import PartitionSpec as P


DT = 0.3
HALF = 0.5 * DT
NU = 1.0 / 3.0
FC = 0.5
DEEP = 3
TILE = 8
LANES = 128
VMEM_BYTES = 20 * 1024 * 1024


def rolled(x, by, axis):
    return pltpu.roll(x, by % x.shape[axis], axis)


def advanced(q, flow, scale, keep):
    height, east, north = q
    soft, slope, turn = scale * NU, scale * 0.5, scale * FC
    stay = keep - 4.0 * soft
    h_soft, e_soft, n_soft = soft * height, soft * east, soft * north
    h_slope = slope * height
    flow_e, flow_n = flow * east, flow * north
    new_h = (
        (rolled(h_soft + flow_e, 1, 1) + rolled(h_soft - flow_e, -1, 1))
        + (rolled(h_soft + flow_n, 1, 0) + rolled(h_soft - flow_n, -1, 0))
        + stay * height
    )
    new_e = (
        (rolled(e_soft + h_slope, 1, 1) + rolled(e_soft - h_slope, -1, 1))
        + (rolled(e_soft, 1, 0) + rolled(e_soft, -1, 0))
        + (stay * east + turn * north)
    )
    new_n = (
        (rolled(n_soft, 1, 1) + rolled(n_soft, -1, 1))
        + (rolled(n_soft + h_slope, 1, 0) + rolled(n_soft - h_slope, -1, 0))
        + (stay * north - turn * east)
    )
    return new_h, new_e, new_n


def tendency(q, half_depth):
    return advanced(q, half_depth, 1.0, 0.0)


def stepped(q, step_depth):
    return advanced(q, step_depth, DT, 1.0)


def dense(width, reach, rows):
    return width % LANES == 0 and 2 * reach <= 32 and rows % TILE == 0


def packed_rows(rows, width, reach):
    if not dense(width, reach, rows):
        return None
    tiles = 3 * rows // TILE
    return 3 * rows * (width // LANES) + TILE * -(-tiles // 4)


def cut(ref, lead, at, size=LANES):
    return ref[lead + (slice(None), pl.ds(pl.multiple_of(at, LANES), size))]


def prepare_body(spaces, width, reach, place, depth, init, edge_out, win_out):
    rows, cols = depth.shape
    for r in range(DEEP):
        edge_out[0, r] = depth[r : r + 1, :]
        edge_out[1, r] = depth[rows - DEEP + r : rows - DEEP + r + 1, :]
    lane = lax.broadcasted_iota(jnp.int32, (rows, LANES), 1)
    for y in range(spaces):
        start = place[2] * (cols // 2) + (place[3] * spaces + y) * width
        after = lax.rem(start + width, cols)
        before = lax.rem(start - LANES + cols, cols)
        for i in range(4):
            ref, lead = (depth, ()) if i == 0 else (init, (i - 1,))
            at = slice(i * rows, (i + 1) * rows)
            win_out[y, at, :width] = cut(ref, lead, start, width)
            win_out[y, at, width:] = jnp.where(
                lane < LANES - reach, cut(ref, lead, after), cut(ref, lead, before)
            )


def blend_body(nodes, depth, low, high, base_out, fk_out, ffk_out, depth_out, state):
    rows, cols = depth.shape
    none = jnp.zeros((TILE, cols), jnp.float32)
    depth_out[:rows, :] = 0.5 * depth[...]
    depth_out[rows:, :] = none
    for r in range(DEEP):
        depth_out[rows + r : rows + r + 1, :] = 0.5 * low[r]
        depth_out[rows + TILE - DEEP + r : rows + TILE - DEEP + r + 1, :] = 0.5 * high[r]
    for f in range(3):
        n0, n1, n2 = nodes[0, f], nodes[1, f], nodes[2, f]
        base_out[f] = (DT / 24.0) * (8.0 * n1 - 7.0 * n0 - n2)
        state[f, :rows, :] = (DT / 4.0) * (n0 - 2.0 * n1 + n2)
        state[f, rows:, :] = none
    half_depth = depth_out[...]
    fk = tendency(tuple(state[f] for f in range(3)), half_depth)
    ffk = tendency(fk, half_depth)
    for f in range(3):
        fk_out[f] = fk[f]
        ffk_out[f] = ffk[f]


def fine_body(place, base, prev, init, fk, ffk, depth_ref, b_out, v_out, give_out, spill_out, state):
    rows, cols = base.shape[1:]
    first = place[0] == 1
    half_depth = depth_ref[...]
    for f in range(3):
        state[f, :rows, :] = HALF * jnp.where(first, init[f], prev[f]) + base[f]
        state[f, rows:, :] = jnp.zeros((TILE, cols), jnp.float32)
    fg = tendency(tuple(state[f] for f in range(3)), half_depth)
    u = tendency(fg, half_depth)
    fu = tendency(u, half_depth)
    wide = rows + TILE
    for f in range(3):
        v_out[f] = fk[f] + HALF * u[f]
        b_out[f] = DT * (u[f] + (1.0 / 6.0) * (HALF * fu[f] + ffk[f]))
    theirs = (1 - place[2]) * (cols // 2) + (cols - LANES)
    for f in range(3):
        for t in range(give_out.shape[1] // LANES):
            at = lax.rem(theirs + t * LANES, cols)
            give_out[f * wide : (f + 1) * wide, t * LANES : (t + 1) * LANES] = cut(b_out, (f,), at)
    for f in range(3):
        for side, spread, edge in ((0, wide - DEEP, 0), (1, rows, rows - 1)):
            for r in range(DEEP):
                spill_out[side, DEEP * f + r] = b_out[f, spread + r : spread + r + 1, :]
            spill_out[side, 9 + f] = b_out[f, edge : edge + 1, :]
            spread = wide - 2 if side == 0 else rows
            for r in range(2):
                spill_out[side, 12 + 2 * f + r] = v_out[f, spread + r : spread + r + 1, :]


def mend_body(b_raw, v_raw, low, high, b_out, v_out):
    rows = v_out.shape[1]
    wide = rows + TILE
    for f in range(3):
        b_out[f] = b_raw[f]
        v_out[f] = v_raw[f, :rows, :]
        for r in range(DEEP):
            for at, more in ((r, high), (rows - DEEP + r, low)):
                b_out[f, at : at + 1, :] = b_raw[f, at : at + 1, :] + more[DEEP * f + r]
        for r in range(2):
            for at, more in ((r, high), (rows - 2 + r, low)):
                v_out[f, at : at + 1, :] = v_raw[f, at : at + 1, :] + more[12 + 2 * f + r]
        for at, more in ((rows, low), (wide - 1, high)):
            b_out[f, at : at + 1, :] = b_raw[f, at : at + 1, :] + more[9 + f]


def pair_body(width, reach, place, b_own, got, depth_ref, msg_out):
    wide, cols = b_own.shape[1:]
    tiles = got.shape[1] // LANES
    mine = place[2] * (cols // 2) + (cols - LANES)
    even = place[2] == 0

    def window(ref, lead):
        parts = [cut(ref, lead, lax.rem(mine + t * LANES, cols)) for t in range(tiles)]
        return jnp.concatenate(parts, axis=1)

    step_depth = DT * window(depth_ref, ())
    own = tuple(window(b_own, (f,)) for f in range(3))
    other = tuple(got[f * wide : (f + 1) * wide, :] for f in range(3))
    first = tuple(jnp.where(even, x, y) for x, y in zip(own, other))
    second = tuple(jnp.where(even, y, x) for x, y in zip(own, other))
    moved = stepped(first, step_depth)
    for f in range(3):
        pack_blocks(second[f] + moved[f], f, width, reach, msg_out)


def pack_blocks(b, f, width, reach, msg_out):
    rows, cols = b.shape
    lane = lax.broadcasted_iota(jnp.int32, (rows, LANES), 1)
    if dense(width, reach, rows):
        small = lax.broadcasted_iota(jnp.int32, (TILE, LANES), 1)
        parts = width // LANES
        for j in range(msg_out.shape[0]):
            for t in range(parts):
                at = LANES + j * width + t * LANES
                msg_out[j, (f * parts + t) * rows : (f * parts + t + 1) * rows, :] = b[:, at : at + LANES]
            after = LANES + (j + 1) * width
            before = j * width
            halo = jnp.where(lane < LANES // 2, b[:, after : after + LANES], b[:, before : before + LANES])
            put_halo(halo, f * rows // TILE, 3 * parts * rows, small, msg_out.at[j])
        return
    span = msg_out.shape[2]
    for j in range(msg_out.shape[0]):
        turned = rolled(b, -(LANES + j * width), 1)
        parts = [turned[:, t : t + LANES] for t in range(0, span, LANES)]
        parts[-1] = jnp.where(lane < LANES - reach, parts[-1], turned[:, cols - LANES :])
        for t, part in enumerate(parts):
            msg_out[j, f * rows : (f + 1) * rows, t * LANES : (t + 1) * LANES] = part


def put_halo(halo, tile, base, small, out):
    for i in range(halo.shape[0] // TILE):
        q = (tile + i) % 4
        at = base + (tile + i) // 4 * TILE
        moved = rolled(halo[i * TILE : (i + 1) * TILE], 16 + 32 * q, 1)
        if q:
            moved = jnp.where(small >= 32 * q, moved, out[at : at + TILE, :])
        out[at : at + TILE, :] = moved


def get_halo(source, tile, count, base):
    found = []
    for i in range(tile, tile + count):
        at = base + i // 4 * TILE
        found.append(rolled(source[at : at + TILE, :], -(16 + 32 * (i % 4)), 1))
    return jnp.concatenate(found, axis=0)


def block_of(message, f, rows, width, reach):
    if not dense(width, reach, rows):
        return message[f * rows : (f + 1) * rows, :]
    parts = width // LANES
    main = [message[(f * parts + t) * rows : (f * parts + t + 1) * rows, :] for t in range(parts)]
    return jnp.concatenate(main + [get_halo(message, f * rows // TILE, rows // TILE, 3 * parts * rows)], axis=1)


def joined(recv, slot, spaces, rows, width, reach):
    wide = rows + TILE
    fields = []
    for f in range(3):
        blocks = [block_of(recv.at[slot * spaces + y], f, wide, width, reach) for y in range(spaces)]
        row = lax.broadcasted_iota(jnp.int32, (TILE, blocks[0].shape[1]), 0)
        tiles = []
        for y in range(spaces):
            here = [blocks[y][t : t + TILE] for t in range(0, rows, TILE)]
            here[0] = here[0] + jnp.where(row < TILE // 2, blocks[(y - 1) % spaces][rows:], 0.0)
            here[-1] = here[-1] + jnp.where(row < TILE // 2, 0.0, blocks[(y + 1) % spaces][rows:])
            tiles += here
        fields.append(jnp.concatenate(tiles, axis=0))
    return tuple(fields)


def window_field(win, i, rows):
    return jnp.concatenate([win[y, i * rows : (i + 1) * rows, :] for y in range(win.shape[0])], axis=0)


def two_steps(q, step_depth):
    return stepped(stepped(q, step_depth), step_depth)


def total_body(spaces, rows, width, reach, recv, win, total_out):
    slots = recv.shape[0] // spaces
    step_depth = HALF * window_field(win, 0, rows)
    q = tuple(window_field(win, 1 + f, rows) for f in range(3))
    for slot in range(slots):
        b = joined(recv, slot, spaces, rows, width, reach)
        q = tuple(x + y for x, y in zip(b, two_steps(q, step_depth)))
    all_rows = rows * spaces
    if not dense(width, reach, rows):
        for f in range(3):
            total_out[f * all_rows : (f + 1) * all_rows, :] = q[f]
        return
    small = lax.broadcasted_iota(jnp.int32, (TILE, LANES), 1)
    parts = width // LANES
    for f in range(3):
        for t in range(parts):
            total_out[(f * parts + t) * all_rows : (f * parts + t + 1) * all_rows, :] = q[f][
                :, t * LANES : (t + 1) * LANES
            ]
        put_halo(q[f][:, width:], f * all_rows // TILE, 3 * parts * all_rows, small, total_out)


def chain_body(spaces, rows, width, reach, place, recv, win, carry, msg_out):
    slots = recv.shape[0] // spaces
    all_rows = rows * spaces
    step_depth = HALF * window_field(win, 0, rows)
    lower = place[1] == 1
    q = tuple(
        jnp.where(lower, window_field(win, 1 + f, rows), block_of(carry, f, all_rows, width, reach))
        for f in range(3)
    )
    for slot in range(slots):
        for y in range(spaces):
            at = slot * spaces + y
            for f in range(3):
                here = q[f][:, :width]
                lo, hi = y * rows, (y + 1) * rows
                msg_out[at, f * rows : (f + 1) * rows, :] = here[lo:hi]
                for r, source in enumerate((hi, hi + 1, lo - 2, lo - 1)):
                    source %= all_rows
                    to = 3 * rows + 4 * f + r
                    msg_out[at, to : to + 1, :] = here[source : source + 1]
            msg_out[at, 3 * rows + 12 :, :] = jnp.zeros((4, width), jnp.float32)
        if slot + 1 < slots:
            b = joined(recv, slot, spaces, rows, width, reach)
            q = tuple(x + y for x, y in zip(b, two_steps(q, step_depth)))


def finish_body(place, mine, other, b_own, b_lent, v_ref, depth_ref, out, state, made, sems):
    rows, cols = v_ref.shape[1:]
    wide = rows + TILE
    pieces, _, width = mine.shape
    even = place[2] == 0
    for f in range(3):
        state[f, rows:, :] = jnp.zeros((TILE, cols), jnp.float32)
        for source, half in ((mine, place[2]), (other, 1 - place[2])):
            for j in range(pieces):
                to = pl.ds(pl.multiple_of(half * (cols // 2) + j * width, LANES), width)
                state[f, :rows, to] = source[j, f * rows : (f + 1) * rows, :]
                for r, row in enumerate((rows, rows + 1, wide - 2, wide - 1)):
                    at = 3 * rows + 4 * f + r
                    state[f, row : row + 1, to] = source[j, at : at + 1, :]
    step_depth = DT * depth_ref[...]
    carried = tuple(state[f] for f in range(3))
    after = tuple(
        jnp.where(even, b_own[f], b_lent[f]) + x for f, x in enumerate(stepped(carried, step_depth))
    )
    last = stepped(after, step_depth)
    copies = []
    for f in range(3):
        begin = jnp.where(even, carried[f][:rows], after[f][:rows])
        end = jnp.where(even, after[f][:rows], b_own[f, :rows, :] + last[f][:rows])
        made[0, f] = begin
        made[1, f] = 0.5 * ((begin + end) - v_ref[f])
        made[2, f] = end
        for part in range(3):
            copy = pltpu.make_async_copy(made.at[part, f], out.at[part, f], sems.at[3 * f + part])
            copy.start()
            copies.append(copy)
    for copy in copies:
        copy.wait()


def kernel(body, shapes, *args, scalars=0, far_in=(), far_out=False, **more):
    def spec(far):
        return pl.BlockSpec(memory_space=pltpu.HBM if far else pltpu.VMEM)

    smem = pl.BlockSpec(memory_space=pltpu.SMEM)
    many = isinstance(shapes, list)
    outs = [jax.ShapeDtypeStruct(s, jnp.float32) for s in (shapes if many else [shapes])]
    return pl.pallas_call(
        body,
        out_shape=outs if many else outs[0],
        in_specs=[smem if i < scalars else spec(i in far_in) for i in range(len(args))],
        out_specs=[spec(far_out)] * len(outs) if many else spec(far_out),
        compiler_params=pltpu.CompilerParams(vmem_limit_bytes=VMEM_BYTES),
        **more,
    )(*args)


def swap_rows(edges):
    count = lax.axis_size("space")
    if count == 2:
        both = lax.ppermute(edges, "space", [(0, 1), (1, 0)])
        return both[0], both[1]
    below = lax.ppermute(edges[0], "space", [((i + 1) % count, i) for i in range(count)])
    above = lax.ppermute(edges[1], "space", [(i, (i + 1) % count) for i in range(count)])
    return below, above


def per_device(fine_nodes, init_state, mean_depth):
    nodes = fine_nodes[0]
    rows, cols = nodes.shape[-2:]
    outer, inner, spaces = lax.axis_size("outer"), lax.axis_size("inner"), lax.axis_size("space")
    group = ("inner", "space")
    owners = inner * spaces
    half = cols // 2
    width = half // owners
    slices = outer * inner * 2
    reach = slices - 2
    span = -(-(width + 2 * reach) // LANES) * LANES
    wide = rows + TILE
    at_outer, at_inner, at_core = (lax.axis_index(name) for name in ("outer", "inner", "core"))
    first = at_outer + at_inner + at_core == 0
    place = jnp.stack([first.astype(jnp.int32), (at_outer == 0).astype(jnp.int32), at_core, at_inner])
    state, spread = (3, rows, cols), (3, wide, cols)
    swapped = [(0, 1), (1, 0)]
    plan = (spaces, rows, width, reach)

    prev = lax.ppermute(nodes[2], ("outer", "inner", "core"), [(i, i + 1) for i in range(slices - 1)])

    edges, windows = kernel(
        functools.partial(prepare_body, spaces, width, reach) if dense(width, reach, rows) else edge_body,
        [(2, DEEP, 1, cols), (spaces, 4 * rows, span)],
        place, mean_depth, init_state, scalars=1,
    )
    if not dense(width, reach, rows):
        windows = sparse_windows(mean_depth, init_state, at_core * half, at_inner, spaces, width, reach, span)
    low, high = swap_rows(edges)
    windows = lax.all_to_all(windows, "space", 0, 0, tiled=True)

    base, fk, ffk, depth = kernel(
        blend_body, [state, spread, spread, (wide, cols)], nodes, mean_depth, low, high,
        scratch_shapes=[pltpu.VMEM(spread, jnp.float32)],
    )
    b_raw, v_raw, give, spill = kernel(
        fine_body, [spread, spread, (3 * wide, half + 2 * LANES), (2, 18, 1, cols)],
        place, base, prev, init_state, fk, ffk, depth, scalars=1,
        scratch_shapes=[pltpu.VMEM(spread, jnp.float32)],
    )
    got = lax.ppermute(give, "core", swapped)
    tight = packed_rows(wide, width, reach)
    msg_shape = (owners, tight, LANES) if tight else (owners, 3 * wide, span)
    msgs = kernel(functools.partial(pair_body, width, reach), msg_shape, place, b_raw, got, depth, scalars=1)
    recv = lax.all_to_all(msgs, group, 0, 0, tiled=True)
    low, high = swap_rows(spill)
    b_own, vee = kernel(mend_body, [spread, state], b_raw, v_raw, low, high)
    b_lent = lax.ppermute(b_own, "core", [(0, 1)])

    tight = packed_rows(spaces * rows, width, reach)
    total_shape = (tight, LANES) if tight else (3 * spaces * rows, span)
    total = kernel(functools.partial(total_body, *plan), total_shape, recv, windows)
    carry = lax.ppermute(total, "outer", [(i, i + 1) for i in range(outer - 1)])
    back = kernel(
        functools.partial(chain_body, *plan), (owners, 3 * rows + 2 * TILE, width),
        place, recv, windows, carry, scalars=1,
    )
    mine = lax.all_to_all(back, group, 0, 0, tiled=True)
    if width % LANES:
        mine = mine.transpose(1, 0, 2).reshape(1, 3 * rows + 2 * TILE, half)
    other = lax.ppermute(mine, "core", swapped)
    out = kernel(
        finish_body, (3,) + state, place, mine, other, b_own, b_lent, vee, depth,
        scalars=1, far_out=True,
        scratch_shapes=[
            pltpu.VMEM(spread, jnp.float32),
            pltpu.VMEM((3,) + state, jnp.float32),
            pltpu.SemaphoreType.DMA((9,)),
        ],
    )
    return out[None]


def edge_body(place, depth, init, edge_out, win_out):
    rows = depth.shape[0]
    win_out[...] = jnp.zeros(win_out.shape, jnp.float32)
    for r in range(DEEP):
        edge_out[0, r] = depth[r : r + 1, :]
        edge_out[1, r] = depth[rows - DEEP + r : rows - DEEP + r + 1, :]


def sparse_windows(depth, init, offset, at_inner, spaces, width, reach, span):
    fixed = jnp.concatenate([depth[None], init], axis=0)
    _, rows, cols = fixed.shape
    onward = jnp.concatenate([fixed, fixed[..., :span]], axis=-1)
    behind = jnp.concatenate([fixed[..., cols - span :], fixed], axis=-1)
    lane = lax.broadcasted_iota(jnp.int32, (4, rows, span), 2)
    windows = []
    for y in range(spaces):
        start = offset + (at_inner * spaces + y) * width
        ahead = lax.dynamic_slice_in_dim(onward, start, span, axis=2)
        back = lax.dynamic_slice_in_dim(behind, start, span, axis=2)
        windows.append(jnp.where(lane < span - reach, ahead, back).reshape(4 * rows, span))
    return jnp.stack(windows)


def solution(mesh):
    slices, spaces = mesh.shape["tm"], mesh.shape["space"]
    split = Mesh(mesh.devices.reshape(2, slices // 4, 2, spaces), ("outer", "inner", "core", "space"))
    nodes = P(("outer", "inner", "core"), None, None, "space", None)
    return jax.shard_map(
        per_device,
        mesh=split,
        in_specs=(nodes, P(None, "space", None), P("space", None)),
        out_specs=nodes,
        check_vma=False,
    )
```

time: 88.1 us -> 82.4 us (0.935)
  blocking collectives: 19.2 us -> 0 us
  starting transfers between devices: 22.7 us -> 35.4 us
  Pallas kernels: 10.4 us -> 19.3 us
  waiting for transfers between devices: 23.6 us -> 19.6 us
  other arithmetic: 3.28 us -> 0.08 us
    all_to_all x1 -> x0, blocking collectives: 19.2 us -> none  [per_device(): mine = lax.all_to_all(back, group, 0, 0, tiled=True)]
    pallas_call x7 -> x8, Pallas kernels: 10.4 us -> 19.3 us  [kernel(): pl.pallas_call(body, out_shape=outs if many else outs[0], in_specs=[smem...]
    ppermute x2, waiting for transfers between devices: 7.72 us -> 0.09 us  [swap_rows(): both = lax.ppermute(edges, 'space', [(0, 1), (1, 0)])]
    all_to_all x1 -> x2, waiting for transfers between devices: 0.01 us -> 6.77 us  [the longest x1 4.11 us: per_device(): mine = lax.all_to_all(back, group, 0, 0, tiled=True)]
    ppermute x2 -> x4, starting transfers between devices: 7.04 us -> 11.6 us  [the longest x1 8.72 us: per_device(): got = lax.ppermute(give, 'core', swapped)]
    all_to_all x1, waiting for transfers between devices: 12.9 us -> 8.52 us  [per_device(): recv = lax.all_to_all(msgs, group, 0, 0, tiled=True)]
    all_to_all x1 -> x2, starting transfers between devices: 4.08 us -> 8.24 us  [the longest x1 4.81 us: per_device(): mine = lax.all_to_all(back, group, 0, 0, tiled=True)]
    ppermute x2 -> x4, waiting for transfers between devices: 0.01 us -> 1.91 us  [the longest x1 1.9 us: per_device(): other = lax.ppermute(mine, 'core', swapped)]
  transfers between devices with their start and end apart: 7 -> 10, of which waited for: 3 -> 6; matrix products, arithmetic and copies ran while one was open for 7% -> 3% of each run, Pallas kernels for 6% -> 11%
where the time goes in v3:
time: 82.4 us; the launch traced here: 81.8 us
  starting transfers between devices  35.4 us (43%)
  waiting for transfers between devices  19.6 us (24%)
  Pallas kernels  19.3 us (23%)
  local copies, waits for them, and re-layouts  7.4 us (9%)
    pallas_call x8, Pallas kernels, kernel(): pl.pallas_call(body, out_shape=outs if many else outs[0], in_specs=[smem...  19.3 us
    ppermute x1, starting transfers between devices, per_device(): got = lax.ppermute(give, 'core', swapped)  8.72 us
    all_to_all x1, waiting for transfers between devices, per_device(): recv = lax.all_to_all(msgs, group, 0, 0, tiled=True)  8.52 us
    ppermute x1, starting transfers between devices, per_device(): carry = lax.ppermute(total, 'outer', [(i, i + 1) for i in range(outer - 1)])  5.36 us
    all_to_all x1, starting transfers between devices, per_device(): recv = lax.all_to_all(msgs, group, 0, 0, tiled=True)  5.16 us
    unnamed x16, local copies, waits for them, and re-layouts  5.12 us
    ppermute x2, starting transfers between devices, swap_rows(): both = lax.ppermute(edges, 'space', [(0, 1), (1, 0)])  5.02 us
    all_to_all x1, starting transfers between devices, per_device(): mine = lax.all_to_all(back, group, 0, 0, tiled=True)  4.81 us
  transfers between devices with their start and end apart: 10, of which 6 were waited for; matrix products, arithmetic and copies ran while one was open for 3% of the time, Pallas kernels for 11%

profile of v3, /device:TPU:0, one launch (start us, length us, event | category | flops | bytes accessed | tf_op | source)
XLA Modules:
  0.0 81.8 jit_solution(708483862544859845)
XLA Ops:
  0.0 0.1 pad_add_fusion.place
  0.1 0.0 copy-start.1
  0.1 1.1 %copy-done.1 = f32[3,16,4096]{2,1,0:T(8,128)S(1)} copy-done((f32[3,16,4096]{2,1,0:T(8,128)S(1)}, f32[3,16,4096]{2,1,0:T(8,128)}, u32[]{:S(2)}) %copy-start.1) | copy-done | bytes 786456
  1.2 0.0 copy-start.5
  1.2 0.9 %copy-done.5 = f32[16,4096]{1,0:T(8,128)S(1)} copy-done((f32[16,4096]{1,0:T(8,128)S(1)}, f32[16,4096]{1,0:T(8,128)}, u32[]{:S(2)}) %copy-start.5) | copy-done | bytes 262168
  2.2 0.0 copy-start
  2.2 1.3 %shard_map.37 = (f32[2,3,1,4096]{3,2,1,0:T(1,128)S(1)}, f32[2,64,384]{2,1,0:T(8,128)}) custom-call(s32[4]{0:T(128)S(1)} %pad_add_fusion.place, f32[16,4096]{1,0:T(8,128)S(1)} %copy-done.5, f32[3,16,4096]{2,1,0:T(8,128)S(1)} %copy-done.1), custom_call_target="tpu_custom_call" | custom-call | tf_op jit(solution)/shard_map/pallas_call | solution.py:343
  3.4 3.0 %collective-permute-start = (f32[2,3,1,4096]{3,2,1,0:T(1,128)S(1)}, f32[2,3,1,4096]{3,2,1,0:T(1,128)S(1)}, u32[]{:S(2)}, u32[]{:S(2)}) collective-permute-start(f32[2,3,1,4096]{3,2,1,0:T(1,128)S(1)} %get-tuple-element.17), channel_id=1, source_target_pairs={{0,1},{1,0},{2,3},{3,2},{4,5},{5,4},{6,7},{7,6},{8,9},{9,8},{10,11... | collective-permute-start | bytes 294920 | tf_op jit(solution)/shard_map/ppermute | solution.py:356
  6.4 1.2 %slice_bitcast_fusion = f32[3,16,4096]{2,1,0:T(8,128)S(1)} fusion(f32[1,3,3,16,4096]{4,3,2,1,0:T(8,128)} %param.3), kind=kLoop, calls=%fused_computation | loop fusion | bytes 1572864 | tf_op jit(solution)/shard_map/squeeze | solution.py:382
  7.6 1.5 %collective-permute-start.1 = (f32[3,16,4096]{2,1,0:T(8,128)S(1)}, f32[3,16,4096]{2,1,0:T(8,128)S(1)}, u32[]{:S(2)}, u32[]{:S(2)}) collective-permute-start(f32[3,16,4096]{2,1,0:T(8,128)S(1)} %slice_bitcast_fusion), channel_id=1, source_target_pairs={{0,2},{2,4},{4,6},{6,8},{8,10},{10,12},{12,14},{14,16},{16,18},{18... | collective-permute-start | bytes 2359304 | tf_op jit(solution)/shard_map/ppermute | solution.py:382
  9.1 0.1 collective-permute-done
  9.2 0.0 copy-done
  9.2 0.0 copy-start.2
  9.2 2.0 %shard_map.38 = (f32[3,16,4096]{2,1,0:T(8,128)S(1)}, f32[3,24,4096]{2,1,0:T(8,128)S(1)}, f32[3,24,4096]{2,1,0:T(8,128)S(1)}, f32[24,4096]{1,0:T(8,128)S(1)}) custom-call(f32[3,3,16,4096]{3,2,1,0:T(8,128)S(1)} %bitcast.16, f32[16,4096]{1,0:T(8,128)S(1)} %copy-done.5, f32[3,1,4096]{2,1,0:T(1,128)S(1)} %get-tuple-element.32.low, ...), custom_call_target="tpu_custom_call" | custom-call | tf_op jit(solution)/shard_map/pallas_call | solution.py:343
  11.3 0.0 collective-permute-done.1.prev
  11.3 0.0 copy-done.2
  11.3 4.7 %shard_map.39 = (f32[3,24,4096]{2,1,0:T(8,128)S(1)}, f32[3,24,4096]{2,1,0:T(8,128)S(1)}, f32[72,2304]{1,0:T(8,128)S(1)}, f32[2,18,1,4096]{3,2,1,0:T(1,128)}) custom-call(s32[4]{0:T(128)S(1)} %pad_add_fusion.place, f32[3,16,4096]{2,1,0:T(8,128)S(1)} %get-tuple-element.18.base, f32[3,16,4096]{2,1,0:T(8,128)S(1)} %collective-permute-done.1.prev, ...), custom_call_target="tpu_custom_call" | custom-call | tf_op jit(solution)/shard_map/pallas_call | solution.py:343
  16.0 0.0 copy-start.3
  16.0 1.0 %copy-done.3 = f32[3,24,4096]{2,1,0:T(8,128)} copy-done((f32[3,24,4096]{2,1,0:T(8,128)}, f32[3,24,4096]{2,1,0:T(8,128)S(1)}, u32[]{:S(2)}) %copy-start.3) | copy-done | bytes 1179672
  17.0 8.7 %collective-permute-start.2 = (f32[72,2304]{1,0:T(8,128)S(1)}, f32[72,2304]{1,0:T(8,128)S(1)}, u32[]{:S(2)}, u32[]{:S(2)}) collective-permute-start(f32[72,2304]{1,0:T(8,128)S(1)} %get-tuple-element.23), channel_id=1, source_target_pairs={{0,2},{2,0},{1,3},{3,1},{4,6},{6,4},{5,7},{7,5},{8,10},{10,8},{9,1... | collective-permute-start | bytes 1990664 | tf_op jit(solution)/shard_map/ppermute | solution.py:403
  25.7 3.4 %all-to-all-start.1 = ((f32[2,64,384]{2,1,0:T(8,128)}), f32[2,64,384]{2,1,0:T(8,128)S(1)}, u32[]{:S(2)}, u32[]{:S(2)}) async-start(f32[2,64,384]{2,1,0:T(8,128)} %get-tuple-element.24), calls=%async_computation.1 | async-start | bytes 393216 | tf_op jit(solution)/shard_map/all_to_all | solution.py:392
  29.2 0.0 collective-permute-done.2.got
  29.2 2.2 %shard_map.40 = f32[8,168,128]{2,1,0:T(8,128)} custom-call(s32[4]{0:T(128)S(1)} %pad_add_fusion.place, f32[3,24,4096]{2,1,0:T(8,128)S(1)} %get-tuple-element.22.b_own.b_raw, f32[72,2304]{1,0:T(8,128)S(1)} %collective-permute-done.2.got, f32[24,4096]{1,0:T(8,128)S(1)} %get-tuple-element.21.depth_ref), custom_call_target="tpu_custom_call" | custom-call | tf_op jit(solution)/shard_map/pallas_call | solution.py:343
  31.4 2.7 %all-to-all-done.1.win = f32[2,64,384]{2,1,0:T(8,128)S(1)} async-done(((f32[2,64,384]{2,1,0:T(8,128)}), f32[2,64,384]{2,1,0:T(8,128)S(1)}, u32[]{:S(2)}, u32[]{:S(2)}) %all-to-all-start.1) | async-done | bytes 196640 | tf_op jit(solution)/shard_map/all_to_all | solution.py:392
  34.1 5.2 %all-to-all-start = ((f32[8,168,128]{2,1,0:T(8,128)}), f32[8,168,128]{2,1,0:T(8,128)S(1)}, u32[]{:S(2)}, u32[]{:S(2)}) async-start(f32[8,168,128]{2,1,0:T(8,128)} %shard_map.40), calls=%async_computation | async-start | bytes 1376256 | tf_op jit(solution)/shard_map/all_to_all | solution.py:407
  39.2 2.0 %collective-permute-start.5 = (f32[2,18,1,4096]{3,2,1,0:T(1,128)}, f32[2,18,1,4096]{3,2,1,0:T(1,128)}, u32[]{:S(2)}, u32[]{:S(2)}) collective-permute-start(f32[2,18,1,4096]{3,2,1,0:T(1,128)} %get-tuple-element.26), channel_id=1, source_target_pairs={{0,1},{1,0},{2,3},{3,2},{4,5},{5,4},{6,7},{7,6},{8,9},{9,8},{10,11... | collective-permute-start | bytes 1769480 | tf_op jit(solution)/shard_map/ppermute | solution.py:356
  41.3 8.5 %all-to-all-done.recv = f32[8,168,128]{2,1,0:T(8,128)S(1)} async-done(((f32[8,168,128]{2,1,0:T(8,128)}), f32[8,168,128]{2,1,0:T(8,128)S(1)}, u32[]{:S(2)}, u32[]{:S(2)}) %all-to-all-start) | async-done | bytes 688160 | tf_op jit(solution)/shard_map/all_to_all | solution.py:407
  49.8 1.2 %shard_map.41 = f32[216,128]{1,0:T(8,128)S(1)} custom-call(f32[8,168,128]{2,1,0:T(8,128)S(1)} %all-to-all-done.recv, f32[2,64,384]{2,1,0:T(8,128)S(1)} %all-to-all-done.1.win), custom_call_target="tpu_custom_call" | custom-call | tf_op jit(solution)/shard_map/pallas_call | solution.py:343
  51.0 5.4 %collective-permute-start.3 = (f32[216,128]{1,0:T(8,128)S(1)}, f32[216,128]{1,0:T(8,128)S(1)}, u32[]{:S(2)}, u32[]{:S(2)}) collective-permute-start(f32[216,128]{1,0:T(8,128)S(1)} %shard_map.41), channel_id=1, source_target_pairs={{0,16},{1,17},{2,18},{3,19},{4,20},{5,21},{6,22},{7,23},{8,24},{9,... | collective-permute-start | bytes 331784 | tf_op jit(solution)/shard_map/ppermute | solution.py:415
  56.3 2.3 %collective-permute-done.3.carry = f32[216,128]{1,0:T(8,128)S(1)} collective-permute-done((f32[216,128]{1,0:T(8,128)S(1)}, f32[216,128]{1,0:T(8,128)S(1)}, u32[]{:S(2)}, u32[]{:S(2)}) %collective-permute-start.3) | collective-permute-done | bytes 110624 | tf_op jit(solution)/shard_map/ppermute | solution.py:415
  58.6 2.2 %shard_map.42 = f32[8,64,256]{2,1,0:T(8,128)} custom-call(s32[4]{0:T(128)S(1)} %pad_add_fusion.place, f32[8,168,128]{2,1,0:T(8,128)S(1)} %all-to-all-done.recv, f32[2,64,384]{2,1,0:T(8,128)S(1)} %all-to-all-done.1.win, f32[216,128]{1,0:T(8,128)S(1)} %collective-permute-done.3.carry), custom_call_target="tpu_custom_call" | custom-call | tf_op jit(solution)/shard_map/pallas_call | solution.py:343
  60.9 0.0 copy-start.4
  60.9 4.8 %all-to-all-start.2 = ((f32[8,64,256]{2,1,0:T(8,128)}), f32[8,64,256]{2,1,0:T(8,128)S(1)}, u32[]{:S(2)}, u32[]{:S(2)}) async-start(f32[8,64,256]{2,1,0:T(8,128)} %shard_map.42), calls=%async_computation.2 | async-start | bytes 1048576 | tf_op jit(solution)/shard_map/all_to_all | solution.py:420
  65.7 0.0 collective-permute-done.5
  65.7 1.1 %slice_bitcast_fusion.1 = (f32[18,1,4096]{2,1,0:T(1,128)S(1)}, f32[18,1,4096]{2,1,0:T(1,128)S(1)}) fusion(f32[2,18,1,4096]{3,2,1,0:T(1,128)} %collective-permute-done.5), kind=kLoop, calls=%fused_computation.1 | loop fusion | bytes 1179648 | tf_op jit(solution)/shard_map/squeeze | solution.py:357
  66.8 0.0 copy-done.4
  66.8 1.3 %shard_map.43 = (f32[3,24,4096]{2,1,0:T(8,128)}, f32[3,16,4096]{2,1,0:T(8,128)S(1)}) custom-call(f32[3,24,4096]{2,1,0:T(8,128)S(1)} %get-tuple-element.22.b_own.b_raw, f32[3,24,4096]{2,1,0:T(8,128)S(1)} %copy-done.4, f32[18,1,4096]{2,1,0:T(1,128)S(1)} %get-tuple-element.30.low, f32[18,1,4096]{2,1,0:T(1,128)S(1)} %get-tuple-element.29.high), custom_call_target="tpu_custom_call" | custom-call | tf_op jit(solution)/shard_map/pallas_call | solution.py:343
  68.1 0.0 copy-start.6
  68.1 0.9 %copy-done.6 = f32[3,16,4096]{2,1,0:T(8,128)} copy-done((f32[3,16,4096]{2,1,0:T(8,128)}, f32[3,16,4096]{2,1,0:T(8,128)S(1)}, u32[]{:S(2)}) %copy-start.6) | copy-done | bytes 786456
  69.0 1.4 %collective-permute-start.6 = (f32[3,24,4096]{2,1,0:T(8,128)}, f32[3,24,4096]{2,1,0:T(8,128)S(1)}, u32[]{:S(2)}, u32[]{:S(2)}) collective-permute-start(f32[3,24,4096]{2,1,0:T(8,128)} %get-tuple-element.27.b_own), channel_id=1, source_target_pairs={{0,2},{1,3},{4,6},{5,7},{8,10},{9,11},{12,14},{13,15},{16,18},{17,... | collective-permute-start | bytes 3538952 | tf_op jit(solution)/shard_map/ppermute | solution.py:410
  70.4 4.1 %all-to-all-done.2.mine = f32[8,64,256]{2,1,0:T(8,128)S(1)} async-done(((f32[8,64,256]{2,1,0:T(8,128)}), f32[8,64,256]{2,1,0:T(8,128)S(1)}, u32[]{:S(2)}, u32[]{:S(2)}) %all-to-all-start.2) | async-done | bytes 524320 | tf_op jit(solution)/shard_map/all_to_all | solution.py:420
  74.5 0.0 collective-permute-start.4
  74.5 0.0 collective-permute-done.6.b_lent
  74.5 1.9 %collective-permute-done.4.other = f32[8,64,256]{2,1,0:T(8,128)S(1)} collective-permute-done((f32[8,64,256]{2,1,0:T(8,128)S(1)}, f32[8,64,256]{2,1,0:T(8,128)S(1)}, u32[]{:S(2)}, u32[]{:S(2)}) %collective-permute-start.4) | collective-permute-done | bytes 524320 | tf_op jit(solution)/shard_map/ppermute | solution.py:423
  76.4 0.0 copy-start.7
  76.4 1.1 %copy-done.7 = f32[3,16,4096]{2,1,0:T(8,128)S(1)} copy-done((f32[3,16,4096]{2,1,0:T(8,128)S(1)}, f32[3,16,4096]{2,1,0:T(8,128)}, u32[]{:S(2)}) %copy-start.7) | copy-done | bytes 786456
  77.5 4.3 %shard_map.44 = f32[3,3,16,4096]{3,2,1,0:T(8,128)} custom-call(s32[4]{0:T(128)S(1)} %pad_add_fusion.place, f32[8,64,256]{2,1,0:T(8,128)S(1)} %all-to-all-done.2.mine, f32[8,64,256]{2,1,0:T(8,128)S(1)} %collective-permute-done.4.other, f32[3,24,4096]{2,1,0:T(8,128)} %get-tuple-element.27.b_own, f32[3,24,4096]{2,1,0:T(8,128)S(1)} %collective-permute-done.6.b_lent, ...), custom_call_target="tpu_custom_call" | custom-call | tf_op jit(solution)/shard_map/pallas_call | solution.py:343
  (1 shorter events, 0.0 us)
Async XLA Ops:
  0.1 1.1 %copy-start.1 = (f32[3,16,4096]{2,1,0:T(8,128)S(1)}, f32[3,16,4096]{2,1,0:T(8,128)}, u32[]{:S(2)}) copy-start(f32[3,16,4096]{2,1,0:T(8,128)} %init.3) | copy-start | bytes 2359300
  1.2 0.9 %copy-start.5 = (f32[16,4096]{1,0:T(8,128)S(1)}, f32[16,4096]{1,0:T(8,128)}, u32[]{:S(2)}) copy-start(f32[16,4096]{1,0:T(8,128)} %depth.3) | copy-start | bytes 786436
  2.2 7.1 %copy-start = (f32[1,3,3,16,4096]{4,3,2,1,0:T(8,128)S(1)}, f32[1,3,3,16,4096]{4,3,2,1,0:T(8,128)}, u32[]{:S(2)}) copy-start(f32[1,3,3,16,4096]{4,3,2,1,0:T(8,128)} %param.3) | copy-start | bytes 7077892
  3.4 5.8 %collective-permute-start = (f32[2,3,1,4096]{3,2,1,0:T(1,128)S(1)}, f32[2,3,1,4096]{3,2,1,0:T(1,128)S(1)}, u32[]{:S(2)}, u32[]{:S(2)}) collective-permute-start(f32[2,3,1,4096]{3,2,1,0:T(1,128)S(1)} %get-tuple-element.17), channel_id=1, source_target_pairs={{0,1},{1,0},{2,3},{3,2},{4,5},{5,4},{6,7},{7,6},{8,9},{9,8},{10,11... | collective-permute-start | bytes 294920 | tf_op jit(solution)/shard_map/ppermute | solution.py:356
  7.6 3.7 %collective-permute-start.1 = (f32[3,16,4096]{2,1,0:T(8,128)S(1)}, f32[3,16,4096]{2,1,0:T(8,128)S(1)}, u32[]{:S(2)}, u32[]{:S(2)}) collective-permute-start(f32[3,16,4096]{2,1,0:T(8,128)S(1)} %slice_bitcast_fusion), channel_id=1, source_target_pairs={{0,2},{2,4},{4,6},{6,8},{8,10},{10,12},{12,14},{14,16},{16,18},{18... | collective-permute-start | bytes 2359304 | tf_op jit(solution)/shard_map/ppermute | solution.py:382
  9.2 2.1 %copy-start.2 = (f32[3,16,4096]{2,1,0:T(8,128)S(1)}, f32[3,16,4096]{2,1,0:T(8,128)}, u32[]{:S(2)}) copy-start(f32[3,16,4096]{2,1,0:T(8,128)} %init.3) | copy-start | bytes 2359300
  16.0 1.0 %copy-start.3 = (f32[3,24,4096]{2,1,0:T(8,128)}, f32[3,24,4096]{2,1,0:T(8,128)S(1)}, u32[]{:S(2)}) copy-start(f32[3,24,4096]{2,1,0:T(8,128)S(1)} %get-tuple-element.25.v_raw) | copy-start | bytes 3538948
  17.0 12.2 %collective-permute-start.2 = (f32[72,2304]{1,0:T(8,128)S(1)}, f32[72,2304]{1,0:T(8,128)S(1)}, u32[]{:S(2)}, u32[]{:S(2)}) collective-permute-start(f32[72,2304]{1,0:T(8,128)S(1)} %get-tuple-element.23), channel_id=1, source_target_pairs={{0,2},{2,0},{1,3},{3,1},{4,6},{6,4},{5,7},{7,5},{8,10},{10,8},{9,1... | collective-permute-start | bytes 1990664 | tf_op jit(solution)/shard_map/ppermute | solution.py:403
  25.7 8.3 %all-to-all-start.1 = ((f32[2,64,384]{2,1,0:T(8,128)}), f32[2,64,384]{2,1,0:T(8,128)S(1)}, u32[]{:S(2)}, u32[]{:S(2)}) async-start(f32[2,64,384]{2,1,0:T(8,128)} %get-tuple-element.24), calls=%async_computation.1 | async-start | bytes 393216 | tf_op jit(solution)/shard_map/all_to_all | solution.py:392
  34.1 15.7 %all-to-all-start = ((f32[8,168,128]{2,1,0:T(8,128)}), f32[8,168,128]{2,1,0:T(8,128)S(1)}, u32[]{:S(2)}, u32[]{:S(2)}) async-start(f32[8,168,128]{2,1,0:T(8,128)} %shard_map.40), calls=%async_computation | async-start | bytes 1376256 | tf_op jit(solution)/shard_map/all_to_all | solution.py:407
  39.2 26.4 %collective-permute-start.5 = (f32[2,18,1,4096]{3,2,1,0:T(1,128)}, f32[2,18,1,4096]{3,2,1,0:T(1,128)}, u32[]{:S(2)}, u32[]{:S(2)}) collective-permute-start(f32[2,18,1,4096]{3,2,1,0:T(1,128)} %get-tuple-element.26), channel_id=1, source_target_pairs={{0,1},{1,0},{2,3},{3,2},{4,5},{5,4},{6,7},{7,6},{8,9},{9,8},{10,11... | collective-permute-start | bytes 1769480 | tf_op jit(solution)/shard_map/ppermute | solution.py:356
  51.0 7.7 %collective-permute-start.3 = (f32[216,128]{1,0:T(8,128)S(1)}, f32[216,128]{1,0:T(8,128)S(1)}, u32[]{:S(2)}, u32[]{:S(2)}) collective-permute-start(f32[216,128]{1,0:T(8,128)S(1)} %shard_map.41), channel_id=1, source_target_pairs={{0,16},{1,17},{2,18},{3,19},{4,20},{5,21},{6,22},{7,23},{8,24},{9,... | collective-permute-start | bytes 331784 | tf_op jit(solution)/shard_map/ppermute | solution.py:415
  60.9 5.9 %copy-start.4 = (f32[3,24,4096]{2,1,0:T(8,128)S(1)}, f32[3,24,4096]{2,1,0:T(8,128)}, u32[]{:S(2)}) copy-start(f32[3,24,4096]{2,1,0:T(8,128)} %copy-done.3) | copy-start | bytes 3538948
  60.9 13.6 %all-to-all-start.2 = ((f32[8,64,256]{2,1,0:T(8,128)}), f32[8,64,256]{2,1,0:T(8,128)S(1)}, u32[]{:S(2)}, u32[]{:S(2)}) async-start(f32[8,64,256]{2,1,0:T(8,128)} %shard_map.42), calls=%async_computation.2 | async-start | bytes 1048576 | tf_op jit(solution)/shard_map/all_to_all | solution.py:420
  68.1 0.9 %copy-start.6 = (f32[3,16,4096]{2,1,0:T(8,128)}, f32[3,16,4096]{2,1,0:T(8,128)S(1)}, u32[]{:S(2)}) copy-start(f32[3,16,4096]{2,1,0:T(8,128)S(1)} %get-tuple-element.28.v_ref) | copy-start | bytes 2359300
  69.0 5.5 %collective-permute-start.6 = (f32[3,24,4096]{2,1,0:T(8,128)}, f32[3,24,4096]{2,1,0:T(8,128)S(1)}, u32[]{:S(2)}, u32[]{:S(2)}) collective-permute-start(f32[3,24,4096]{2,1,0:T(8,128)} %get-tuple-element.27.b_own), channel_id=1, source_target_pairs={{0,2},{1,3},{4,6},{5,7},{8,10},{9,11},{12,14},{13,15},{16,18},{17,... | collective-permute-start | bytes 3538952 | tf_op jit(solution)/shard_map/ppermute | solution.py:410
  74.5 1.9 %collective-permute-start.4 = (f32[8,64,256]{2,1,0:T(8,128)S(1)}, f32[8,64,256]{2,1,0:T(8,128)S(1)}, u32[]{:S(2)}, u32[]{:S(2)}) collective-permute-start(f32[8,64,256]{2,1,0:T(8,128)S(1)} %all-to-all-done.2.mine), channel_id=1, source_target_pairs={{0,2},{2,0},{1,3},{3,1},{4,6},{6,4},{5,7},{7,5},{8,10},{10,8},{9,1... | collective-permute-start | bytes 1572872 | tf_op jit(solution)/shard_map/ppermute | solution.py:423
  76.4 1.1 %copy-start.7 = (f32[3,16,4096]{2,1,0:T(8,128)S(1)}, f32[3,16,4096]{2,1,0:T(8,128)}, u32[]{:S(2)}) copy-start(f32[3,16,4096]{2,1,0:T(8,128)} %copy-done.6) | copy-start | bytes 2359300

commit v4 on v3

v4 whole, which is shorter than its diff:
```python
import functools

import jax
import jax.numpy as jnp
from jax import lax
from jax.experimental import pallas as pl
from jax.experimental.pallas import tpu as pltpu
from jax.sharding import Mesh
from jax.sharding import PartitionSpec as P


DT = 0.3
HALF = 0.5 * DT
NU = 1.0 / 3.0
FC = 0.5
DEEP = 3
TILE = 8
LANES = 128
VMEM_BYTES = 20 * 1024 * 1024


def rolled(x, by, axis):
    return pltpu.roll(x, by % x.shape[axis], axis)


def advanced(q, flow, scale, keep):
    height, east, north = q
    soft, slope, turn = scale * NU, scale * 0.5, scale * FC
    stay = keep - 4.0 * soft
    h_soft, e_soft, n_soft = soft * height, soft * east, soft * north
    h_slope = slope * height
    flow_e, flow_n = flow * east, flow * north
    new_h = (
        (rolled(h_soft + flow_e, 1, 1) + rolled(h_soft - flow_e, -1, 1))
        + (rolled(h_soft + flow_n, 1, 0) + rolled(h_soft - flow_n, -1, 0))
        + stay * height
    )
    new_e = (
        (rolled(e_soft + h_slope, 1, 1) + rolled(e_soft - h_slope, -1, 1))
        + (rolled(e_soft, 1, 0) + rolled(e_soft, -1, 0))
        + (stay * east + turn * north)
    )
    new_n = (
        (rolled(n_soft, 1, 1) + rolled(n_soft, -1, 1))
        + (rolled(n_soft + h_slope, 1, 0) + rolled(n_soft - h_slope, -1, 0))
        + (stay * north - turn * east)
    )
    return new_h, new_e, new_n


def tendency(q, half_depth):
    return advanced(q, half_depth, 1.0, 0.0)


def stepped(q, step_depth):
    return advanced(q, step_depth, DT, 1.0)


def dense(width, reach, rows):
    return width % LANES == 0 and 2 * reach <= 32 and rows % TILE == 0


def packed_rows(rows, width, reach):
    if not dense(width, reach, rows):
        return None
    tiles = 3 * rows // TILE
    return 3 * rows * (width // LANES) + TILE * -(-tiles // 4)


def cut(ref, lead, at, size=LANES):
    return ref[lead + (slice(None), pl.ds(pl.multiple_of(at, LANES), size))]


def prepare_body(width, reach, place, depth, init, own_out, edge_out):
    rows, cols = depth.shape
    lane = lax.broadcasted_iota(jnp.int32, (rows, LANES), 1)
    for out, y in ((own_out, place[4]), (edge_out, 1 - place[4])):
        start = place[2] * (cols // 2) + (place[3] * 2 + y) * width
        after = lax.rem(start + width, cols)
        before = lax.rem(start - LANES + cols, cols)
        for i in range(4):
            ref, lead = (depth, ()) if i == 0 else (init, (i - 1,))
            parts = [cut(ref, lead, start + t * LANES) for t in range(width // LANES)]
            parts.append(jnp.where(lane < LANES - reach, cut(ref, lead, after), cut(ref, lead, before)))
            for t, part in enumerate(parts):
                at = (4 * t + i) * rows
                out[at : at + rows, :] = part
    at = own_out.shape[0]
    for r in (*range(DEEP), *range(rows - DEEP, rows)):
        for t in range(cols // LANES):
            edge_out[at : at + 1, :] = depth[r : r + 1, t * LANES : (t + 1) * LANES]
            at += 1


def blend_body(nodes, depth, base_out, fk_out, state, near, sems):
    rows, cols = depth.shape
    copies = [pltpu.make_async_copy(nodes.at[:, f], near.at[f], sems.at[f]) for f in range(3)]
    for copy in copies:
        copy.start()
    none = jnp.zeros((TILE, cols), jnp.float32)
    for f in range(3):
        copies[f].wait()
        n0, n1, n2 = near[f, 0], near[f, 1], near[f, 2]
        base_out[f] = (DT / 24.0) * (8.0 * n1 - 7.0 * n0 - n2)
        state[f, :rows, :] = (DT / 4.0) * (n0 - 2.0 * n1 + n2)
        state[f, rows:, :] = none
    half_depth = jnp.concatenate([0.5 * depth[...], none], axis=0)
    fk = tendency(tuple(state[f] for f in range(3)), half_depth)
    for f in range(3):
        fk_out[f] = fk[f]


def second_body(fk, depth, *rest):
    *edges, ffk_out, depth_out = rest
    rows, cols = depth.shape
    depth_out[:rows, :] = 0.5 * depth[...]
    depth_out[rows:, :] = jnp.zeros((TILE, cols), jnp.float32)
    for r in range(DEEP):
        below, above = rows + r, rows + TILE - DEEP + r
        if len(edges) == 2:
            depth_out[below : below + 1, :] = 0.5 * edges[0][r]
            depth_out[above : above + 1, :] = 0.5 * edges[1][r]
            continue
        tiles = cols // LANES
        base = edges[0].shape[0] - 2 * DEEP * tiles
        for t in range(tiles):
            for to, at in ((below, base + r * tiles + t), (above, base + (DEEP + r) * tiles + t)):
                depth_out[to : to + 1, t * LANES : (t + 1) * LANES] = 0.5 * edges[0][at : at + 1, :]
    ffk = tendency(tuple(fk[f] for f in range(3)), depth_out[...])
    for f in range(3):
        ffk_out[f] = ffk[f]


def window(ref, lead, half):
    cols = ref.shape[-1]
    start = half * (cols // 2) + (cols - LANES)
    parts = [cut(ref, lead, lax.rem(start + t * LANES, cols)) for t in range(cols // 2 // LANES + 2)]
    return jnp.concatenate(parts, axis=1)


def fine_body(own_half, place, base, prev, init, fk, ffk, depth_ref, b_out, v_out):
    half = place[2] if own_half else 1 - place[2]
    first = place[0] == 1
    wide = fk.shape[1]
    half_depth = window(depth_ref, (), half)
    none = jnp.zeros((TILE, half_depth.shape[1]), jnp.float32)
    g = []
    for f in range(3):
        start = jnp.where(first, window(init, (f,), half), window(prev, (f,), half))
        g.append(jnp.concatenate([HALF * start + window(base, (f,), half), none], axis=0))
    u = tendency(tendency(tuple(g), half_depth), half_depth)
    fu = tendency(u, half_depth)
    for f in range(3):
        at = slice(f * wide, (f + 1) * wide)
        v = window(fk, (f,), half) + HALF * u[f]
        v_out[at, :] = v[:, LANES : v.shape[1] - LANES]
        b_out[at, :] = DT * (u[f] + (1.0 / 6.0) * (HALF * fu[f] + window(ffk, (f,), half)))


def spill_body(b_keep, b_give, v_keep, v_give, spill_out):
    wide = b_keep.shape[0] // 3
    rows = wide - TILE
    for h, (b, v) in enumerate(((b_keep, v_keep), (b_give, v_give))):
        inside = slice(LANES, b.shape[1] - LANES)
        for f in range(3):
            top = f * wide
            for side, spread, edge in ((0, wide - DEEP, 0), (1, rows, rows - 1)):
                for r in range(DEEP):
                    spill_out[side, h, DEEP * f + r] = b[top + spread + r : top + spread + r + 1, inside]
                spill_out[side, h, 9 + f] = b[top + edge : top + edge + 1, inside]
                spread = wide - 2 if side == 0 else rows
                for r in range(2):
                    spill_out[side, h, 12 + 2 * f + r] = v[top + spread + r : top + spread + r + 1, :]


def mend_body(place, b_keep, b_give, v_keep, v_give, low, high, b_out, v_far, v_out, sem):
    rows = v_out.shape[1]
    wide = rows + TILE
    size = v_keep.shape[1]
    halves = ((place[2], b_keep, v_keep), (1 - place[2], b_give, v_give))
    for h, (half, _, v) in enumerate(halves):
        to = pl.ds(pl.multiple_of(half * size, LANES), size)
        for f in range(3):
            v_out[f, :, to] = v[f * wide : f * wide + rows, :]
            for r in range(2):
                for at, more in ((r, high), (rows - 2 + r, low)):
                    old = v[f * wide + at : f * wide + at + 1, :]
                    v_out[f, at : at + 1, to] = old + more[h, 12 + 2 * f + r]
    copy = pltpu.make_async_copy(v_out, v_far, sem)
    copy.start()
    for h, (half, b, _) in enumerate(halves):
        to = pl.ds(pl.multiple_of(half * size, LANES), size)
        inside = slice(LANES, LANES + size)
        for f in range(3):
            top = f * wide
            b_out[f, :, to] = b[top : top + wide, inside]
            adds = [(rows, 9 + f, low), (wide - 1, 9 + f, high)]
            for r in range(DEEP):
                adds += [(r, DEEP * f + r, high), (rows - DEEP + r, DEEP * f + r, low)]
            for at, i, more in adds:
                b_out[f, at : at + 1, to] = b[top + at : top + at + 1, inside] + more[h, i]
    copy.wait()


def pair_body(width, reach, count, place, depth_ref, got, *rest):
    near, far = rest[:count], rest[count + 1 : 2 * count + 1]
    msg_far, msg_out, sems = rest[count], rest[-2], rest[-1]
    owners = msg_out.shape[0]
    copies = [pltpu.make_async_copy(a, b, sems.at[owners + i]) for i, (a, b) in enumerate(zip(near, far))]
    for copy in copies:
        copy.start()
    keep = near[0]
    wide = keep.shape[0] // 3
    even = place[2] == 0
    step_depth = DT * window(depth_ref, (), place[2])
    own = tuple(keep[f * wide : (f + 1) * wide, :] for f in range(3))
    other = tuple(got[f * wide : (f + 1) * wide, :] for f in range(3))
    first = tuple(jnp.where(even, x, y) for x, y in zip(own, other))
    second = tuple(jnp.where(even, y, x) for x, y in zip(own, other))
    both = tuple(x + y for x, y in zip(second, stepped(first, step_depth)))
    for j in range(owners):
        for f in range(3):
            pack_block(both[f], f, j, width, reach, msg_out.at[j])
    copies.append(pltpu.make_async_copy(msg_out, msg_far, sems.at[0]))
    copies[-1].start()
    for copy in copies:
        copy.wait()


def pack_block(b, f, j, width, reach, out):
    rows, cols = b.shape
    at = LANES + j * width
    lane = lax.broadcasted_iota(jnp.int32, (rows, LANES), 1)
    if dense(width, reach, rows):
        small = lax.broadcasted_iota(jnp.int32, (TILE, LANES), 1)
        parts = width // LANES
        for t in range(parts):
            out[(f * parts + t) * rows : (f * parts + t + 1) * rows, :] = b[:, at + t * LANES : at + (t + 1) * LANES]
        after, before = at + width, at - LANES
        halo = jnp.where(lane < LANES // 2, b[:, after : after + LANES], b[:, before : before + LANES])
        put_halo(halo, f * rows // TILE, 3 * parts * rows, small, out)
        return
    span = out.shape[1]
    turned = rolled(b, -at, 1)
    parts = [turned[:, t : t + LANES] for t in range(0, span, LANES)]
    parts[-1] = jnp.where(lane < LANES - reach, parts[-1], turned[:, cols - LANES :])
    for t, part in enumerate(parts):
        out[f * rows : (f + 1) * rows, t * LANES : (t + 1) * LANES] = part


def put_halo(halo, tile, base, small, out):
    for i in range(halo.shape[0] // TILE):
        q = (tile + i) % 4
        at = base + (tile + i) // 4 * TILE
        moved = rolled(halo[i * TILE : (i + 1) * TILE], 16 + 32 * q, 1)
        if q:
            moved = jnp.where(small >= 32 * q, moved, out[at : at + TILE, :])
        out[at : at + TILE, :] = moved


def get_halo(source, tile, count, base):
    found = []
    for i in range(tile, tile + count):
        at = base + i // 4 * TILE
        found.append(rolled(source[at : at + TILE, :], -(16 + 32 * (i % 4)), 1))
    return jnp.concatenate(found, axis=0)


def block_of(message, f, rows, width, reach):
    if not dense(width, reach, rows):
        return message[f * rows : (f + 1) * rows, :]
    parts = width // LANES
    main = [message[(f * parts + t) * rows : (f * parts + t + 1) * rows, :] for t in range(parts)]
    return jnp.concatenate(main + [get_halo(message, f * rows // TILE, rows // TILE, 3 * parts * rows)], axis=1)


def joined(recv, slot, spaces, rows, width, reach):
    wide = rows + TILE
    fields = []
    for f in range(3):
        blocks = [block_of(recv.at[slot * spaces + y], f, wide, width, reach) for y in range(spaces)]
        row = lax.broadcasted_iota(jnp.int32, (TILE, blocks[0].shape[1]), 0)
        tiles = []
        for y in range(spaces):
            here = [blocks[y][t : t + TILE] for t in range(0, rows, TILE)]
            here[0] = here[0] + jnp.where(row < TILE // 2, blocks[(y - 1) % spaces][rows:], 0.0)
            here[-1] = here[-1] + jnp.where(row < TILE // 2, 0.0, blocks[(y + 1) % spaces][rows:])
            tiles += here
        fields.append(jnp.concatenate(tiles, axis=0))
    return tuple(fields)


def window_field(win, i, rows, place):
    if len(win) == 1:
        return jnp.concatenate([win[0][y, i * rows : (i + 1) * rows, :] for y in range(win[0].shape[0])], axis=0)
    own, theirs = (
        jnp.concatenate([part[at : at + rows, :] for at in range(i * rows, part.shape[0], 4 * rows)], axis=1)
        for part in (win[0], win[1].at[: win[0].shape[0]])
    )
    above = place[4] == 0
    return jnp.concatenate([jnp.where(above, own, theirs), jnp.where(above, theirs, own)], axis=0)


def two_steps(q, step_depth):
    return stepped(stepped(q, step_depth), step_depth)


def total_body(spaces, rows, width, reach, place, recv, *rest):
    *win, total_out = rest
    slots = recv.shape[0] // spaces
    step_depth = HALF * window_field(win, 0, rows, place)
    q = tuple(window_field(win, 1 + f, rows, place) for f in range(3))
    for slot in range(slots):
        b = joined(recv, slot, spaces, rows, width, reach)
        q = tuple(x + y for x, y in zip(b, two_steps(q, step_depth)))
    all_rows = rows * spaces
    if not dense(width, reach, rows):
        for f in range(3):
            total_out[f * all_rows : (f + 1) * all_rows, :] = q[f]
        return
    small = lax.broadcasted_iota(jnp.int32, (TILE, LANES), 1)
    parts = width // LANES
    for f in range(3):
        for t in range(parts):
            total_out[(f * parts + t) * all_rows : (f * parts + t + 1) * all_rows, :] = q[f][
                :, t * LANES : (t + 1) * LANES
            ]
        put_halo(q[f][:, width:], f * all_rows // TILE, 3 * parts * all_rows, small, total_out)


def chain_body(spaces, rows, width, reach, place, recv, carry, *rest):
    *win, msg_far, msg_out, sems = rest
    slots = recv.shape[0] // spaces
    all_rows = rows * spaces
    copies = []
    step_depth = HALF * window_field(win, 0, rows, place)
    lower = place[1] == 1
    q = tuple(
        jnp.where(lower, window_field(win, 1 + f, rows, place), block_of(carry, f, all_rows, width, reach))
        for f in range(3)
    )
    for slot in range(slots):
        for y in range(spaces):
            at = slot * spaces + y
            for f in range(3):
                here = q[f][:, :width]
                lo, hi = y * rows, (y + 1) * rows
                msg_out[at, f * rows : (f + 1) * rows, :] = here[lo:hi]
                for r, source in enumerate((hi, hi + 1, lo - 2, lo - 1)):
                    source %= all_rows
                    to = 3 * rows + 4 * f + r
                    msg_out[at, to : to + 1, :] = here[source : source + 1]
            msg_out[at, 3 * rows + 12 :, :] = jnp.zeros((4, width), jnp.float32)
            copies.append(pltpu.make_async_copy(msg_out.at[at], msg_far.at[at], sems.at[at]))
            copies[-1].start()
        if slot + 1 < slots:
            b = joined(recv, slot, spaces, rows, width, reach)
            q = tuple(x + y for x, y in zip(b, two_steps(q, step_depth)))
    for copy in copies:
        copy.wait()


def finish_body(place, mine, other, b_far, b_lent, v_far, depth_ref, out, state, made, v_ref, b_own, sems):
    rows, cols = v_ref.shape[1:]
    fetches = [pltpu.make_async_copy(b_far, b_own, sems.at[9]), pltpu.make_async_copy(v_far, v_ref, sems.at[10])]
    for fetch in fetches:
        fetch.start()
    wide = rows + TILE
    pieces, _, width = mine.shape
    even = place[2] == 0
    for f in range(3):
        state[f, rows:, :] = jnp.zeros((TILE, cols), jnp.float32)
        for source, half in ((mine, place[2]), (other, 1 - place[2])):
            for j in range(pieces):
                to = pl.ds(pl.multiple_of(half * (cols // 2) + j * width, LANES), width)
                state[f, :rows, to] = source[j, f * rows : (f + 1) * rows, :]
                for r, row in enumerate((rows, rows + 1, wide - 2, wide - 1)):
                    at = 3 * rows + 4 * f + r
                    state[f, row : row + 1, to] = source[j, at : at + 1, :]
    step_depth = DT * depth_ref[...]
    carried = tuple(state[f] for f in range(3))
    for fetch in fetches:
        fetch.wait()
    after = tuple(
        jnp.where(even, b_own[f], b_lent[f]) + x for f, x in enumerate(stepped(carried, step_depth))
    )
    last = stepped(after, step_depth)
    copies = []
    for f in range(3):
        begin = jnp.where(even, carried[f][:rows], after[f][:rows])
        end = jnp.where(even, after[f][:rows], b_own[f, :rows, :] + last[f][:rows])
        made[0, f] = begin
        made[1, f] = 0.5 * ((begin + end) - v_ref[f])
        made[2, f] = end
        for part in range(3):
            copy = pltpu.make_async_copy(made.at[part, f], out.at[part, f], sems.at[3 * f + part])
            copy.start()
            copies.append(copy)
    for copy in copies:
        copy.wait()


def kernel(body, shapes, *args, scalars=0, far=(), far_out=(), **more):
    vmem = pl.BlockSpec(memory_space=pltpu.VMEM)
    hbm = pl.BlockSpec(memory_space=pltpu.HBM)
    smem = pl.BlockSpec(memory_space=pltpu.SMEM)
    many = isinstance(shapes, list)
    outs = [
        pltpu.HBM(shape, jnp.float32) if i in far_out else jax.ShapeDtypeStruct(shape, jnp.float32)
        for i, shape in enumerate(shapes if many else [shapes])
    ]
    specs = [hbm if i in far_out else vmem for i in range(len(outs))]
    return pl.pallas_call(
        body,
        out_shape=outs if many else outs[0],
        in_specs=[smem if i < scalars else hbm if i in far else vmem for i in range(len(args))],
        out_specs=specs if many else specs[0],
        compiler_params=pltpu.CompilerParams(vmem_limit_bytes=VMEM_BYTES),
        **more,
    )(*[pltpu.with_memory_space_constraint(x, pltpu.HBM) if i in far else x for i, x in enumerate(args)])


def swap_rows(edges):
    count = lax.axis_size("space")
    if count == 2:
        both = lax.ppermute(edges, "space", [(0, 1), (1, 0)])
        return both[0], both[1]
    below = lax.ppermute(edges[0], "space", [((i + 1) % count, i) for i in range(count)])
    above = lax.ppermute(edges[1], "space", [(i, (i + 1) % count) for i in range(count)])
    return below, above


def per_device(fine_nodes, init_state, mean_depth):
    nodes = fine_nodes[0]
    rows, cols = nodes.shape[-2:]
    outer, inner, spaces = lax.axis_size("outer"), lax.axis_size("inner"), lax.axis_size("space")
    group = ("inner", "space")
    owners = inner * spaces
    half = cols // 2
    width = half // owners
    slices = outer * inner * 2
    reach = slices - 2
    span = -(-(width + 2 * reach) // LANES) * LANES
    wide = rows + TILE
    at_outer, at_inner, at_core, at_space = (
        lax.axis_index(name) for name in ("outer", "inner", "core", "space")
    )
    first = at_outer + at_inner + at_core == 0
    place = jnp.stack([first.astype(jnp.int32), (at_outer == 0).astype(jnp.int32), at_core, at_inner, at_space])
    state, spread = (3, rows, cols), (3, wide, cols)
    swapped = [(0, 1), (1, 0)]
    plan = (spaces, rows, width, reach)

    prev = lax.ppermute(nodes[2], ("outer", "inner", "core"), [(i, i + 1) for i in range(slices - 1)])

    if spaces == 2 and dense(width, reach, rows):
        own_rows = 4 * rows * span // LANES
        own, edges = kernel(
            functools.partial(prepare_body, width, reach),
            [(own_rows, LANES), (own_rows + 2 * DEEP * cols // LANES, LANES)],
            place, mean_depth, init_state, scalars=1,
        )
        edges = lax.ppermute(edges, "space", swapped)
        windows, edges = (own, edges), (edges,)
    else:
        windows = all_windows(mean_depth, init_state, at_core * half, at_inner, spaces, width, reach, span)
        windows = (lax.all_to_all(windows, "space", 0, 0, tiled=True),)
        edges = jnp.stack([mean_depth[:DEEP, None], mean_depth[rows - DEEP :, None]])
        edges = swap_rows(edges)

    base, fk = kernel(
        blend_body, [state, spread], nodes, mean_depth, far=(0,),
        scratch_shapes=[
            pltpu.VMEM(spread, jnp.float32),
            pltpu.VMEM((3,) + state, jnp.float32),
            pltpu.SemaphoreType.DMA((3,)),
        ],
    )
    ffk, depth = kernel(second_body, [spread, (wide, cols)], fk, mean_depth, *edges)
    fine_shapes = [(3 * wide, half + 2 * LANES), (3 * wide, half)]
    fine_args = (place, base, prev, init_state, fk, ffk, depth)
    give, v_give = kernel(functools.partial(fine_body, False), fine_shapes, *fine_args, scalars=1)
    got = lax.ppermute(give, "core", swapped)
    keep, v_keep = kernel(functools.partial(fine_body, True), fine_shapes, *fine_args, scalars=1)
    tight = packed_rows(wide, width, reach)
    msg_shape = (owners, tight, LANES) if tight else (owners, 3 * wide, span)
    parts = (keep, give, v_keep, v_give)
    msgs, *parts = kernel(
        functools.partial(pair_body, width, reach, len(parts)), [msg_shape] + [x.shape for x in parts],
        place, depth, got, *parts, scalars=1, far_out=range(1 + len(parts)),
        scratch_shapes=[pltpu.VMEM(msg_shape, jnp.float32), pltpu.SemaphoreType.DMA((owners + len(parts),))],
    )
    recv = lax.all_to_all(msgs, group, 0, 0, tiled=True)
    spill = kernel(spill_body, (2, 2, 18, 1, half), *parts)
    low, high = swap_rows(spill)
    b_own, vee = kernel(
        mend_body, [spread, state], place, *parts, low, high, scalars=1, far_out=(1,),
        scratch_shapes=[pltpu.VMEM(state, jnp.float32), pltpu.SemaphoreType.DMA],
    )
    b_lent = lax.ppermute(b_own, "core", [(0, 1)])

    tight = packed_rows(spaces * rows, width, reach)
    total_shape = (tight, LANES) if tight else (3 * spaces * rows, span)
    total = kernel(functools.partial(total_body, *plan), total_shape, place, recv, *windows, scalars=1)
    carry = lax.ppermute(total, "outer", [(i, i + 1) for i in range(outer - 1)])
    back = kernel(
        functools.partial(chain_body, *plan), (owners, 3 * rows + 2 * TILE, width),
        place, recv, carry, *windows, scalars=1, far_out=(0,),
        scratch_shapes=[
            pltpu.VMEM((owners, 3 * rows + 2 * TILE, width), jnp.float32),
            pltpu.SemaphoreType.DMA((owners,)),
        ],
    )
    mine = lax.all_to_all(back, group, 0, 0, tiled=True)
    if width % LANES:
        mine = mine.transpose(1, 0, 2).reshape(1, 3 * rows + 2 * TILE, half)
    other = lax.ppermute(mine, "core", swapped)
    out = kernel(
        finish_body, (3,) + state, place, mine, other, b_own, b_lent, vee, depth,
        scalars=1, far=(3, 5), far_out=(0,),
        scratch_shapes=[
            pltpu.VMEM(spread, jnp.float32),
            pltpu.VMEM((3,) + state, jnp.float32),
            pltpu.VMEM(state, jnp.float32),
            pltpu.VMEM(spread, jnp.float32),
            pltpu.SemaphoreType.DMA((11,)),
        ],
    )
    return out[None]


def all_windows(depth, init, offset, at_inner, spaces, width, reach, span):
    fixed = jnp.concatenate([depth[None], init], axis=0)
    _, rows, cols = fixed.shape
    onward = jnp.concatenate([fixed, fixed[..., :span]], axis=-1)
    behind = jnp.concatenate([fixed[..., cols - span :], fixed], axis=-1)
    lane = lax.broadcasted_iota(jnp.int32, (4, rows, span), 2)
    windows = []
    for y in range(spaces):
        start = offset + (at_inner * spaces + y) * width
        ahead = lax.dynamic_slice_in_dim(onward, start, span, axis=2)
        back = lax.dynamic_slice_in_dim(behind, start, span, axis=2)
        windows.append(jnp.where(lane < span - reach, ahead, back).reshape(4 * rows, span))
    return jnp.stack(windows)


def solution(mesh):
    slices, spaces = mesh.shape["tm"], mesh.shape["space"]
    split = Mesh(mesh.devices.reshape(2, slices // 4, 2, spaces), ("outer", "inner", "core", "space"))
    nodes = P(("outer", "inner", "core"), None, None, "space", None)
    return jax.shard_map(
        per_device,
        mesh=split,
        in_specs=(nodes, P(None, "space", None), P("space", None)),
        out_specs=nodes,
        check_vma=False,
    )
```

time: 82.4 us -> 72.5 us (0.88)
  starting transfers between devices: 35.4 us -> 26.5 us
  Pallas kernels: 19.3 us -> 24.6 us
  waiting for transfers between devices: 19.6 us -> 15.8 us
  local copies, waits for them, and re-layouts: 7.4 us -> 4.59 us
    ppermute x1, starting transfers between devices: 8.72 us -> 2.69 us  [per_device(): got = lax.ppermute(give, 'core', swapped)]
    pallas_call x8 -> x11, Pallas kernels: 19.3 us -> 24.6 us  [kernel(): pl.pallas_call(body, out_shape=outs if many else outs[0], in_specs=[smem...]
    all_to_all x1 -> x0, starting transfers between devices: 3.43 us -> none  [per_device(): windows = lax.all_to_all(windows, 'space', 0, 0, tiled=True)]
    ppermute x2 -> x1, starting transfers between devices: 5.02 us -> 2.01 us  [swap_rows(): both = lax.ppermute(edges, 'space', [(0, 1), (1, 0)])]
    unnamed x16, local copies, waits for them, and re-layouts: 5.12 us -> 2.15 us
    all_to_all x1 -> x0, waiting for transfers between devices: 2.67 us -> none  [per_device(): windows = lax.all_to_all(windows, 'space', 0, 0, tiled=True)]
    ppermute x0 -> x1, starting transfers between devices: none -> 2.4 us  [per_device(): edges = lax.ppermute(edges, 'space', swapped)]
    all_to_all x1, waiting for transfers between devices: 8.52 us -> 6.19 us  [per_device(): recv = lax.all_to_all(msgs, group, 0, 0, tiled=True)]
  transfers between devices with their start and end apart: 10 -> 9, of which waited for: 6 -> 5; matrix products, arithmetic and copies ran while one was open for 3% -> 2% of each run, Pallas kernels for 11% -> 19%
where the time goes in v4:
time: 72.5 us; the launch traced here: 71.9 us
  starting transfers between devices  26.5 us (37%)
  Pallas kernels  24.6 us (34%)
  waiting for transfers between devices  15.8 us (22%)
  local copies, waits for them, and re-layouts  4.59 us (6%)
    pallas_call x11, Pallas kernels, kernel(): pl.pallas_call(body, out_shape=outs if many else outs[0], in_specs=[smem...  24.6 us
    all_to_all x1, waiting for transfers between devices, per_device(): recv = lax.all_to_all(msgs, group, 0, 0, tiled=True)  6.19 us
    all_to_all x1, starting transfers between devices, per_device(): recv = lax.all_to_all(msgs, group, 0, 0, tiled=True)  5.77 us
    all_to_all x1, starting transfers between devices, per_device(): mine = lax.all_to_all(back, group, 0, 0, tiled=True)  5.16 us
    ppermute x1, starting transfers between devices, per_device(): carry = lax.ppermute(total, 'outer', [(i, i + 1) for i in range(outer - 1)])  4.5 us
    all_to_all x1, waiting for transfers between devices, per_device(): mine = lax.all_to_all(back, group, 0, 0, tiled=True)  3.12 us
    ppermute x1, starting transfers between devices, per_device(): got = lax.ppermute(give, 'core', swapped)  2.69 us
    ppermute x1, starting transfers between devices, per_device(): lax.ppermute(nodes[2], ('outer', 'inner', 'core'), [(i, i + 1) for i in r...  2.45 us
  transfers between devices with their start and end apart: 9, of which 5 were waited for; matrix products, arithmetic and copies ran while one was open for 2% of the time, Pallas kernels for 19%

profile of v4, /device:TPU:0, one launch (start us, length us, event | category | flops | bytes accessed | tf_op | source)
XLA Modules:
  0.0 71.9 jit_solution(8697791546021835806)
XLA Ops:
  0.0 0.0 copy-start.3
  0.0 0.0 copy-start
  0.0 1.3 %slice_bitcast_fusion = f32[3,16,4096]{2,1,0:T(8,128)S(1)} fusion(f32[1,3,3,16,4096]{4,3,2,1,0:T(8,128)} %param.3), kind=kLoop, calls=%fused_computation | loop fusion | bytes 1572864 | tf_op jit(solution)/shard_map/squeeze | solution.py:454
  1.3 2.4 %collective-permute-start.1 = (f32[3,16,4096]{2,1,0:T(8,128)S(1)}, f32[3,16,4096]{2,1,0:T(8,128)S(1)}, u32[]{:S(2)}, u32[]{:S(2)}) collective-permute-start(f32[3,16,4096]{2,1,0:T(8,128)S(1)} %slice_bitcast_fusion), channel_id=1, source_target_pairs={{0,2},{2,4},{4,6},{6,8},{8,10},{10,12},{12,14},{14,16},{16,18},{18... | collective-permute-start | bytes 2359304 | tf_op jit(solution)/shard_map/ppermute | solution.py:454
  3.7 0.1 stack.31.place
  3.8 0.0 copy-done.3
  3.8 0.0 copy-done
  3.8 0.6 shard_map.38
  4.5 2.4 %collective-permute-start = (f32[384,128]{1,0:T(8,128)S(1)}, f32[384,128]{1,0:T(8,128)S(1)}, u32[]{:S(2)}, u32[]{:S(2)}) collective-permute-start(f32[384,128]{1,0:T(8,128)S(1)} %get-tuple-element.23), channel_id=1, source_target_pairs={{0,1},{1,0},{2,3},{3,2},{4,5},{5,4},{6,7},{7,6},{8,9},{9,8},{10,11... | collective-permute-start | bytes 589832 | tf_op jit(solution)/shard_map/ppermute | solution.py:463
  6.9 2.5 %shard_map.37 = (f32[3,16,4096]{2,1,0:T(8,128)S(1)}, f32[3,24,4096]{2,1,0:T(8,128)S(1)}) custom-call(f32[3,3,16,4096]{3,2,1,0:T(8,128)} %bitcast.13, f32[16,4096]{1,0:T(8,128)S(1)} %copy-done.3), custom_call_target="tpu_custom_call" | custom-call | tf_op jit(solution)/shard_map/pallas_call | solution.py:413
  9.4 2.1 %collective-permute-done.rest_0_.rest_1_ = f32[384,128]{1,0:T(8,128)S(1)} collective-permute-done((f32[384,128]{1,0:T(8,128)S(1)}, f32[384,128]{1,0:T(8,128)S(1)}, u32[]{:S(2)}, u32[]{:S(2)}) %collective-permute-start) | collective-permute-done | bytes 196640 | tf_op jit(solution)/shard_map/ppermute | solution.py:463
  11.4 1.1 %shard_map.39 = (f32[3,24,4096]{2,1,0:T(8,128)S(1)}, f32[24,4096]{1,0:T(8,128)S(1)}) custom-call(f32[3,24,4096]{2,1,0:T(8,128)S(1)} %get-tuple-element.22.fk, f32[16,4096]{1,0:T(8,128)S(1)} %copy-done.3, f32[384,128]{1,0:T(8,128)S(1)} %collective-permute-done.rest_0_.rest_1_), custom_call_target="tpu_custom_call" | custom-call | tf_op jit(solution)/shard_map/pallas_call | solution.py:413
  12.5 0.0 collective-permute-done.1.prev
  12.6 2.3 %shard_map.40 = (f32[72,2304]{1,0:T(8,128)S(1)}, f32[72,2048]{1,0:T(8,128)S(1)}) custom-call(s32[5]{0:T(128)S(1)} %stack.31.place, f32[3,16,4096]{2,1,0:T(8,128)S(1)} %get-tuple-element.25.base, f32[3,16,4096]{2,1,0:T(8,128)S(1)} %collective-permute-done.1.prev, f32[3,16,4096]{2,1,0:T(8,128)S(1)} %copy-done, f32[3,24,4096]{2,1,0:T(8,128)S(1)} %get-tuple-element.22.fk, ...), custom_call_target="tpu_custom_call" | custom-call | tf_op jit(solution)/shard_map/pallas_call | solution.py:413
  14.8 2.7 %collective-permute-start.2 = (f32[72,2304]{1,0:T(8,128)S(1)}, f32[72,2304]{1,0:T(8,128)S(1)}, u32[]{:S(2)}, u32[]{:S(2)}) collective-permute-start(f32[72,2304]{1,0:T(8,128)S(1)} %get-tuple-element.27.rest_1_), channel_id=1, source_target_pairs={{0,2},{2,0},{1,3},{3,1},{4,6},{6,4},{5,7},{7,5},{8,10},{10,8},{9,1... | collective-permute-start | bytes 1990664 | tf_op jit(solution)/shard_map/ppermute | solution.py:483
  17.5 2.3 %shard_map.41 = (f32[72,2304]{1,0:T(8,128)S(1)}, f32[72,2048]{1,0:T(8,128)S(1)}) custom-call(s32[5]{0:T(128)S(1)} %stack.31.place, f32[3,16,4096]{2,1,0:T(8,128)S(1)} %get-tuple-element.25.base, f32[3,16,4096]{2,1,0:T(8,128)S(1)} %collective-permute-done.1.prev, f32[3,16,4096]{2,1,0:T(8,128)S(1)} %copy-done, f32[3,24,4096]{2,1,0:T(8,128)S(1)} %get-tuple-element.22.fk, ...), custom_call_target="tpu_custom_call" | custom-call | tf_op jit(solution)/shard_map/pallas_call | solution.py:413
  19.8 0.0 collective-permute-done.2.got
  19.8 2.8 %shard_map.42 = (f32[8,168,128]{2,1,0:T(8,128)}, f32[72,2304]{1,0:T(8,128)}, f32[72,2304]{1,0:T(8,128)}, f32[72,2048]{1,0:T(8,128)}, f32[72,2048]{1,0:T(8,128)}) custom-call(s32[5]{0:T(128)S(1)} %stack.31.place, f32[24,4096]{1,0:T(8,128)S(1)} %get-tuple-element.24.depth_ref, f32[72,2304]{1,0:T(8,128)S(1)} %collective-permute-done.2.got, ...), custom_call_target="tpu_custom_call" | custom-call | tf_op jit(solution)/shard_map/pallas_call | solution.py:413
  22.6 0.0 copy-start.1
  22.6 0.0 copy-start.2
  22.7 5.8 %all-to-all-start = ((f32[8,168,128]{2,1,0:T(8,128)}), f32[8,168,128]{2,1,0:T(8,128)S(1)}, u32[]{:S(2)}, u32[]{:S(2)}) async-start(f32[8,168,128]{2,1,0:T(8,128)} %get-tuple-element.31), calls=%async_computation | async-start | bytes 1376256 | tf_op jit(solution)/shard_map/all_to_all | solution.py:493
  28.4 0.0 copy-done.1
  28.4 0.0 copy-done.2
  28.4 0.0 copy-start.4
  28.4 1.1 %copy-done.4 = f32[72,2048]{1,0:T(8,128)S(1)} copy-done((f32[72,2048]{1,0:T(8,128)S(1)}, f32[72,2048]{1,0:T(8,128)}, u32[]{:S(2)}) %copy-start.4) | copy-done | bytes 589848
  29.5 0.0 copy-start.6
  29.5 1.1 %copy-done.6 = f32[72,2048]{1,0:T(8,128)S(1)} copy-done((f32[72,2048]{1,0:T(8,128)S(1)}, f32[72,2048]{1,0:T(8,128)}, u32[]{:S(2)}) %copy-start.6) | copy-done | bytes 589848
  30.6 0.9 %shard_map.45 = f32[2,2,18,1,2048]{4,3,2,1,0:T(1,128)} custom-call(f32[72,2304]{1,0:T(8,128)S(1)} %copy-done.1, f32[72,2304]{1,0:T(8,128)S(1)} %copy-done.2, f32[72,2048]{1,0:T(8,128)S(1)} %copy-done.4, f32[72,2048]{1,0:T(8,128)S(1)} %copy-done.6), custom_call_target="tpu_custom_call" | custom-call | tf_op jit(solution)/shard_map/pallas_call | solution.py:413
  31.5 2.0 %collective-permute-start.5 = (f32[2,2,18,1,2048]{4,3,2,1,0:T(1,128)}, f32[2,2,18,1,2048]{4,3,2,1,0:T(1,128)}, u32[]{:S(2)}, u32[]{:S(2)}) collective-permute-start(f32[2,2,18,1,2048]{4,3,2,1,0:T(1,128)} %shard_map.45), channel_id=1, source_target_pairs={{0,1},{1,0},{2,3},{3,2},{4,5},{5,4},{6,7},{7,6},{8,9},{9,8},{10,11... | collective-permute-start | bytes 1769480 | tf_op jit(solution)/shard_map/ppermute | solution.py:426
  33.5 6.2 %all-to-all-done.recv = f32[8,168,128]{2,1,0:T(8,128)S(1)} async-done(((f32[8,168,128]{2,1,0:T(8,128)}), f32[8,168,128]{2,1,0:T(8,128)S(1)}, u32[]{:S(2)}, u32[]{:S(2)}) %all-to-all-start) | async-done | bytes 688160 | tf_op jit(solution)/shard_map/all_to_all | solution.py:493
  39.7 1.7 %shard_map.43 = f32[216,128]{1,0:T(8,128)S(1)} custom-call(s32[5]{0:T(128)S(1)} %stack.31.place, f32[8,168,128]{2,1,0:T(8,128)S(1)} %all-to-all-done.recv, f32[192,128]{1,0:T(8,128)S(1)} %get-tuple-element.32.rest_0_, f32[384,128]{1,0:T(8,128)S(1)} %collective-permute-done.rest_0_.rest_1_), custom_call_target="tpu_custom_call" | custom-call | tf_op jit(solution)/shard_map/pallas_call | solution.py:413
  41.4 4.5 %collective-permute-start.3 = (f32[216,128]{1,0:T(8,128)S(1)}, f32[216,128]{1,0:T(8,128)S(1)}, u32[]{:S(2)}, u32[]{:S(2)}) collective-permute-start(f32[216,128]{1,0:T(8,128)S(1)} %shard_map.43), channel_id=1, source_target_pairs={{0,16},{1,17},{2,18},{3,19},{4,20},{5,21},{6,22},{7,23},{8,24},{9,... | collective-permute-start | bytes 331784 | tf_op jit(solution)/shard_map/ppermute | solution.py:505
  45.9 2.3 %collective-permute-done.3.carry = f32[216,128]{1,0:T(8,128)S(1)} collective-permute-done((f32[216,128]{1,0:T(8,128)S(1)}, f32[216,128]{1,0:T(8,128)S(1)}, u32[]{:S(2)}, u32[]{:S(2)}) %collective-permute-start.3) | collective-permute-done | bytes 110624 | tf_op jit(solution)/shard_map/ppermute | solution.py:505
  48.2 2.1 %shard_map.44 = f32[8,64,256]{2,1,0:T(8,128)} custom-call(s32[5]{0:T(128)S(1)} %stack.31.place, f32[8,168,128]{2,1,0:T(8,128)S(1)} %all-to-all-done.recv, f32[216,128]{1,0:T(8,128)S(1)} %collective-permute-done.3.carry, f32[192,128]{1,0:T(8,128)S(1)} %get-tuple-element.32.rest_0_, f32[384,128]{1,0:T(8,128)S(1)} %collective-permute-done.rest_0_.rest_1_), custom_call_target="tpu_custom_call" | custom-call | tf_op jit(solution)/shard_map/pallas_call | solution.py:413
  50.4 0.0 copy-start.5
  50.4 0.0 copy-start.7
  50.4 5.2 %all-to-all-start.1 = ((f32[8,64,256]{2,1,0:T(8,128)}), f32[8,64,256]{2,1,0:T(8,128)}, u32[]{:S(2)}, u32[]{:S(2)}) async-start(f32[8,64,256]{2,1,0:T(8,128)} %shard_map.44), calls=%async_computation.1 | async-start | bytes 1048576 | tf_op jit(solution)/shard_map/all_to_all | solution.py:514
  55.6 0.0 collective-permute-done.5
  55.6 1.1 %slice_bitcast_fusion.1 = (f32[2,18,1,2048]{3,2,1,0:T(1,128)S(1)}, f32[2,18,1,2048]{3,2,1,0:T(1,128)S(1)}) fusion(f32[2,2,18,1,2048]{4,3,2,1,0:T(1,128)} %collective-permute-done.5), kind=kLoop, calls=%fused_computation.1 | loop fusion | bytes 1179648 | tf_op jit(solution)/shard_map/squeeze | solution.py:427
  56.7 0.0 copy-done.5
  56.7 0.0 copy-done.7
  56.7 2.7 %shard_map.46 = (f32[3,24,4096]{2,1,0:T(8,128)}, f32[3,16,4096]{2,1,0:T(8,128)}) custom-call(s32[5]{0:T(128)S(1)} %stack.31.place, f32[72,2304]{1,0:T(8,128)S(1)} %copy-done.1, f32[72,2304]{1,0:T(8,128)S(1)} %copy-done.2, f32[72,2048]{1,0:T(8,128)S(1)} %copy-done.5, f32[72,2048]{1,0:T(8,128)S(1)} %copy-done.7, f32[2,18,1,2048]{3,2,1,0:T(1,128)S(1)} %get-tuple-element.40.low, ...), custom_call_target="tpu_custom_call" | custom-call | tf_op jit(solution)/shard_map/pallas_call | solution.py:413
  59.4 1.5 %collective-permute-start.6 = (f32[3,24,4096]{2,1,0:T(8,128)}, f32[3,24,4096]{2,1,0:T(8,128)S(1)}, u32[]{:S(2)}, u32[]{:S(2)}) collective-permute-start(f32[3,24,4096]{2,1,0:T(8,128)} %get-tuple-element.37.b_far), channel_id=1, source_target_pairs={{0,2},{1,3},{4,6},{5,7},{8,10},{9,11},{12,14},{13,15},{16,18},{17,... | collective-permute-start | bytes 3538952 | tf_op jit(solution)/shard_map/ppermute | solution.py:500
  61.0 3.1 %all-to-all-done.1.mine = f32[8,64,256]{2,1,0:T(8,128)} async-done(((f32[8,64,256]{2,1,0:T(8,128)}), f32[8,64,256]{2,1,0:T(8,128)}, u32[]{:S(2)}, u32[]{:S(2)}) %all-to-all-start.1) | async-done | bytes 524320 | tf_op jit(solution)/shard_map/all_to_all | solution.py:514
  64.1 0.0 collective-permute-start.4
  64.1 0.0 collective-permute-done.6.b_lent
  64.1 2.1 %collective-permute-done.4.other = f32[8,64,256]{2,1,0:T(8,128)S(1)} collective-permute-done((f32[8,64,256]{2,1,0:T(8,128)}, f32[8,64,256]{2,1,0:T(8,128)S(1)}, u32[]{:S(2)}, u32[]{:S(2)}) %collective-permute-start.4) | collective-permute-done | bytes 524320 | tf_op jit(solution)/shard_map/ppermute | solution.py:517
  66.2 5.5 %shard_map.47 = f32[3,3,16,4096]{3,2,1,0:T(8,128)} custom-call(s32[5]{0:T(128)S(1)} %stack.31.place, f32[8,64,256]{2,1,0:T(8,128)} %all-to-all-done.1.mine, f32[8,64,256]{2,1,0:T(8,128)S(1)} %collective-permute-done.4.other, f32[3,24,4096]{2,1,0:T(8,128)} %get-tuple-element.37.b_far, f32[3,24,4096]{2,1,0:T(8,128)S(1)} %collective-permute-done.6.b_lent, ...), custom_call_target="tpu_custom_call" | custom-call | tf_op jit(solution)/shard_map/pallas_call | solution.py:413
Async XLA Ops:
  0.0 3.8 %copy-start.3 = (f32[16,4096]{1,0:T(8,128)S(1)}, f32[16,4096]{1,0:T(8,128)}, u32[]{:S(2)}) copy-start(f32[16,4096]{1,0:T(8,128)} %depth.5) | copy-start | bytes 786436
  0.0 3.8 %copy-start = (f32[3,16,4096]{2,1,0:T(8,128)S(1)}, f32[3,16,4096]{2,1,0:T(8,128)}, u32[]{:S(2)}) copy-start(f32[3,16,4096]{2,1,0:T(8,128)} %init.5) | copy-start | bytes 2359300
  1.3 11.3 %collective-permute-start.1 = (f32[3,16,4096]{2,1,0:T(8,128)S(1)}, f32[3,16,4096]{2,1,0:T(8,128)S(1)}, u32[]{:S(2)}, u32[]{:S(2)}) collective-permute-start(f32[3,16,4096]{2,1,0:T(8,128)S(1)} %slice_bitcast_fusion), channel_id=1, source_target_pairs={{0,2},{2,4},{4,6},{6,8},{8,10},{10,12},{12,14},{14,16},{16,18},{18... | collective-permute-start | bytes 2359304 | tf_op jit(solution)/shard_map/ppermute | solution.py:454
  4.5 6.9 %collective-permute-start = (f32[384,128]{1,0:T(8,128)S(1)}, f32[384,128]{1,0:T(8,128)S(1)}, u32[]{:S(2)}, u32[]{:S(2)}) collective-permute-start(f32[384,128]{1,0:T(8,128)S(1)} %get-tuple-element.23), channel_id=1, source_target_pairs={{0,1},{1,0},{2,3},{3,2},{4,5},{5,4},{6,7},{7,6},{8,9},{9,8},{10,11... | collective-permute-start | bytes 589832 | tf_op jit(solution)/shard_map/ppermute | solution.py:463
  14.8 5.0 %collective-permute-start.2 = (f32[72,2304]{1,0:T(8,128)S(1)}, f32[72,2304]{1,0:T(8,128)S(1)}, u32[]{:S(2)}, u32[]{:S(2)}) collective-permute-start(f32[72,2304]{1,0:T(8,128)S(1)} %get-tuple-element.27.rest_1_), channel_id=1, source_target_pairs={{0,2},{2,0},{1,3},{3,1},{4,6},{6,4},{5,7},{7,5},{8,10},{10,8},{9,1... | collective-permute-start | bytes 1990664 | tf_op jit(solution)/shard_map/ppermute | solution.py:483
  22.6 5.8 %copy-start.1 = (f32[72,2304]{1,0:T(8,128)S(1)}, f32[72,2304]{1,0:T(8,128)}, u32[]{:S(2)}) copy-start(f32[72,2304]{1,0:T(8,128)} %get-tuple-element.33.b_keep) | copy-start | bytes 1990660
  22.6 5.8 %copy-start.2 = (f32[72,2304]{1,0:T(8,128)S(1)}, f32[72,2304]{1,0:T(8,128)}, u32[]{:S(2)}) copy-start(f32[72,2304]{1,0:T(8,128)} %get-tuple-element.34.b_give) | copy-start | bytes 1990660
  22.7 17.1 %all-to-all-start = ((f32[8,168,128]{2,1,0:T(8,128)}), f32[8,168,128]{2,1,0:T(8,128)S(1)}, u32[]{:S(2)}, u32[]{:S(2)}) async-start(f32[8,168,128]{2,1,0:T(8,128)} %get-tuple-element.31), calls=%async_computation | async-start | bytes 1376256 | tf_op jit(solution)/shard_map/all_to_all | solution.py:493
  28.4 1.1 %copy-start.4 = (f32[72,2048]{1,0:T(8,128)S(1)}, f32[72,2048]{1,0:T(8,128)}, u32[]{:S(2)}) copy-start(f32[72,2048]{1,0:T(8,128)} %get-tuple-element.35.v_keep) | copy-start | bytes 1769476
  29.5 1.1 %copy-start.6 = (f32[72,2048]{1,0:T(8,128)S(1)}, f32[72,2048]{1,0:T(8,128)}, u32[]{:S(2)}) copy-start(f32[72,2048]{1,0:T(8,128)} %get-tuple-element.36.v_give) | copy-start | bytes 1769476
  31.5 24.1 %collective-permute-start.5 = (f32[2,2,18,1,2048]{4,3,2,1,0:T(1,128)}, f32[2,2,18,1,2048]{4,3,2,1,0:T(1,128)}, u32[]{:S(2)}, u32[]{:S(2)}) collective-permute-start(f32[2,2,18,1,2048]{4,3,2,1,0:T(1,128)} %shard_map.45), channel_id=1, source_target_pairs={{0,1},{1,0},{2,3},{3,2},{4,5},{5,4},{6,7},{7,6},{8,9},{9,8},{10,11... | collective-permute-start | bytes 1769480 | tf_op jit(solution)/shard_map/ppermute | solution.py:426
  41.4 6.8 %collective-permute-start.3 = (f32[216,128]{1,0:T(8,128)S(1)}, f32[216,128]{1,0:T(8,128)S(1)}, u32[]{:S(2)}, u32[]{:S(2)}) collective-permute-start(f32[216,128]{1,0:T(8,128)S(1)} %shard_map.43), channel_id=1, source_target_pairs={{0,16},{1,17},{2,18},{3,19},{4,20},{5,21},{6,22},{7,23},{8,24},{9,... | collective-permute-start | bytes 331784 | tf_op jit(solution)/shard_map/ppermute | solution.py:505
  50.4 6.3 %copy-start.5 = (f32[72,2048]{1,0:T(8,128)S(1)}, f32[72,2048]{1,0:T(8,128)}, u32[]{:S(2)}) copy-start(f32[72,2048]{1,0:T(8,128)} %get-tuple-element.35.v_keep) | copy-start | bytes 1769476
  50.4 6.3 %copy-start.7 = (f32[72,2048]{1,0:T(8,128)S(1)}, f32[72,2048]{1,0:T(8,128)}, u32[]{:S(2)}) copy-start(f32[72,2048]{1,0:T(8,128)} %get-tuple-element.36.v_give) | copy-start | bytes 1769476
  50.4 13.7 %all-to-all-start.1 = ((f32[8,64,256]{2,1,0:T(8,128)}), f32[8,64,256]{2,1,0:T(8,128)}, u32[]{:S(2)}, u32[]{:S(2)}) async-start(f32[8,64,256]{2,1,0:T(8,128)} %shard_map.44), calls=%async_computation.1 | async-start | bytes 1048576 | tf_op jit(solution)/shard_map/all_to_all | solution.py:514
  59.4 4.7 %collective-permute-start.6 = (f32[3,24,4096]{2,1,0:T(8,128)}, f32[3,24,4096]{2,1,0:T(8,128)S(1)}, u32[]{:S(2)}, u32[]{:S(2)}) collective-permute-start(f32[3,24,4096]{2,1,0:T(8,128)} %get-tuple-element.37.b_far), channel_id=1, source_target_pairs={{0,2},{1,3},{4,6},{5,7},{8,10},{9,11},{12,14},{13,15},{16,18},{17,... | collective-permute-start | bytes 3538952 | tf_op jit(solution)/shard_map/ppermute | solution.py:500
  64.1 2.1 %collective-permute-start.4 = (f32[8,64,256]{2,1,0:T(8,128)}, f32[8,64,256]{2,1,0:T(8,128)S(1)}, u32[]{:S(2)}, u32[]{:S(2)}) collective-permute-start(f32[8,64,256]{2,1,0:T(8,128)} %all-to-all-done.1.mine), channel_id=1, source_target_pairs={{0,2},{2,0},{1,3},{3,1},{4,6},{6,4},{5,7},{7,5},{8,10},{10,8},{9,1... | collective-permute-start | bytes 1572872 | tf_op jit(solution)/shard_map/ppermute | solution.py:517

commit v5 on v4

--- a/solution.py
+++ b/solution.py
@@ -71,17 +71,41 @@
     return ref[lead + (slice(None), pl.ds(pl.multiple_of(at, LANES), size))]
 
 
-def prepare_body(width, reach, place, depth, init, own_out, edge_out):
+def last_body(nodes, out, sem):
+    copy = pltpu.make_async_copy(nodes.at[2], out, sem)
+    copy.start()
+    copy.wait()
+
+
+def prepare_body(width, reach, place, depth_far, init, own_out, edge_out, depth, held, sems):
     rows, cols = depth.shape
     lane = lax.broadcasted_iota(jnp.int32, (rows, LANES), 1)
-    for out, y in ((own_out, place[4]), (edge_out, 1 - place[4])):
+    copies = [pltpu.make_async_copy(depth_far, depth, sems.at[0])]
+    for h, y in enumerate((place[4], 1 - place[4])):
         start = place[2] * (cols // 2) + (place[3] * 2 + y) * width
         after = lax.rem(start + width, cols)
         before = lax.rem(start - LANES + cols, cols)
         for i in range(4):
-            ref, lead = (depth, ()) if i == 0 else (init, (i - 1,))
-            parts = [cut(ref, lead, start + t * LANES) for t in range(width // LANES)]
-            parts.append(jnp.where(lane < LANES - reach, cut(ref, lead, after), cut(ref, lead, before)))
+            ref = depth_far if i == 0 else init.at[i - 1]
+            for k, (at, to, size) in enumerate(
+                ((start, 0, width), (after, width, LANES), (before, width + LANES, LANES))
+            ):
+                copies.append(
+                    pltpu.make_async_copy(
+                        ref.at[:, pl.ds(pl.multiple_of(at, LANES), size)],
+                        held.at[h, i, :, to : to + size],
+                        sems.at[1 + (h * 4 + i) * 3 + k],
+                    )
+                )
+    for copy in copies:
+        copy.start()
+    for copy in copies:
+        copy.wait()
+    for h, out in enumerate((own_out, edge_out)):
+        for i in range(4):
+            parts = [held[h, i, :, t * LANES : (t + 1) * LANES] for t in range(width // LANES)]
+            after, before = held[h, i, :, width : width + LANES], held[h, i, :, width + LANES :]
+            parts.append(jnp.where(lane < LANES - reach, after, before))
             for t, part in enumerate(parts):
                 at = (4 * t + i) * rows
                 out[at : at + rows, :] = part
@@ -92,9 +116,10 @@
             at += 1
 
 
-def blend_body(nodes, depth, base_out, fk_out, state, near, sems):
+def blend_body(nodes, depth_far, base_out, fk_out, depth_out, state, near, depth, sems):
     rows, cols = depth.shape
     copies = [pltpu.make_async_copy(nodes.at[:, f], near.at[f], sems.at[f]) for f in range(3)]
+    copies.append(pltpu.make_async_copy(depth_far, depth, sems.at[3]))
     for copy in copies:
         copy.start()
     none = jnp.zeros((TILE, cols), jnp.float32)
@@ -104,22 +129,24 @@
         base_out[f] = (DT / 24.0) * (8.0 * n1 - 7.0 * n0 - n2)
         state[f, :rows, :] = (DT / 4.0) * (n0 - 2.0 * n1 + n2)
         state[f, rows:, :] = none
+    copies[3].wait()
     half_depth = jnp.concatenate([0.5 * depth[...], none], axis=0)
+    depth_out[...] = half_depth
     fk = tendency(tuple(state[f] for f in range(3)), half_depth)
     for f in range(3):
         fk_out[f] = fk[f]
 
 
-def second_body(fk, depth, *rest):
+def second_body(fk, bare, *rest):
     *edges, ffk_out, depth_out = rest
-    rows, cols = depth.shape
-    depth_out[:rows, :] = 0.5 * depth[...]
-    depth_out[rows:, :] = jnp.zeros((TILE, cols), jnp.float32)
+    rows, cols = bare.shape[0] - TILE, bare.shape[1]
+    depth_out[...] = bare[...]
     for r in range(DEEP):
         below, above = rows + r, rows + TILE - DEEP + r
-        if len(edges) == 2:
-            depth_out[below : below + 1, :] = 0.5 * edges[0][r]
-            depth_out[above : above + 1, :] = 0.5 * edges[1][r]
+        if len(edges) == 2 or len(edges[0].shape) > 2:
+            low, high = edges if len(edges) == 2 else (edges[0].at[0], edges[0].at[1])
+            depth_out[below : below + 1, :] = 0.5 * low[r]
+            depth_out[above : above + 1, :] = 0.5 * high[r]
             continue
         tiles = cols // LANES
         base = edges[0].shape[0] - 2 * DEEP * tiles
@@ -157,10 +184,17 @@
         b_out[at, :] = DT * (u[f] + (1.0 / 6.0) * (HALF * fu[f] + window(ffk, (f,), half)))
 
 
-def spill_body(b_keep, b_give, v_keep, v_give, spill_out):
+def spill_body(b_keep, b_give, v_keep, v_give, spill_out, v_spread, sems):
     wide = b_keep.shape[0] // 3
     rows = wide - TILE
-    for h, (b, v) in enumerate(((b_keep, v_keep), (b_give, v_give))):
+    copies = [
+        pltpu.make_async_copy(v.at[pl.ds(f * wide + rows, TILE), :], v_spread.at[h, f], sems.at[3 * h + f])
+        for h, v in enumerate((v_keep, v_give))
+        for f in range(3)
+    ]
+    for copy in copies:
+        copy.start()
+    for h, b in enumerate((b_keep, b_give)):
         inside = slice(LANES, b.shape[1] - LANES)
         for f in range(3):
             top = f * wide
@@ -168,12 +202,24 @@
                 for r in range(DEEP):
                     spill_out[side, h, DEEP * f + r] = b[top + spread + r : top + spread + r + 1, inside]
                 spill_out[side, h, 9 + f] = b[top + edge : top + edge + 1, inside]
-                spread = wide - 2 if side == 0 else rows
+    for copy in copies:
+        copy.wait()
+    for h in range(2):
+        for f in range(3):
+            for side, spread in ((0, TILE - 2), (1, 0)):
                 for r in range(2):
-                    spill_out[side, h, 12 + 2 * f + r] = v[top + spread + r : top + spread + r + 1, :]
-
-
-def mend_body(place, b_keep, b_give, v_keep, v_give, low, high, b_out, v_far, v_out, sem):
+                    spill_out[side, h, 12 + 2 * f + r] = v_spread[h, f, spread + r : spread + r + 1, :]
+
+
+def mend_body(place, *refs):
+    far, edges, (b_out, v_far, v_out, *near, sems) = refs[:4], refs[4:-8], refs[-8:]
+    low, high = (edges[0].at[0], edges[0].at[1]) if len(edges) == 1 else edges
+    copies = [pltpu.make_async_copy(x, y, sems.at[i]) for i, (x, y) in enumerate(zip(far, near))]
+    for i in (2, 3, 0, 1):
+        copies[i].start()
+    b_keep, b_give, v_keep, v_give = near
+    copies[2].wait()
+    copies[3].wait()
     rows = v_out.shape[1]
     wide = rows + TILE
     size = v_keep.shape[1]
@@ -186,8 +232,10 @@
                 for at, more in ((r, high), (rows - 2 + r, low)):
                     old = v[f * wide + at : f * wide + at + 1, :]
                     v_out[f, at : at + 1, to] = old + more[h, 12 + 2 * f + r]
-    copy = pltpu.make_async_copy(v_out, v_far, sem)
+    copy = pltpu.make_async_copy(v_out, v_far, sems.at[4])
     copy.start()
+    copies[0].wait()
+    copies[1].wait()
     for h, (half, b, _) in enumerate(halves):
         to = pl.ds(pl.multiple_of(half * size, LANES), size)
         inside = slice(LANES, LANES + size)
@@ -305,14 +353,25 @@
     return stepped(stepped(q, step_depth), step_depth)
 
 
-def total_body(spaces, rows, width, reach, place, recv, *rest):
+def ahead_body(slots, rows, place, *rest):
+    *win, out = rest
+    step_depth = HALF * window_field(win, 0, rows, place)
+    q = tuple(window_field(win, 1 + f, rows, place) for f in range(3))
+    for _ in range(slots):
+        q = two_steps(q, step_depth)
+    for f in range(3):
+        out[f] = q[f]
+
+
+def total_body(spaces, rows, width, reach, place, recv, ahead, *rest):
     *win, total_out = rest
     slots = recv.shape[0] // spaces
     step_depth = HALF * window_field(win, 0, rows, place)
-    q = tuple(window_field(win, 1 + f, rows, place) for f in range(3))
-    for slot in range(slots):
+    q = joined(recv, 0, spaces, rows, width, reach)
+    for slot in range(1, slots):
         b = joined(recv, slot, spaces, rows, width, reach)
         q = tuple(x + y for x, y in zip(b, two_steps(q, step_depth)))
+    q = tuple(x + ahead[f] for f, x in enumerate(q))
     all_rows = rows * spaces
     if not dense(width, reach, rows):
         for f in range(3):
@@ -360,30 +419,58 @@
         copy.wait()
 
 
-def finish_body(place, mine, other, b_far, b_lent, v_far, depth_ref, out, state, made, v_ref, b_own, sems):
-    rows, cols = v_ref.shape[1:]
-    fetches = [pltpu.make_async_copy(b_far, b_own, sems.at[9]), pltpu.make_async_copy(v_far, v_ref, sems.at[10])]
-    for fetch in fetches:
-        fetch.start()
+def finish_body(near, place, *refs):
+    if near:
+        mine, b_far, b_lent, v_far, depth_ref, out, state, b_own, v_ref, made, sems = refs
+        other = None
+    else:
+        mine, other, b_far, b_lent, v_far, depth_ref, _, out, state, b_own, v_ref, made, sems = refs
+    rows = v_ref.shape[1]
     wide = rows + TILE
-    pieces, _, width = mine.shape
+    half = depth_ref.shape[1] // 2
+    ours, theirs = place[2] * half, (1 - place[2]) * half
+    side = 2 * LANES
+    if near:
+        parts = [(ours, half, mine, 0)]
+        pieces = [(LANES, half - 2 * LANES, ours + LANES)]
+    else:
+        parts = [(ours + half - side, side, mine, half - side), (theirs, half, other, 0), (ours, side, mine, 0)]
+        pieces = [(LANES, LANES, ours + half - LANES), (side, half, theirs), (side + half, LANES, ours)]
+
+    def at(start, size):
+        return pl.ds(pl.multiple_of(start, LANES), size)
+
+    fetches, local = [], 0
+    for i, (start, size, source, first) in enumerate(parts):
+        width = source.shape[2]
+        here = slice(local, local + size)
+        for k, (far, held) in enumerate(((b_far, b_own), (v_far, v_ref))):
+            copy = pltpu.make_async_copy(far.at[:, :, at(start, size)], held.at[:, :, here], sems.at[2 * i + k])
+            copy.start()
+            fetches.append(copy)
+        step = min(width, size)
+        for c in range(0, size, step):
+            j, off = (first + c) // width, (first + c) % width
+            to = slice(local + c, local + c + step)
+            for f in range(3):
+                state[f, :rows, to] = source[j, f * rows : (f + 1) * rows, off : off + step]
+                for r, row in enumerate((rows, rows + 1, wide - 2, wide - 1)):
+                    line = 3 * rows + 4 * f + r
+                    state[f, row : row + 1, to] = source[j, line : line + 1, off : off + step]
+        local += size
+    for f in range(3):
+        state[f, rows + 2 : wide - 2, :] = jnp.zeros((TILE - 4, local), jnp.float32)
+
+    def taken(ref, lead):
+        return jnp.concatenate([cut(ref, lead, start, size) for start, size, _, _ in parts], axis=1)
+
     even = place[2] == 0
-    for f in range(3):
-        state[f, rows:, :] = jnp.zeros((TILE, cols), jnp.float32)
-        for source, half in ((mine, place[2]), (other, 1 - place[2])):
-            for j in range(pieces):
-                to = pl.ds(pl.multiple_of(half * (cols // 2) + j * width, LANES), width)
-                state[f, :rows, to] = source[j, f * rows : (f + 1) * rows, :]
-                for r, row in enumerate((rows, rows + 1, wide - 2, wide - 1)):
-                    at = 3 * rows + 4 * f + r
-                    state[f, row : row + 1, to] = source[j, at : at + 1, :]
-    step_depth = DT * depth_ref[...]
+    step_depth = DT * taken(depth_ref, ())
     carried = tuple(state[f] for f in range(3))
+    moved = stepped(carried, step_depth)
     for fetch in fetches:
         fetch.wait()
-    after = tuple(
-        jnp.where(even, b_own[f], b_lent[f]) + x for f, x in enumerate(stepped(carried, step_depth))
-    )
+    after = tuple(jnp.where(even, b_own[f], taken(b_lent, (f,))) + x for f, x in enumerate(moved))
     last = stepped(after, step_depth)
     copies = []
     for f in range(3):
@@ -393,22 +480,31 @@
         made[1, f] = 0.5 * ((begin + end) - v_ref[f])
         made[2, f] = end
         for part in range(3):
-            copy = pltpu.make_async_copy(made.at[part, f], out.at[part, f], sems.at[3 * f + part])
-            copy.start()
-            copies.append(copy)
+            for i, (lo, size, to) in enumerate(pieces):
+                copy = pltpu.make_async_copy(
+                    made.at[part, f, :, lo : lo + size],
+                    out.at[part, f, :, at(to, size)],
+                    sems.at[6 + (3 * f + part) * 3 + i],
+                )
+                copy.start()
+                copies.append(copy)
     for copy in copies:
         copy.wait()
 
 
-def kernel(body, shapes, *args, scalars=0, far=(), far_out=(), **more):
+def kernel(body, shapes, *args, scalars=0, far=(), far_out=(), near=(), near_out=(), **more):
     vmem = pl.BlockSpec(memory_space=pltpu.VMEM)
     hbm = pl.BlockSpec(memory_space=pltpu.HBM)
     smem = pl.BlockSpec(memory_space=pltpu.SMEM)
     many = isinstance(shapes, list)
-    outs = [
-        pltpu.HBM(shape, jnp.float32) if i in far_out else jax.ShapeDtypeStruct(shape, jnp.float32)
-        for i, shape in enumerate(shapes if many else [shapes])
-    ]
+    outs = []
+    for i, shape in enumerate(shapes if many else [shapes]):
+        make = pltpu.HBM if i in far_out else pltpu.VMEM if i in near_out else jax.ShapeDtypeStruct
+        outs.append(make(shape, jnp.float32))
+    placed = list(args)
+    for held, space in ((far, pltpu.HBM), (near, pltpu.VMEM)):
+        for i in held:
+            placed[i] = pltpu.with_memory_space_constraint(args[i], space)
     specs = [hbm if i in far_out else vmem for i in range(len(outs))]
     return pl.pallas_call(
         body,
@@ -417,14 +513,13 @@
         out_specs=specs if many else specs[0],
         compiler_params=pltpu.CompilerParams(vmem_limit_bytes=VMEM_BYTES),
         **more,
-    )(*[pltpu.with_memory_space_constraint(x, pltpu.HBM) if i in far else x for i, x in enumerate(args)])
+    )(*placed)
 
 
 def swap_rows(edges):
     count = lax.axis_size("space")
     if count == 2:
-        both = lax.ppermute(edges, "space", [(0, 1), (1, 0)])
-        return both[0], both[1]
+        return (lax.ppermute(edges, "space", [(0, 1), (1, 0)]),)
     below = lax.ppermute(edges[0], "space", [((i + 1) % count, i) for i in range(count)])
     above = lax.ppermute(edges[1], "space", [(i, (i + 1) % count) for i in range(count)])
     return below, above
@@ -451,14 +546,20 @@
     swapped = [(0, 1), (1, 0)]
     plan = (spaces, rows, width, reach)
 
-    prev = lax.ppermute(nodes[2], ("outer", "inner", "core"), [(i, i + 1) for i in range(slices - 1)])
+    last = kernel(last_body, state, nodes, far=(0,), scratch_shapes=[pltpu.SemaphoreType.DMA])
+    prev = lax.ppermute(last, ("outer", "inner", "core"), [(i, i + 1) for i in range(slices - 1)])
 
     if spaces == 2 and dense(width, reach, rows):
         own_rows = 4 * rows * span // LANES
         own, edges = kernel(
             functools.partial(prepare_body, width, reach),
             [(own_rows, LANES), (own_rows + 2 * DEEP * cols // LANES, LANES)],
-            place, mean_depth, init_state, scalars=1,
+            place, mean_depth, init_state, scalars=1, far=(1, 2),
+            scratch_shapes=[
+                pltpu.VMEM((rows, cols), jnp.float32),
+                pltpu.VMEM((2, 4, rows, width + 2 * LANES), jnp.float32),
+                pltpu.SemaphoreType.DMA((25,)),
+            ],
         )
         edges = lax.ppermute(edges, "space", swapped)
         windows, edges = (own, edges), (edges,)
@@ -468,15 +569,16 @@
         edges = jnp.stack([mean_depth[:DEEP, None], mean_depth[rows - DEEP :, None]])
         edges = swap_rows(edges)
 
-    base, fk = kernel(
-        blend_body, [state, spread], nodes, mean_depth, far=(0,),
+    base, fk, bare = kernel(
+        blend_body, [state, spread, (wide, cols)], nodes, mean_depth, far=(0, 1),
         scratch_shapes=[
             pltpu.VMEM(spread, jnp.float32),
             pltpu.VMEM((3,) + state, jnp.float32),
-            pltpu.SemaphoreType.DMA((3,)),
+            pltpu.VMEM((rows, cols), jnp.float32),
+            pltpu.SemaphoreType.DMA((4,)),
         ],
     )
-    ffk, depth = kernel(second_body, [spread, (wide, cols)], fk, mean_depth, *edges)
+    ffk, depth = kernel(second_body, [spread, (wide, cols)], fk, bare, *edges)
     fine_shapes = [(3 * wide, half + 2 * LANES), (3 * wide, half)]
     fine_args = (place, base, prev, init_state, fk, ffk, depth)
     give, v_give = kernel(functools.partial(fine_body, False), fine_shapes, *fine_args, scalars=1)
@@ -485,23 +587,33 @@
     tight = packed_rows(wide, width, reach)
     msg_shape = (owners, tight, LANES) if tight else (owners, 3 * wide, span)
     parts = (keep, give, v_keep, v_give)
-    msgs, *parts = kernel(
+    msgs, *far_parts = kernel(
         functools.partial(pair_body, width, reach, len(parts)), [msg_shape] + [x.shape for x in parts],
         place, depth, got, *parts, scalars=1, far_out=range(1 + len(parts)),
         scratch_shapes=[pltpu.VMEM(msg_shape, jnp.float32), pltpu.SemaphoreType.DMA((owners + len(parts),))],
     )
     recv = lax.all_to_all(msgs, group, 0, 0, tiled=True)
-    spill = kernel(spill_body, (2, 2, 18, 1, half), *parts)
-    low, high = swap_rows(spill)
+    spill = kernel(
+        spill_body, (2, 2, 18, 1, half), keep, give, *far_parts[2:], far=(2, 3),
+        scratch_shapes=[pltpu.VMEM((2, 3, TILE, half), jnp.float32), pltpu.SemaphoreType.DMA((6,))],
+    )
+    ahead = kernel(
+        functools.partial(ahead_body, inner, rows), (3, spaces * rows, span),
+        place, *windows, scalars=1,
+    )
+    spill = swap_rows(spill)
     b_own, vee = kernel(
-        mend_body, [spread, state], place, *parts, low, high, scalars=1, far_out=(1,),
-        scratch_shapes=[pltpu.VMEM(state, jnp.float32), pltpu.SemaphoreType.DMA],
+        mend_body, [spread, state], place, *far_parts, *spill, scalars=1,
+        far=range(1, 5), far_out=(1,),
+        scratch_shapes=[pltpu.VMEM(state, jnp.float32)]
+        + [pltpu.VMEM(x.shape, jnp.float32) for x in far_parts]
+        + [pltpu.SemaphoreType.DMA((5,))],
     )
     b_lent = lax.ppermute(b_own, "core", [(0, 1)])
 
     tight = packed_rows(spaces * rows, width, reach)
     total_shape = (tight, LANES) if tight else (3 * spaces * rows, span)
-    total = kernel(functools.partial(total_body, *plan), total_shape, place, recv, *windows, scalars=1)
+    total = kernel(functools.partial(total_body, *plan), total_shape, place, recv, ahead, *windows, scalars=1)
     carry = lax.ppermute(total, "outer", [(i, i + 1) for i in range(outer - 1)])
     back = kernel(
         functools.partial(chain_body, *plan), (owners, 3 * rows + 2 * TILE, width),
@@ -515,16 +627,26 @@
     if width % LANES:
         mine = mine.transpose(1, 0, 2).reshape(1, 3 * rows + 2 * TILE, half)
     other = lax.ppermute(mine, "core", swapped)
-    out = kernel(
-        finish_body, (3,) + state, place, mine, other, b_own, b_lent, vee, depth,
-        scalars=1, far=(3, 5), far_out=(0,),
-        scratch_shapes=[
-            pltpu.VMEM(spread, jnp.float32),
-            pltpu.VMEM((3,) + state, jnp.float32),
-            pltpu.VMEM(state, jnp.float32),
-            pltpu.VMEM(spread, jnp.float32),
-            pltpu.SemaphoreType.DMA((11,)),
-        ],
+
+    def finish(near, cols_held, *args, **more):
+        held = (3, wide, cols_held)
+        return kernel(
+            functools.partial(finish_body, near), (3,) + state,
+            place, *args, scalars=1, far_out=(0,),
+            scratch_shapes=[
+                pltpu.VMEM(held, jnp.float32),
+                pltpu.VMEM(held, jnp.float32),
+                pltpu.VMEM((3, rows, cols_held), jnp.float32),
+                pltpu.VMEM((3, 3, rows, cols_held), jnp.float32),
+                pltpu.SemaphoreType.DMA((33,)),
+            ],
+            **more,
+        )
+
+    out = finish(True, half, mine, b_own, b_lent, vee, depth, far=(2, 4))
+    out = finish(
+        False, half + 4 * LANES, mine, other, b_own, b_lent, vee, depth, out,
+        far=(3, 5, 7), input_output_aliases={7: 0},
     )
     return out[None]
 

time: 72.5 us -> 71.2 us (0.982)
  the two profiles are of different devices: /device:TPU:0 before, /device:TPU:17 now
where the time goes in v5:
time: 71.2 us; the launch traced here: 70.6 us
  Pallas kernels  30.9 us (43%)
  starting transfers between devices  24.3 us (34%)
  waiting for transfers between devices  15 us (21%)
    pallas_call x14, Pallas kernels, kernel(): pl.pallas_call(body, out_shape=outs if many else outs[0], in_specs=[smem...  30.9 us
    all_to_all x1, starting transfers between devices, per_device(): mine = lax.all_to_all(back, group, 0, 0, tiled=True)  6.69 us
    ppermute x1, waiting for transfers between devices, per_device(): carry = lax.ppermute(total, 'outer', [(i, i + 1) for i in range(outer - 1)])  5.12 us
    all_to_all x1, waiting for transfers between devices, per_device(): recv = lax.all_to_all(msgs, group, 0, 0, tiled=True)  4.68 us
    ppermute x1, starting transfers between devices, per_device(): lax.ppermute(last, ('outer', 'inner', 'core'), [(i, i + 1) for i in range...  3.68 us
    all_to_all x1, starting transfers between devices, per_device(): recv = lax.all_to_all(msgs, group, 0, 0, tiled=True)  3.57 us
    ppermute x1, starting transfers between devices, per_device(): other = lax.ppermute(mine, 'core', swapped)  3.01 us
    all_to_all x1, waiting for transfers between devices, per_device(): mine = lax.all_to_all(back, group, 0, 0, tiled=True)  2.7 us
  transfers between devices with their start and end apart: 9, of which 4 were waited for; matrix products, arithmetic and copies ran while one was open for 0% of the time, Pallas kernels for 30%

profile of v5, /device:TPU:17, one launch (start us, length us, event | category | flops | bytes accessed | tf_op | source)
XLA Modules:
  0.0 70.6 jit_solution(4422163447424146498)
XLA Ops:
  0.0 1.1 %shard_map.40 = f32[3,16,4096]{2,1,0:T(8,128)S(1)} custom-call(f32[3,3,16,4096]{3,2,1,0:T(8,128)} %bitcast.7), custom_call_target="tpu_custom_call" | custom-call | tf_op jit(solution)/shard_map/pallas_call | solution.py:509
  1.1 3.7 %collective-permute-start.1 = (f32[3,16,4096]{2,1,0:T(8,128)S(1)}, f32[3,16,4096]{2,1,0:T(8,128)S(1)}, u32[]{:S(2)}, u32[]{:S(2)}) collective-permute-start(f32[3,16,4096]{2,1,0:T(8,128)S(1)} %shard_map.40), channel_id=1, source_target_pairs={{0,2},{2,4},{4,6},{6,8},{8,10},{10,12},{12,14},{14,16},{16,18},{18... | collective-permute-start | bytes 2359304 | tf_op jit(solution)/shard_map/ppermute | solution.py:550
  4.8 0.1 stack.31.place
  4.9 1.9 %shard_map.38 = (f32[192,128]{1,0:T(8,128)S(1)}, f32[384,128]{1,0:T(8,128)S(1)}) custom-call(s32[5]{0:T(128)S(1)} %stack.31.place, f32[16,4096]{1,0:T(8,128)} %depth_far.3, f32[3,16,4096]{2,1,0:T(8,128)} %init.5), custom_call_target="tpu_custom_call" | custom-call | tf_op jit(solution)/shard_map/pallas_call | solution.py:509
  6.8 1.3 %collective-permute-start = (f32[384,128]{1,0:T(8,128)S(1)}, f32[384,128]{1,0:T(8,128)S(1)}, u32[]{:S(2)}, u32[]{:S(2)}) collective-permute-start(f32[384,128]{1,0:T(8,128)S(1)} %get-tuple-element.25), channel_id=1, source_target_pairs={{0,1},{1,0},{2,3},{3,2},{4,5},{5,4},{6,7},{7,6},{8,9},{9,8},{10,11... | collective-permute-start | bytes 589832 | tf_op jit(solution)/shard_map/ppermute | solution.py:564
  8.1 2.5 %shard_map.37 = (f32[3,16,4096]{2,1,0:T(8,128)S(1)}, f32[3,24,4096]{2,1,0:T(8,128)S(1)}, f32[24,4096]{1,0:T(8,128)S(1)}) custom-call(f32[3,3,16,4096]{3,2,1,0:T(8,128)} %bitcast.8, f32[16,4096]{1,0:T(8,128)} %depth_far.3), custom_call_target="tpu_custom_call" | custom-call | tf_op jit(solution)/shard_map/pallas_call | solution.py:509
  10.6 0.0 copy-start
  10.6 2.5 %collective-permute-done.rest_0_.rest_1_ = f32[384,128]{1,0:T(8,128)S(1)} collective-permute-done((f32[384,128]{1,0:T(8,128)S(1)}, f32[384,128]{1,0:T(8,128)S(1)}, u32[]{:S(2)}, u32[]{:S(2)}) %collective-permute-start) | collective-permute-done | bytes 196640 | tf_op jit(solution)/shard_map/ppermute | solution.py:564
  13.1 1.2 %shard_map.39 = (f32[3,24,4096]{2,1,0:T(8,128)S(1)}, f32[24,4096]{1,0:T(8,128)S(1)}) custom-call(f32[3,24,4096]{2,1,0:T(8,128)S(1)} %get-tuple-element.23.fk, f32[24,4096]{1,0:T(8,128)S(1)} %get-tuple-element.24.bare, f32[384,128]{1,0:T(8,128)S(1)} %collective-permute-done.rest_0_.rest_1_), custom_call_target="tpu_custom_call" | custom-call | tf_op jit(solution)/shard_map/pallas_call | solution.py:509
  14.3 0.0 collective-permute-done.1.prev
  14.4 0.0 copy-done
  14.4 2.3 %shard_map.41 = (f32[72,2304]{1,0:T(8,128)S(1)}, f32[72,2048]{1,0:T(8,128)S(1)}) custom-call(s32[5]{0:T(128)S(1)} %stack.31.place, f32[3,16,4096]{2,1,0:T(8,128)S(1)} %get-tuple-element.27.base, f32[3,16,4096]{2,1,0:T(8,128)S(1)} %collective-permute-done.1.prev, f32[3,16,4096]{2,1,0:T(8,128)S(1)} %copy-done, f32[3,24,4096]{2,1,0:T(8,128)S(1)} %get-tuple-element.23.fk, ...), custom_call_target="tpu_custom_call" | custom-call | tf_op jit(solution)/shard_map/pallas_call | solution.py:509
  16.6 1.7 %collective-permute-start.2 = (f32[72,2304]{1,0:T(8,128)S(1)}, f32[72,2304]{1,0:T(8,128)S(1)}, u32[]{:S(2)}, u32[]{:S(2)}) collective-permute-start(f32[72,2304]{1,0:T(8,128)S(1)} %get-tuple-element.29.rest_1_.b_give), channel_id=1, source_target_pairs={{0,2},{2,0},{1,3},{3,1},{4,6},{6,4},{5,7},{7,5},{8,10},{10,8},{9,1... | collective-permute-start | bytes 1990664 | tf_op jit(solution)/shard_map/ppermute | solution.py:585
  18.4 2.3 %shard_map.42 = (f32[72,2304]{1,0:T(8,128)S(1)}, f32[72,2048]{1,0:T(8,128)S(1)}) custom-call(s32[5]{0:T(128)S(1)} %stack.31.place, f32[3,16,4096]{2,1,0:T(8,128)S(1)} %get-tuple-element.27.base, f32[3,16,4096]{2,1,0:T(8,128)S(1)} %collective-permute-done.1.prev, f32[3,16,4096]{2,1,0:T(8,128)S(1)} %copy-done, f32[3,24,4096]{2,1,0:T(8,128)S(1)} %get-tuple-element.23.fk, ...), custom_call_target="tpu_custom_call" | custom-call | tf_op jit(solution)/shard_map/pallas_call | solution.py:509
  20.6 0.0 collective-permute-done.2.got
  20.7 2.8 %shard_map.43 = (f32[8,168,128]{2,1,0:T(8,128)}, f32[72,2304]{1,0:T(8,128)}, f32[72,2304]{1,0:T(8,128)}, f32[72,2048]{1,0:T(8,128)}, f32[72,2048]{1,0:T(8,128)}) custom-call(s32[5]{0:T(128)S(1)} %stack.31.place, f32[24,4096]{1,0:T(8,128)S(1)} %get-tuple-element.26.depth_ref.refs_4_.refs_5_, f32[72,2304]{1,0:T(8,128)S(1)} %collective-permute-done.2.got, ...), custom_call_target="tpu_custom_call" | custom-call | tf_op jit(solution)/shard_map/pallas_call | solution.py:509
  23.5 3.6 %all-to-all-start = ((f32[8,168,128]{2,1,0:T(8,128)}), f32[8,168,128]{2,1,0:T(8,128)S(1)}, u32[]{:S(2)}, u32[]{:S(2)}) async-start(f32[8,168,128]{2,1,0:T(8,128)} %get-tuple-element.33), calls=%async_computation | async-start | bytes 1376256 | tf_op jit(solution)/shard_map/all_to_all | solution.py:595
  27.1 1.9 %shard_map.47 = f32[2,2,18,1,2048]{4,3,2,1,0:T(1,128)} custom-call(f32[72,2304]{1,0:T(8,128)S(1)} %get-tuple-element.30.rest_0_.b_keep, f32[72,2304]{1,0:T(8,128)S(1)} %get-tuple-element.29.rest_1_.b_give, f32[72,2048]{1,0:T(8,128)} %get-tuple-element.37.v_keep.refs_2_, f32[72,2048]{1,0:T(8,128)} %get-tuple-element.38.v_give.refs_3_), custom_call_target="tpu_custom_call" | custom-call | tf_op jit(solution)/shard_map/pallas_call | solution.py:509
  29.0 1.5 %collective-permute-start.5 = (f32[2,2,18,1,2048]{4,3,2,1,0:T(1,128)}, f32[2,2,18,1,2048]{4,3,2,1,0:T(1,128)S(1)}, u32[]{:S(2)}, u32[]{:S(2)}) collective-permute-start(f32[2,2,18,1,2048]{4,3,2,1,0:T(1,128)} %shard_map.47), channel_id=1, source_target_pairs={{0,1},{1,0},{2,3},{3,2},{4,5},{5,4},{6,7},{7,6},{8,9},{9,8},{10,11... | collective-permute-start | bytes 1769480 | tf_op jit(solution)/shard_map/ppermute | solution.py:522
  30.5 1.6 %shard_map.44.ahead = f32[3,32,384]{2,1,0:T(8,128)S(1)} custom-call(s32[5]{0:T(128)S(1)} %stack.31.place, f32[192,128]{1,0:T(8,128)S(1)} %get-tuple-element.34.rest_0_, f32[384,128]{1,0:T(8,128)S(1)} %collective-permute-done.rest_0_.rest_1_), custom_call_target="tpu_custom_call" | custom-call | tf_op jit(solution)/shard_map/pallas_call | solution.py:509
  32.1 4.7 %all-to-all-done.recv = f32[8,168,128]{2,1,0:T(8,128)S(1)} async-done(((f32[8,168,128]{2,1,0:T(8,128)}), f32[8,168,128]{2,1,0:T(8,128)S(1)}, u32[]{:S(2)}, u32[]{:S(2)}) %all-to-all-start) | async-done | bytes 688160 | tf_op jit(solution)/shard_map/all_to_all | solution.py:595
  36.8 1.4 %shard_map.45 = f32[216,128]{1,0:T(8,128)S(1)} custom-call(s32[5]{0:T(128)S(1)} %stack.31.place, f32[8,168,128]{2,1,0:T(8,128)S(1)} %all-to-all-done.recv, f32[3,32,384]{2,1,0:T(8,128)S(1)} %shard_map.44.ahead, f32[192,128]{1,0:T(8,128)S(1)} %get-tuple-element.34.rest_0_, f32[384,128]{1,0:T(8,128)S(1)} %collective-permute-done.rest_0_.rest_1_), custom_call_target="tpu_custom_call" | custom-call | tf_op jit(solution)/shard_map/pallas_call | solution.py:509
  38.3 1.3 %collective-permute-start.3 = (f32[216,128]{1,0:T(8,128)S(1)}, f32[216,128]{1,0:T(8,128)S(1)}, u32[]{:S(2)}, u32[]{:S(2)}) collective-permute-start(f32[216,128]{1,0:T(8,128)S(1)} %shard_map.45), channel_id=1, source_target_pairs={{0,16},{1,17},{2,18},{3,19},{4,20},{5,21},{6,22},{7,23},{8,24},{9,... | collective-permute-start | bytes 331784 | tf_op jit(solution)/shard_map/ppermute | solution.py:617
  39.6 5.1 %collective-permute-done.3.carry = f32[216,128]{1,0:T(8,128)S(1)} collective-permute-done((f32[216,128]{1,0:T(8,128)S(1)}, f32[216,128]{1,0:T(8,128)S(1)}, u32[]{:S(2)}, u32[]{:S(2)}) %collective-permute-start.3) | collective-permute-done | bytes 110624 | tf_op jit(solution)/shard_map/ppermute | solution.py:617
  44.7 2.1 %shard_map.46 = f32[8,64,256]{2,1,0:T(8,128)} custom-call(s32[5]{0:T(128)S(1)} %stack.31.place, f32[8,168,128]{2,1,0:T(8,128)S(1)} %all-to-all-done.recv, f32[216,128]{1,0:T(8,128)S(1)} %collective-permute-done.3.carry, f32[192,128]{1,0:T(8,128)S(1)} %get-tuple-element.34.rest_0_, f32[384,128]{1,0:T(8,128)S(1)} %collective-permute-done.rest_0_.rest_1_), custom_call_target="tpu_custom_call" | custom-call | tf_op jit(solution)/shard_map/pallas_call | solution.py:509
  46.8 6.7 %all-to-all-start.1 = ((f32[8,64,256]{2,1,0:T(8,128)}), f32[8,64,256]{2,1,0:T(8,128)S(1)}, u32[]{:S(2)}, u32[]{:S(2)}) async-start(f32[8,64,256]{2,1,0:T(8,128)} %shard_map.46), calls=%async_computation.1 | async-start | bytes 1048576 | tf_op jit(solution)/shard_map/all_to_all | solution.py:626
  53.5 0.0 collective-permute-done.5.refs_4_
  53.5 2.8 %shard_map.48 = (f32[3,24,4096]{2,1,0:T(8,128)S(1)}, f32[3,16,4096]{2,1,0:T(8,128)}) custom-call(s32[5]{0:T(128)S(1)} %stack.31.place, f32[72,2304]{1,0:T(8,128)} %get-tuple-element.35.refs_0_, f32[72,2304]{1,0:T(8,128)} %get-tuple-element.36.refs_1_, f32[72,2048]{1,0:T(8,128)} %get-tuple-element.37.v_keep.refs_2_, ...), custom_call_target="tpu_custom_call" | custom-call | tf_op jit(solution)/shard_map/pallas_call | solution.py:509
  56.3 0.0 copy-start.1
  56.4 1.5 %collective-permute-start.6 = (f32[3,24,4096]{2,1,0:T(8,128)S(1)}, f32[3,24,4096]{2,1,0:T(8,128)S(1)}, u32[]{:S(2)}, u32[]{:S(2)}) collective-permute-start(f32[3,24,4096]{2,1,0:T(8,128)S(1)} %get-tuple-element.39.refs_1_.refs_2_), channel_id=1, source_target_pairs={{0,2},{1,3},{4,6},{5,7},{8,10},{9,11},{12,14},{13,15},{16,18},{17,... | collective-permute-start | bytes 3538952 | tf_op jit(solution)/shard_map/ppermute | solution.py:612
  57.8 2.7 %all-to-all-done.1.refs_0_ = f32[8,64,256]{2,1,0:T(8,128)S(1)} async-done(((f32[8,64,256]{2,1,0:T(8,128)}), f32[8,64,256]{2,1,0:T(8,128)S(1)}, u32[]{:S(2)}, u32[]{:S(2)}) %all-to-all-start.1) | async-done | bytes 524320 | tf_op jit(solution)/shard_map/all_to_all | solution.py:626
  60.5 3.0 %collective-permute-start.4 = (f32[8,64,256]{2,1,0:T(8,128)S(1)}, f32[8,64,256]{2,1,0:T(8,128)S(1)}, u32[]{:S(2)}, u32[]{:S(2)}) collective-permute-start(f32[8,64,256]{2,1,0:T(8,128)S(1)} %all-to-all-done.1.refs_0_), channel_id=1, source_target_pairs={{0,2},{2,0},{1,3},{3,1},{4,6},{6,4},{5,7},{7,5},{8,10},{10,8},{9,1... | collective-permute-start | bytes 1572872 | tf_op jit(solution)/shard_map/ppermute | solution.py:629
  63.5 0.0 collective-permute-done.6.refs_2_.refs_3_
  63.5 0.0 copy-done.1
  63.5 3.2 %shard_map.49.refs_6_ = f32[3,3,16,4096]{3,2,1,0:T(8,128)} custom-call(s32[5]{0:T(128)S(1)} %stack.31.place, f32[8,64,256]{2,1,0:T(8,128)S(1)} %all-to-all-done.1.refs_0_, f32[3,24,4096]{2,1,0:T(8,128)} %copy-done.1, f32[3,24,4096]{2,1,0:T(8,128)S(1)} %collective-permute-done.6.refs_2_.refs_3_, f32[3,16,4096]{2,1,0:T(8,128)} %get-tuple-element.40.refs_3_.refs_4_, ...), custom_call_target="tpu_custom_call" | custom-call | tf_op jit(solution)/shard_map/pallas_call | solution.py:509
  66.8 0.0 collective-permute-done.4.refs_1_
  66.8 3.7 %shard_map.50 = f32[3,3,16,4096]{3,2,1,0:T(8,128)} custom-call(s32[5]{0:T(128)S(1)} %stack.31.place, f32[8,64,256]{2,1,0:T(8,128)S(1)} %all-to-all-done.1.refs_0_, f32[8,64,256]{2,1,0:T(8,128)S(1)} %collective-permute-done.4.refs_1_, f32[3,24,4096]{2,1,0:T(8,128)} %copy-done.1, ...), custom_call_target="tpu_custom_call", output_to_operand_aliasing={{}: (7, {})} | custom-call | tf_op jit(solution)/shard_map/pallas_call | solution.py:509
Async XLA Ops:
  1.1 13.2 %collective-permute-start.1 = (f32[3,16,4096]{2,1,0:T(8,128)S(1)}, f32[3,16,4096]{2,1,0:T(8,128)S(1)}, u32[]{:S(2)}, u32[]{:S(2)}) collective-permute-start(f32[3,16,4096]{2,1,0:T(8,128)S(1)} %shard_map.40), channel_id=1, source_target_pairs={{0,2},{2,4},{4,6},{6,8},{8,10},{10,12},{12,14},{14,16},{16,18},{18... | collective-permute-start | bytes 2359304 | tf_op jit(solution)/shard_map/ppermute | solution.py:550
  6.8 6.3 %collective-permute-start = (f32[384,128]{1,0:T(8,128)S(1)}, f32[384,128]{1,0:T(8,128)S(1)}, u32[]{:S(2)}, u32[]{:S(2)}) collective-permute-start(f32[384,128]{1,0:T(8,128)S(1)} %get-tuple-element.25), channel_id=1, source_target_pairs={{0,1},{1,0},{2,3},{3,2},{4,5},{5,4},{6,7},{7,6},{8,9},{9,8},{10,11... | collective-permute-start | bytes 589832 | tf_op jit(solution)/shard_map/ppermute | solution.py:564
  10.6 3.8 %copy-start = (f32[3,16,4096]{2,1,0:T(8,128)S(1)}, f32[3,16,4096]{2,1,0:T(8,128)}, u32[]{:S(2)}) copy-start(f32[3,16,4096]{2,1,0:T(8,128)} %init.5) | copy-start | bytes 2359300
  16.6 4.0 %collective-permute-start.2 = (f32[72,2304]{1,0:T(8,128)S(1)}, f32[72,2304]{1,0:T(8,128)S(1)}, u32[]{:S(2)}, u32[]{:S(2)}) collective-permute-start(f32[72,2304]{1,0:T(8,128)S(1)} %get-tuple-element.29.rest_1_.b_give), channel_id=1, source_target_pairs={{0,2},{2,0},{1,3},{3,1},{4,6},{6,4},{5,7},{7,5},{8,10},{10,8},{9,1... | collective-permute-start | bytes 1990664 | tf_op jit(solution)/shard_map/ppermute | solution.py:585
  23.5 13.3 %all-to-all-start = ((f32[8,168,128]{2,1,0:T(8,128)}), f32[8,168,128]{2,1,0:T(8,128)S(1)}, u32[]{:S(2)}, u32[]{:S(2)}) async-start(f32[8,168,128]{2,1,0:T(8,128)} %get-tuple-element.33), calls=%async_computation | async-start | bytes 1376256 | tf_op jit(solution)/shard_map/all_to_all | solution.py:595
  29.0 24.5 %collective-permute-start.5 = (f32[2,2,18,1,2048]{4,3,2,1,0:T(1,128)}, f32[2,2,18,1,2048]{4,3,2,1,0:T(1,128)S(1)}, u32[]{:S(2)}, u32[]{:S(2)}) collective-permute-start(f32[2,2,18,1,2048]{4,3,2,1,0:T(1,128)} %shard_map.47), channel_id=1, source_target_pairs={{0,1},{1,0},{2,3},{3,2},{4,5},{5,4},{6,7},{7,6},{8,9},{9,8},{10,11... | collective-permute-start | bytes 1769480 | tf_op jit(solution)/shard_map/ppermute | solution.py:522
  38.3 6.4 %collective-permute-start.3 = (f32[216,128]{1,0:T(8,128)S(1)}, f32[216,128]{1,0:T(8,128)S(1)}, u32[]{:S(2)}, u32[]{:S(2)}) collective-permute-start(f32[216,128]{1,0:T(8,128)S(1)} %shard_map.45), channel_id=1, source_target_pairs={{0,16},{1,17},{2,18},{3,19},{4,20},{5,21},{6,22},{7,23},{8,24},{9,... | collective-permute-start | bytes 331784 | tf_op jit(solution)/shard_map/ppermute | solution.py:617
  46.8 13.7 %all-to-all-start.1 = ((f32[8,64,256]{2,1,0:T(8,128)}), f32[8,64,256]{2,1,0:T(8,128)S(1)}, u32[]{:S(2)}, u32[]{:S(2)}) async-start(f32[8,64,256]{2,1,0:T(8,128)} %shard_map.46), calls=%async_computation.1 | async-start | bytes 1048576 | tf_op jit(solution)/shard_map/all_to_all | solution.py:626
  56.3 7.2 %copy-start.1 = (f32[3,24,4096]{2,1,0:T(8,128)}, f32[3,24,4096]{2,1,0:T(8,128)S(1)}, u32[]{:S(2)}) copy-start(f32[3,24,4096]{2,1,0:T(8,128)S(1)} %get-tuple-element.39.refs_1_.refs_2_) | copy-start | bytes 3538948
  56.4 7.2 %collective-permute-start.6 = (f32[3,24,4096]{2,1,0:T(8,128)S(1)}, f32[3,24,4096]{2,1,0:T(8,128)S(1)}, u32[]{:S(2)}, u32[]{:S(2)}) collective-permute-start(f32[3,24,4096]{2,1,0:T(8,128)S(1)} %get-tuple-element.39.refs_1_.refs_2_), channel_id=1, source_target_pairs={{0,2},{1,3},{4,6},{5,7},{8,10},{9,11},{12,14},{13,15},{16,18},{17,... | collective-permute-start | bytes 3538952 | tf_op jit(solution)/shard_map/ppermute | solution.py:612
  60.5 6.3 %collective-permute-start.4 = (f32[8,64,256]{2,1,0:T(8,128)S(1)}, f32[8,64,256]{2,1,0:T(8,128)S(1)}, u32[]{:S(2)}, u32[]{:S(2)}) collective-permute-start(f32[8,64,256]{2,1,0:T(8,128)S(1)} %all-to-all-done.1.refs_0_), channel_id=1, source_target_pairs={{0,2},{2,0},{1,3},{3,1},{4,6},{6,4},{5,7},{7,5},{8,10},{10,8},{9,1... | collective-permute-start | bytes 1572872 | tf_op jit(solution)/shard_map/ppermute | solution.py:629

commit v6 on v5

--- a/solution.py
+++ b/solution.py
@@ -71,10 +71,24 @@
     return ref[lead + (slice(None), pl.ds(pl.multiple_of(at, LANES), size))]
 
 
-def last_body(nodes, out, sem):
-    copy = pltpu.make_async_copy(nodes.at[2], out, sem)
-    copy.start()
-    copy.wait()
+def last_body(place, nodes, soon_out, late_out, sems):
+    cols = nodes.shape[-1]
+    half = cols // 2
+    start = place[2] * half
+    before, after = lax.rem(start + (cols - LANES), cols), lax.rem(start + half, cols)
+    cuts = (
+        (before, LANES, soon_out, 0),
+        (start, half, soon_out, LANES),
+        (after, LANES, soon_out, LANES + half),
+        (after, half, late_out, 0),
+    )
+    copies = []
+    for i, (at, size, out, to) in enumerate(cuts):
+        source = nodes.at[2, :, :, pl.ds(pl.multiple_of(at, LANES), size)]
+        copies.append(pltpu.make_async_copy(source, out.at[:, :, to : to + size], sems.at[i]))
+        copies[-1].start()
+    for copy in copies:
+        copy.wait()
 
 
 def prepare_body(width, reach, place, depth_far, init, own_out, edge_out, depth, held, sems):
@@ -165,7 +179,8 @@
     return jnp.concatenate(parts, axis=1)
 
 
-def fine_body(own_half, place, base, prev, init, fk, ffk, depth_ref, b_out, v_out):
+def fine_body(own_half, place, base, init, fk, ffk, depth_ref, prev, *rest):
+    *late, b_out, v_out = rest
     half = place[2] if own_half else 1 - place[2]
     first = place[0] == 1
     wide = fk.shape[1]
@@ -173,7 +188,11 @@
     none = jnp.zeros((TILE, half_depth.shape[1]), jnp.float32)
     g = []
     for f in range(3):
-        start = jnp.where(first, window(init, (f,), half), window(prev, (f,), half))
+        before = prev[f]
+        if own_half:
+            size = late[0].shape[2]
+            before = jnp.concatenate([before[:, size : size + LANES], late[0][f], before[:, LANES : 2 * LANES]], axis=1)
+        start = jnp.where(first, window(init, (f,), half), before)
         g.append(jnp.concatenate([HALF * start + window(base, (f,), half), none], axis=0))
     u = tendency(tendency(tuple(g), half_depth), half_depth)
     fu = tendency(u, half_depth)
@@ -546,8 +565,13 @@
     swapped = [(0, 1), (1, 0)]
     plan = (spaces, rows, width, reach)
 
-    last = kernel(last_body, state, nodes, far=(0,), scratch_shapes=[pltpu.SemaphoreType.DMA])
-    prev = lax.ppermute(last, ("outer", "inner", "core"), [(i, i + 1) for i in range(slices - 1)])
+    soon, late = kernel(
+        last_body, [(3, rows, half + 2 * LANES), (3, rows, half)], place, nodes, scalars=1, far=(1,),
+        scratch_shapes=[pltpu.SemaphoreType.DMA((4,))],
+    )
+    onward = [(i, i + 1) for i in range(slices - 1)]
+    prev = lax.ppermute(soon, ("outer", "inner", "core"), onward)
+    prev_late = lax.ppermute(late, ("outer", "inner", "core"), onward)
 
     if spaces == 2 and dense(width, reach, rows):
         own_rows = 4 * rows * span // LANES
@@ -580,10 +604,10 @@
     )
     ffk, depth = kernel(second_body, [spread, (wide, cols)], fk, bare, *edges)
     fine_shapes = [(3 * wide, half + 2 * LANES), (3 * wide, half)]
-    fine_args = (place, base, prev, init_state, fk, ffk, depth)
+    fine_args = (place, base, init_state, fk, ffk, depth, prev)
     give, v_give = kernel(functools.partial(fine_body, False), fine_shapes, *fine_args, scalars=1)
     got = lax.ppermute(give, "core", swapped)
-    keep, v_keep = kernel(functools.partial(fine_body, True), fine_shapes, *fine_args, scalars=1)
+    keep, v_keep = kernel(functools.partial(fine_body, True), fine_shapes, *fine_args, prev_late, scalars=1)
     tight = packed_rows(wide, width, reach)
     msg_shape = (owners, tight, LANES) if tight else (owners, 3 * wide, span)
     parts = (keep, give, v_keep, v_give)

time: 71.2 us -> 76.8 us (1.079)
  the two profiles are of different devices: /device:TPU:17 before, /device:TPU:1 now
where the time goes in v6:
time: 76.8 us; the launch traced here: 76.2 us
  Pallas kernels  31.4 us (41%)
  starting transfers between devices  30.2 us (39%)
  waiting for transfers between devices  14.2 us (18%)
    pallas_call x14, Pallas kernels, kernel(): pl.pallas_call(body, out_shape=outs if many else outs[0], in_specs=[smem...  31.4 us
    ppermute x1, starting transfers between devices, per_device(): other = lax.ppermute(mine, 'core', swapped)  6.63 us
    ppermute x1, waiting for transfers between devices, per_device(): prev_late = lax.ppermute(late, ('outer', 'inner', 'core'), onward)  4.7 us
    all_to_all x1, starting transfers between devices, per_device(): recv = lax.all_to_all(msgs, group, 0, 0, tiled=True)  4.51 us
    ppermute x1, starting transfers between devices, per_device(): prev = lax.ppermute(soon, ('outer', 'inner', 'core'), onward)  4.5 us
    all_to_all x1, starting transfers between devices, per_device(): mine = lax.all_to_all(back, group, 0, 0, tiled=True)  4.18 us
    ppermute x1, starting transfers between devices, per_device(): prev_late = lax.ppermute(late, ('outer', 'inner', 'core'), onward)  4.16 us
    all_to_all x1, waiting for transfers between devices, per_device(): recv = lax.all_to_all(msgs, group, 0, 0, tiled=True)  3.93 us
  transfers between devices with their start and end apart: 10, of which 6 were waited for; matrix products, arithmetic and copies ran while one was open for 0% of the time, Pallas kernels for 27%

profile of v6, /device:TPU:1, one launch (start us, length us, event | category | flops | bytes accessed | tf_op | source)
XLA Modules:
  0.0 76.2 jit_solution(979966837374765571)
XLA Ops:
  0.0 0.1 stack.31.place
  0.1 1.7 %shard_map.40 = (f32[3,16,2304]{2,1,0:T(8,128)S(1)}, f32[3,16,2048]{2,1,0:T(8,128)S(1)}) custom-call(s32[5]{0:T(128)S(1)} %stack.31.place, f32[3,3,16,4096]{3,2,1,0:T(8,128)} %bitcast.7), custom_call_target="tpu_custom_call" | custom-call | tf_op jit(solution)/shard_map/pallas_call | solution.py:528
  1.8 4.5 %collective-permute-start.1 = (f32[3,16,2304]{2,1,0:T(8,128)S(1)}, f32[3,16,2304]{2,1,0:T(8,128)S(1)}, u32[]{:S(2)}, u32[]{:S(2)}) collective-permute-start(f32[3,16,2304]{2,1,0:T(8,128)S(1)} %get-tuple-element.31), channel_id=1, source_target_pairs={{0,2},{2,4},{4,6},{6,8},{8,10},{10,12},{12,14},{14,16},{16,18},{18... | collective-permute-start | bytes 1327112 | tf_op jit(solution)/shard_map/ppermute | solution.py:573
  6.3 1.9 %shard_map.38 = (f32[192,128]{1,0:T(8,128)S(1)}, f32[384,128]{1,0:T(8,128)S(1)}) custom-call(s32[5]{0:T(128)S(1)} %stack.31.place, f32[16,4096]{1,0:T(8,128)} %depth_far.3, f32[3,16,4096]{2,1,0:T(8,128)} %init.5), custom_call_target="tpu_custom_call" | custom-call | tf_op jit(solution)/shard_map/pallas_call | solution.py:528
  8.2 1.3 %collective-permute-start = (f32[384,128]{1,0:T(8,128)S(1)}, f32[384,128]{1,0:T(8,128)S(1)}, u32[]{:S(2)}, u32[]{:S(2)}) collective-permute-start(f32[384,128]{1,0:T(8,128)S(1)} %get-tuple-element.27), channel_id=1, source_target_pairs={{0,1},{1,0},{2,3},{3,2},{4,5},{5,4},{6,7},{7,6},{8,9},{9,8},{10,11... | collective-permute-start | bytes 589832 | tf_op jit(solution)/shard_map/ppermute | solution.py:588
  9.5 2.5 %shard_map.37 = (f32[3,16,4096]{2,1,0:T(8,128)S(1)}, f32[3,24,4096]{2,1,0:T(8,128)S(1)}, f32[24,4096]{1,0:T(8,128)S(1)}) custom-call(f32[3,3,16,4096]{3,2,1,0:T(8,128)} %bitcast.8, f32[16,4096]{1,0:T(8,128)} %depth_far.3), custom_call_target="tpu_custom_call" | custom-call | tf_op jit(solution)/shard_map/pallas_call | solution.py:528
  12.0 0.0 copy-start
  12.0 1.6 %collective-permute-done.rest_0_.rest_1_ = f32[384,128]{1,0:T(8,128)S(1)} collective-permute-done((f32[384,128]{1,0:T(8,128)S(1)}, f32[384,128]{1,0:T(8,128)S(1)}, u32[]{:S(2)}, u32[]{:S(2)}) %collective-permute-start) | collective-permute-done | bytes 196640 | tf_op jit(solution)/shard_map/ppermute | solution.py:588
  13.6 1.2 %shard_map.39 = (f32[3,24,4096]{2,1,0:T(8,128)S(1)}, f32[24,4096]{1,0:T(8,128)S(1)}) custom-call(f32[3,24,4096]{2,1,0:T(8,128)S(1)} %get-tuple-element.25.fk, f32[24,4096]{1,0:T(8,128)S(1)} %get-tuple-element.26.bare, f32[384,128]{1,0:T(8,128)S(1)} %collective-permute-done.rest_0_.rest_1_), custom_call_target="tpu_custom_call" | custom-call | tf_op jit(solution)/shard_map/pallas_call | solution.py:528
  14.8 0.0 collective-permute-done.1.prev
  14.8 0.0 copy-done
  14.8 2.3 %shard_map.41 = (f32[72,2304]{1,0:T(8,128)S(1)}, f32[72,2048]{1,0:T(8,128)S(1)}) custom-call(s32[5]{0:T(128)S(1)} %stack.31.place, f32[3,16,4096]{2,1,0:T(8,128)S(1)} %get-tuple-element.29.base, f32[3,16,4096]{2,1,0:T(8,128)S(1)} %copy-done, f32[3,24,4096]{2,1,0:T(8,128)S(1)} %get-tuple-element.25.fk, f32[3,24,4096]{2,1,0:T(8,128)S(1)} %get-tuple-element.30.ffk, ...), custom_call_target="tpu_custom_call" | custom-call | tf_op jit(solution)/shard_map/pallas_call | solution.py:528
  17.1 0.1 collective-permute-start.2
  17.1 4.2 %collective-permute-start.3 = (f32[3,16,2048]{2,1,0:T(8,128)S(1)}, f32[3,16,2048]{2,1,0:T(8,128)S(1)}, u32[]{:S(2)}, u32[]{:S(2)}) collective-permute-start(f32[3,16,2048]{2,1,0:T(8,128)S(1)} %get-tuple-element.33), channel_id=1, source_target_pairs={{0,2},{2,4},{4,6},{6,8},{8,10},{10,12},{12,14},{14,16},{16,18},{18... | collective-permute-start | bytes 1179656 | tf_op jit(solution)/shard_map/ppermute | solution.py:574
  21.3 4.7 %collective-permute-done.3.rest_0_ = f32[3,16,2048]{2,1,0:T(8,128)S(1)} collective-permute-done((f32[3,16,2048]{2,1,0:T(8,128)S(1)}, f32[3,16,2048]{2,1,0:T(8,128)S(1)}, u32[]{:S(2)}, u32[]{:S(2)}) %collective-permute-start.3) | collective-permute-done | bytes 393248 | tf_op jit(solution)/shard_map/ppermute | solution.py:574
  26.0 2.2 %shard_map.42 = (f32[72,2304]{1,0:T(8,128)S(1)}, f32[72,2048]{1,0:T(8,128)S(1)}) custom-call(s32[5]{0:T(128)S(1)} %stack.31.place, f32[3,16,4096]{2,1,0:T(8,128)S(1)} %get-tuple-element.29.base, f32[3,16,4096]{2,1,0:T(8,128)S(1)} %copy-done, f32[3,24,4096]{2,1,0:T(8,128)S(1)} %get-tuple-element.25.fk, f32[3,24,4096]{2,1,0:T(8,128)S(1)} %get-tuple-element.30.ffk, ...), custom_call_target="tpu_custom_call" | custom-call | tf_op jit(solution)/shard_map/pallas_call | solution.py:528
  28.3 0.0 collective-permute-done.2.got
  28.3 2.8 %shard_map.43 = (f32[8,168,128]{2,1,0:T(8,128)}, f32[72,2304]{1,0:T(8,128)}, f32[72,2304]{1,0:T(8,128)}, f32[72,2048]{1,0:T(8,128)}, f32[72,2048]{1,0:T(8,128)}) custom-call(s32[5]{0:T(128)S(1)} %stack.31.place, f32[24,4096]{1,0:T(8,128)S(1)} %get-tuple-element.28.depth_ref.refs_4_.refs_5_, f32[72,2304]{1,0:T(8,128)S(1)} %collective-permute-done.2.got, ...), custom_call_target="tpu_custom_call" | custom-call | tf_op jit(solution)/shard_map/pallas_call | solution.py:528
  31.1 4.5 %all-to-all-start = ((f32[8,168,128]{2,1,0:T(8,128)}), f32[8,168,128]{2,1,0:T(8,128)S(1)}, u32[]{:S(2)}, u32[]{:S(2)}) async-start(f32[8,168,128]{2,1,0:T(8,128)} %get-tuple-element.37), calls=%async_computation | async-start | bytes 1376256 | tf_op jit(solution)/shard_map/all_to_all | solution.py:619
  35.6 1.9 %shard_map.47 = f32[2,2,18,1,2048]{4,3,2,1,0:T(1,128)} custom-call(f32[72,2304]{1,0:T(8,128)S(1)} %get-tuple-element.34.rest_0_.b_keep, f32[72,2304]{1,0:T(8,128)S(1)} %get-tuple-element.32.rest_1_.b_give, f32[72,2048]{1,0:T(8,128)} %get-tuple-element.41.v_keep.refs_2_, f32[72,2048]{1,0:T(8,128)} %get-tuple-element.42.v_give.refs_3_), custom_call_target="tpu_custom_call" | custom-call | tf_op jit(solution)/shard_map/pallas_call | solution.py:528
  37.5 1.5 %collective-permute-start.6 = (f32[2,2,18,1,2048]{4,3,2,1,0:T(1,128)}, f32[2,2,18,1,2048]{4,3,2,1,0:T(1,128)S(1)}, u32[]{:S(2)}, u32[]{:S(2)}) collective-permute-start(f32[2,2,18,1,2048]{4,3,2,1,0:T(1,128)} %shard_map.47), channel_id=1, source_target_pairs={{0,1},{1,0},{2,3},{3,2},{4,5},{5,4},{6,7},{7,6},{8,9},{9,8},{10,11... | collective-permute-start | bytes 1769480 | tf_op jit(solution)/shard_map/ppermute | solution.py:541
  39.1 1.6 %shard_map.44.ahead = f32[3,32,384]{2,1,0:T(8,128)S(1)} custom-call(s32[5]{0:T(128)S(1)} %stack.31.place, f32[192,128]{1,0:T(8,128)S(1)} %get-tuple-element.38.rest_0_, f32[384,128]{1,0:T(8,128)S(1)} %collective-permute-done.rest_0_.rest_1_), custom_call_target="tpu_custom_call" | custom-call | tf_op jit(solution)/shard_map/pallas_call | solution.py:528
  40.7 3.9 %all-to-all-done.recv = f32[8,168,128]{2,1,0:T(8,128)S(1)} async-done(((f32[8,168,128]{2,1,0:T(8,128)}), f32[8,168,128]{2,1,0:T(8,128)S(1)}, u32[]{:S(2)}, u32[]{:S(2)}) %all-to-all-start) | async-done | bytes 688160 | tf_op jit(solution)/shard_map/all_to_all | solution.py:619
  44.6 1.4 %shard_map.45 = f32[216,128]{1,0:T(8,128)S(1)} custom-call(s32[5]{0:T(128)S(1)} %stack.31.place, f32[8,168,128]{2,1,0:T(8,128)S(1)} %all-to-all-done.recv, f32[3,32,384]{2,1,0:T(8,128)S(1)} %shard_map.44.ahead, f32[192,128]{1,0:T(8,128)S(1)} %get-tuple-element.38.rest_0_, f32[384,128]{1,0:T(8,128)S(1)} %collective-permute-done.rest_0_.rest_1_), custom_call_target="tpu_custom_call" | custom-call | tf_op jit(solution)/shard_map/pallas_call | solution.py:528
  46.1 1.9 %collective-permute-start.4 = (f32[216,128]{1,0:T(8,128)S(1)}, f32[216,128]{1,0:T(8,128)S(1)}, u32[]{:S(2)}, u32[]{:S(2)}) collective-permute-start(f32[216,128]{1,0:T(8,128)S(1)} %shard_map.45), channel_id=1, source_target_pairs={{0,16},{1,17},{2,18},{3,19},{4,20},{5,21},{6,22},{7,23},{8,24},{9,... | collective-permute-start | bytes 331784 | tf_op jit(solution)/shard_map/ppermute | solution.py:641
  47.9 1.7 %collective-permute-done.4.carry = f32[216,128]{1,0:T(8,128)S(1)} collective-permute-done((f32[216,128]{1,0:T(8,128)S(1)}, f32[216,128]{1,0:T(8,128)S(1)}, u32[]{:S(2)}, u32[]{:S(2)}) %collective-permute-start.4) | collective-permute-done | bytes 110624 | tf_op jit(solution)/shard_map/ppermute | solution.py:641
  49.7 2.1 %shard_map.46 = f32[8,64,256]{2,1,0:T(8,128)} custom-call(s32[5]{0:T(128)S(1)} %stack.31.place, f32[8,168,128]{2,1,0:T(8,128)S(1)} %all-to-all-done.recv, f32[216,128]{1,0:T(8,128)S(1)} %collective-permute-done.4.carry, f32[192,128]{1,0:T(8,128)S(1)} %get-tuple-element.38.rest_0_, f32[384,128]{1,0:T(8,128)S(1)} %collective-permute-done.rest_0_.rest_1_), custom_call_target="tpu_custom_call" | custom-call | tf_op jit(solution)/shard_map/pallas_call | solution.py:528
  51.8 4.2 %all-to-all-start.1 = ((f32[8,64,256]{2,1,0:T(8,128)}), f32[8,64,256]{2,1,0:T(8,128)S(1)}, u32[]{:S(2)}, u32[]{:S(2)}) async-start(f32[8,64,256]{2,1,0:T(8,128)} %shard_map.46), calls=%async_computation.1 | async-start | bytes 1048576 | tf_op jit(solution)/shard_map/all_to_all | solution.py:650
  56.0 1.6 %collective-permute-done.6.refs_4_ = f32[2,2,18,1,2048]{4,3,2,1,0:T(1,128)S(1)} collective-permute-done((f32[2,2,18,1,2048]{4,3,2,1,0:T(1,128)}, f32[2,2,18,1,2048]{4,3,2,1,0:T(1,128)S(1)}, u32[]{:S(2)}, u32[]{:S(2)}) %collective-permute-start.6) | collective-permute-done | bytes 589856 | tf_op jit(solution)/shard_map/ppermute | solution.py:541
  57.6 2.8 %shard_map.48 = (f32[3,24,4096]{2,1,0:T(8,128)S(1)}, f32[3,16,4096]{2,1,0:T(8,128)}) custom-call(s32[5]{0:T(128)S(1)} %stack.31.place, f32[72,2304]{1,0:T(8,128)} %get-tuple-element.39.refs_0_, f32[72,2304]{1,0:T(8,128)} %get-tuple-element.40.refs_1_, f32[72,2048]{1,0:T(8,128)} %get-tuple-element.41.v_keep.refs_2_, ...), custom_call_target="tpu_custom_call" | custom-call | tf_op jit(solution)/shard_map/pallas_call | solution.py:528
  60.4 0.0 copy-start.1
  60.5 1.5 %collective-permute-start.7 = (f32[3,24,4096]{2,1,0:T(8,128)S(1)}, f32[3,24,4096]{2,1,0:T(8,128)S(1)}, u32[]{:S(2)}, u32[]{:S(2)}) collective-permute-start(f32[3,24,4096]{2,1,0:T(8,128)S(1)} %get-tuple-element.43.refs_1_.refs_2_), channel_id=1, source_target_pairs={{0,2},{1,3},{4,6},{5,7},{8,10},{9,11},{12,14},{13,15},{16,18},{17,... | collective-permute-start | bytes 3538952 | tf_op jit(solution)/shard_map/ppermute | solution.py:636
  61.9 0.6 all-to-all-done.1.refs_0_
  62.5 6.6 %collective-permute-start.5 = (f32[8,64,256]{2,1,0:T(8,128)S(1)}, f32[8,64,256]{2,1,0:T(8,128)S(1)}, u32[]{:S(2)}, u32[]{:S(2)}) collective-permute-start(f32[8,64,256]{2,1,0:T(8,128)S(1)} %all-to-all-done.1.refs_0_), channel_id=1, source_target_pairs={{0,2},{2,0},{1,3},{3,1},{4,6},{6,4},{5,7},{7,5},{8,10},{10,8},{9,1... | collective-permute-start | bytes 1572872 | tf_op jit(solution)/shard_map/ppermute | solution.py:653
  69.1 0.0 collective-permute-done.7.refs_2_.refs_3_
  69.2 0.0 copy-done.1
  69.2 3.2 %shard_map.49.refs_6_ = f32[3,3,16,4096]{3,2,1,0:T(8,128)} custom-call(s32[5]{0:T(128)S(1)} %stack.31.place, f32[8,64,256]{2,1,0:T(8,128)S(1)} %all-to-all-done.1.refs_0_, f32[3,24,4096]{2,1,0:T(8,128)} %copy-done.1, f32[3,24,4096]{2,1,0:T(8,128)S(1)} %collective-permute-done.7.refs_2_.refs_3_, f32[3,16,4096]{2,1,0:T(8,128)} %get-tuple-element.44.refs_3_.refs_4_, ...), custom_call_target="tpu_custom_call" | custom-call | tf_op jit(solution)/shard_map/pallas_call | solution.py:528
  72.4 0.0 collective-permute-done.5.refs_1_
  72.4 3.7 %shard_map.50 = f32[3,3,16,4096]{3,2,1,0:T(8,128)} custom-call(s32[5]{0:T(128)S(1)} %stack.31.place, f32[8,64,256]{2,1,0:T(8,128)S(1)} %all-to-all-done.1.refs_0_, f32[8,64,256]{2,1,0:T(8,128)S(1)} %collective-permute-done.5.refs_1_, f32[3,24,4096]{2,1,0:T(8,128)} %copy-done.1, ...), custom_call_target="tpu_custom_call", output_to_operand_aliasing={{}: (7, {})} | custom-call | tf_op jit(solution)/shard_map/pallas_call | solution.py:528
Async XLA Ops:
  1.8 13.0 %collective-permute-start.1 = (f32[3,16,2304]{2,1,0:T(8,128)S(1)}, f32[3,16,2304]{2,1,0:T(8,128)S(1)}, u32[]{:S(2)}, u32[]{:S(2)}) collective-permute-start(f32[3,16,2304]{2,1,0:T(8,128)S(1)} %get-tuple-element.31), channel_id=1, source_target_pairs={{0,2},{2,4},{4,6},{6,8},{8,10},{10,12},{12,14},{14,16},{16,18},{18... | collective-permute-start | bytes 1327112 | tf_op jit(solution)/shard_map/ppermute | solution.py:573
  8.2 5.4 %collective-permute-start = (f32[384,128]{1,0:T(8,128)S(1)}, f32[384,128]{1,0:T(8,128)S(1)}, u32[]{:S(2)}, u32[]{:S(2)}) collective-permute-start(f32[384,128]{1,0:T(8,128)S(1)} %get-tuple-element.27), channel_id=1, source_target_pairs={{0,1},{1,0},{2,3},{3,2},{4,5},{5,4},{6,7},{7,6},{8,9},{9,8},{10,11... | collective-permute-start | bytes 589832 | tf_op jit(solution)/shard_map/ppermute | solution.py:588
  12.0 2.8 %copy-start = (f32[3,16,4096]{2,1,0:T(8,128)S(1)}, f32[3,16,4096]{2,1,0:T(8,128)}, u32[]{:S(2)}) copy-start(f32[3,16,4096]{2,1,0:T(8,128)} %init.5) | copy-start | bytes 2359300
  17.1 11.2 %collective-permute-start.2 = (f32[72,2304]{1,0:T(8,128)S(1)}, f32[72,2304]{1,0:T(8,128)S(1)}, u32[]{:S(2)}, u32[]{:S(2)}) collective-permute-start(f32[72,2304]{1,0:T(8,128)S(1)} %get-tuple-element.32.rest_1_.b_give), channel_id=1, source_target_pairs={{0,2},{2,0},{1,3},{3,1},{4,6},{6,4},{5,7},{7,5},{8,10},{10,8},{9,1... | collective-permute-start | bytes 1990664 | tf_op jit(solution)/shard_map/ppermute | solution.py:609
  17.1 8.9 %collective-permute-start.3 = (f32[3,16,2048]{2,1,0:T(8,128)S(1)}, f32[3,16,2048]{2,1,0:T(8,128)S(1)}, u32[]{:S(2)}, u32[]{:S(2)}) collective-permute-start(f32[3,16,2048]{2,1,0:T(8,128)S(1)} %get-tuple-element.33), channel_id=1, source_target_pairs={{0,2},{2,4},{4,6},{6,8},{8,10},{10,12},{12,14},{14,16},{16,18},{18... | collective-permute-start | bytes 1179656 | tf_op jit(solution)/shard_map/ppermute | solution.py:574
  31.1 13.5 %all-to-all-start = ((f32[8,168,128]{2,1,0:T(8,128)}), f32[8,168,128]{2,1,0:T(8,128)S(1)}, u32[]{:S(2)}, u32[]{:S(2)}) async-start(f32[8,168,128]{2,1,0:T(8,128)} %get-tuple-element.37), calls=%async_computation | async-start | bytes 1376256 | tf_op jit(solution)/shard_map/all_to_all | solution.py:619
  37.5 20.1 %collective-permute-start.6 = (f32[2,2,18,1,2048]{4,3,2,1,0:T(1,128)}, f32[2,2,18,1,2048]{4,3,2,1,0:T(1,128)S(1)}, u32[]{:S(2)}, u32[]{:S(2)}) collective-permute-start(f32[2,2,18,1,2048]{4,3,2,1,0:T(1,128)} %shard_map.47), channel_id=1, source_target_pairs={{0,1},{1,0},{2,3},{3,2},{4,5},{5,4},{6,7},{7,6},{8,9},{9,8},{10,11... | collective-permute-start | bytes 1769480 | tf_op jit(solution)/shard_map/ppermute | solution.py:541
  46.1 3.6 %collective-permute-start.4 = (f32[216,128]{1,0:T(8,128)S(1)}, f32[216,128]{1,0:T(8,128)S(1)}, u32[]{:S(2)}, u32[]{:S(2)}) collective-permute-start(f32[216,128]{1,0:T(8,128)S(1)} %shard_map.45), channel_id=1, source_target_pairs={{0,16},{1,17},{2,18},{3,19},{4,20},{5,21},{6,22},{7,23},{8,24},{9,... | collective-permute-start | bytes 331784 | tf_op jit(solution)/shard_map/ppermute | solution.py:641
  51.8 10.7 %all-to-all-start.1 = ((f32[8,64,256]{2,1,0:T(8,128)}), f32[8,64,256]{2,1,0:T(8,128)S(1)}, u32[]{:S(2)}, u32[]{:S(2)}) async-start(f32[8,64,256]{2,1,0:T(8,128)} %shard_map.46), calls=%async_computation.1 | async-start | bytes 1048576 | tf_op jit(solution)/shard_map/all_to_all | solution.py:650
  60.4 8.7 %copy-start.1 = (f32[3,24,4096]{2,1,0:T(8,128)}, f32[3,24,4096]{2,1,0:T(8,128)S(1)}, u32[]{:S(2)}) copy-start(f32[3,24,4096]{2,1,0:T(8,128)S(1)} %get-tuple-element.43.refs_1_.refs_2_) | copy-start | bytes 3538948
  60.5 8.7 %collective-permute-start.7 = (f32[3,24,4096]{2,1,0:T(8,128)S(1)}, f32[3,24,4096]{2,1,0:T(8,128)S(1)}, u32[]{:S(2)}, u32[]{:S(2)}) collective-permute-start(f32[3,24,4096]{2,1,0:T(8,128)S(1)} %get-tuple-element.43.refs_1_.refs_2_), channel_id=1, source_target_pairs={{0,2},{1,3},{4,6},{5,7},{8,10},{9,11},{12,14},{13,15},{16,18},{17,... | collective-permute-start | bytes 3538952 | tf_op jit(solution)/shard_map/ppermute | solution.py:636
  62.5 9.9 %collective-permute-start.5 = (f32[8,64,256]{2,1,0:T(8,128)S(1)}, f32[8,64,256]{2,1,0:T(8,128)S(1)}, u32[]{:S(2)}, u32[]{:S(2)}) collective-permute-start(f32[8,64,256]{2,1,0:T(8,128)S(1)} %all-to-all-done.1.refs_0_), channel_id=1, source_target_pairs={{0,2},{2,0},{1,3},{3,1},{4,6},{6,4},{5,7},{7,5},{8,10},{10,8},{9,1... | collective-permute-start | bytes 1572872 | tf_op jit(solution)/shard_map/ppermute | solution.py:653

commit v7 on v6

--- a/solution.py
+++ b/solution.py
@@ -71,7 +71,7 @@
     return ref[lead + (slice(None), pl.ds(pl.multiple_of(at, LANES), size))]
 
 
-def last_body(place, nodes, soon_out, late_out, sems):
+def last_copies(place, nodes, soon_out, late_out, sems):
     cols = nodes.shape[-1]
     half = cols // 2
     start = place[2] * half
@@ -87,6 +87,17 @@
         source = nodes.at[2, :, :, pl.ds(pl.multiple_of(at, LANES), size)]
         copies.append(pltpu.make_async_copy(source, out.at[:, :, to : to + size], sems.at[i]))
         copies[-1].start()
+    return copies
+
+
+def last_body(place, nodes, soon_out, late_out, sems):
+    for copy in last_copies(place, nodes, soon_out, late_out, sems):
+        copy.wait()
+
+
+def begin_body(width, reach, place, nodes, depth_far, init, soon_out, late_out, own_out, edge_out, depth, held, sems, more):
+    copies = last_copies(place, nodes, soon_out, late_out, more)
+    prepare_body(width, reach, place, depth_far, init, own_out, edge_out, depth, held, sems)
     for copy in copies:
         copy.wait()
 
@@ -565,26 +576,30 @@
     swapped = [(0, 1), (1, 0)]
     plan = (spaces, rows, width, reach)
 
-    soon, late = kernel(
-        last_body, [(3, rows, half + 2 * LANES), (3, rows, half)], place, nodes, scalars=1, far=(1,),
-        scratch_shapes=[pltpu.SemaphoreType.DMA((4,))],
-    )
     onward = [(i, i + 1) for i in range(slices - 1)]
-    prev = lax.ppermute(soon, ("outer", "inner", "core"), onward)
-    prev_late = lax.ppermute(late, ("outer", "inner", "core"), onward)
-
-    if spaces == 2 and dense(width, reach, rows):
+    last_shapes = [(3, rows, half + 2 * LANES), (3, rows, half)]
+    paired = spaces == 2 and dense(width, reach, rows)
+    if paired:
         own_rows = 4 * rows * span // LANES
-        own, edges = kernel(
-            functools.partial(prepare_body, width, reach),
-            [(own_rows, LANES), (own_rows + 2 * DEEP * cols // LANES, LANES)],
-            place, mean_depth, init_state, scalars=1, far=(1, 2),
+        soon, late, own, edges = kernel(
+            functools.partial(begin_body, width, reach),
+            last_shapes + [(own_rows, LANES), (own_rows + 2 * DEEP * cols // LANES, LANES)],
+            place, nodes, mean_depth, init_state, scalars=1, far=(1, 2, 3),
             scratch_shapes=[
                 pltpu.VMEM((rows, cols), jnp.float32),
                 pltpu.VMEM((2, 4, rows, width + 2 * LANES), jnp.float32),
                 pltpu.SemaphoreType.DMA((25,)),
+                pltpu.SemaphoreType.DMA((4,)),
             ],
         )
+    else:
+        soon, late = kernel(
+            last_body, last_shapes, place, nodes, scalars=1, far=(1,),
+            scratch_shapes=[pltpu.SemaphoreType.DMA((4,))],
+        )
+    prev = lax.ppermute(soon, ("outer", "inner", "core"), onward)
+    prev_late = lax.ppermute(late, ("outer", "inner", "core"), onward)
+    if paired:
         edges = lax.ppermute(edges, "space", swapped)
         windows, edges = (own, edges), (edges,)
     else:

time: 76.8 us -> 75.7 us (0.986)
  Pallas kernels: 31.4 us -> 30 us
    pallas_call x14 -> x13, Pallas kernels: 31.4 us -> 30 us  [kernel(): pl.pallas_call(body, out_shape=outs if many else outs[0], in_specs=[smem...]
  transfers between devices with their start and end apart: 10 -> 10, of which waited for: 6 -> 6; matrix products, arithmetic and copies ran while one was open for 0% -> 0% of each run, Pallas kernels for 27% -> 25%
where the time goes in v7:
time: 75.7 us; the launch traced here: 75.2 us
  starting transfers between devices  30.5 us (40%)
  Pallas kernels  30 us (40%)
  waiting for transfers between devices  14.2 us (19%)
    pallas_call x13, Pallas kernels, kernel(): pl.pallas_call(body, out_shape=outs if many else outs[0], in_specs=[smem...  30 us
    ppermute x1, starting transfers between devices, per_device(): other = lax.ppermute(mine, 'core', swapped)  6.63 us
    ppermute x1, waiting for transfers between devices, per_device(): prev_late = lax.ppermute(late, ('outer', 'inner', 'core'), onward)  4.7 us
    all_to_all x1, starting transfers between devices, per_device(): recv = lax.all_to_all(msgs, group, 0, 0, tiled=True)  4.67 us
    ppermute x1, starting transfers between devices, per_device(): prev = lax.ppermute(soon, ('outer', 'inner', 'core'), onward)  4.5 us
    ppermute x1, starting transfers between devices, per_device(): prev_late = lax.ppermute(late, ('outer', 'inner', 'core'), onward)  4.29 us
    all_to_all x1, starting transfers between devices, per_device(): mine = lax.all_to_all(back, group, 0, 0, tiled=True)  4.19 us
    all_to_all x1, waiting for transfers between devices, per_device(): recv = lax.all_to_all(msgs, group, 0, 0, tiled=True)  3.96 us
  transfers between devices with their start and end apart: 10, of which 6 were waited for; matrix products, arithmetic and copies ran while one was open for 0% of the time, Pallas kernels for 25%

profile of v7, /device:TPU:1, one launch (start us, length us, event | category | flops | bytes accessed | tf_op | source)
XLA Modules:
  0.0 75.2 jit_solution(16252705573677551492)
XLA Ops:
  0.0 0.1 stack.31.place
  0.1 2.2 %shard_map.38 = (f32[3,16,2304]{2,1,0:T(8,128)S(1)}, f32[3,16,2048]{2,1,0:T(8,128)S(1)}, f32[192,128]{1,0:T(8,128)S(1)}, f32[384,128]{1,0:T(8,128)S(1)}) custom-call(s32[5]{0:T(128)S(1)} %stack.31.place, f32[3,3,16,4096]{3,2,1,0:T(8,128)} %bitcast.7, f32[16,4096]{1,0:T(8,128)} %depth_far.3, f32[3,16,4096]{2,1,0:T(8,128)} %init.5), custom_call_target="tpu_custom_call" | custom-call | tf_op jit(solution)/shard_map/pallas_call | solution.py:539
  2.3 4.5 %collective-permute-start.1 = (f32[3,16,2304]{2,1,0:T(8,128)S(1)}, f32[3,16,2304]{2,1,0:T(8,128)S(1)}, u32[]{:S(2)}, u32[]{:S(2)}) collective-permute-start(f32[3,16,2304]{2,1,0:T(8,128)S(1)} %get-tuple-element.31), channel_id=1, source_target_pairs={{0,2},{2,4},{4,6},{6,8},{8,10},{10,12},{12,14},{14,16},{16,18},{18... | collective-permute-start | bytes 1327112 | tf_op jit(solution)/shard_map/ppermute | solution.py:600
  6.8 1.3 %collective-permute-start = (f32[384,128]{1,0:T(8,128)S(1)}, f32[384,128]{1,0:T(8,128)S(1)}, u32[]{:S(2)}, u32[]{:S(2)}) collective-permute-start(f32[384,128]{1,0:T(8,128)S(1)} %get-tuple-element.27), channel_id=1, source_target_pairs={{0,1},{1,0},{2,3},{3,2},{4,5},{5,4},{6,7},{7,6},{8,9},{9,8},{10,11... | collective-permute-start | bytes 589832 | tf_op jit(solution)/shard_map/ppermute | solution.py:603
  8.1 2.5 %shard_map.37 = (f32[3,16,4096]{2,1,0:T(8,128)S(1)}, f32[3,24,4096]{2,1,0:T(8,128)S(1)}, f32[24,4096]{1,0:T(8,128)S(1)}) custom-call(f32[3,3,16,4096]{3,2,1,0:T(8,128)} %bitcast.8, f32[16,4096]{1,0:T(8,128)} %depth_far.3), custom_call_target="tpu_custom_call" | custom-call | tf_op jit(solution)/shard_map/pallas_call | solution.py:539
  10.6 0.0 copy-start
  10.6 1.6 %collective-permute-done.rest_0_.rest_1_ = f32[384,128]{1,0:T(8,128)S(1)} collective-permute-done((f32[384,128]{1,0:T(8,128)S(1)}, f32[384,128]{1,0:T(8,128)S(1)}, u32[]{:S(2)}, u32[]{:S(2)}) %collective-permute-start) | collective-permute-done | bytes 196640 | tf_op jit(solution)/shard_map/ppermute | solution.py:603
  12.2 1.2 %shard_map.39 = (f32[3,24,4096]{2,1,0:T(8,128)S(1)}, f32[24,4096]{1,0:T(8,128)S(1)}) custom-call(f32[3,24,4096]{2,1,0:T(8,128)S(1)} %get-tuple-element.25.fk, f32[24,4096]{1,0:T(8,128)S(1)} %get-tuple-element.26.bare, f32[384,128]{1,0:T(8,128)S(1)} %collective-permute-done.rest_0_.rest_1_), custom_call_target="tpu_custom_call" | custom-call | tf_op jit(solution)/shard_map/pallas_call | solution.py:539
  13.4 0.0 collective-permute-done.1.prev
  13.4 0.0 copy-done
  13.4 2.3 %shard_map.40 = (f32[72,2304]{1,0:T(8,128)S(1)}, f32[72,2048]{1,0:T(8,128)S(1)}) custom-call(s32[5]{0:T(128)S(1)} %stack.31.place, f32[3,16,4096]{2,1,0:T(8,128)S(1)} %get-tuple-element.29.base, f32[3,16,4096]{2,1,0:T(8,128)S(1)} %copy-done, f32[3,24,4096]{2,1,0:T(8,128)S(1)} %get-tuple-element.25.fk, f32[3,24,4096]{2,1,0:T(8,128)S(1)} %get-tuple-element.30.ffk, ...), custom_call_target="tpu_custom_call" | custom-call | tf_op jit(solution)/shard_map/pallas_call | solution.py:539
  15.7 0.1 collective-permute-start.2
  15.8 4.3 %collective-permute-start.3 = (f32[3,16,2048]{2,1,0:T(8,128)S(1)}, f32[3,16,2048]{2,1,0:T(8,128)S(1)}, u32[]{:S(2)}, u32[]{:S(2)}) collective-permute-start(f32[3,16,2048]{2,1,0:T(8,128)S(1)} %get-tuple-element.33), channel_id=1, source_target_pairs={{0,2},{2,4},{4,6},{6,8},{8,10},{10,12},{12,14},{14,16},{16,18},{18... | collective-permute-start | bytes 1179656 | tf_op jit(solution)/shard_map/ppermute | solution.py:601
  20.1 4.7 %collective-permute-done.3.rest_0_ = f32[3,16,2048]{2,1,0:T(8,128)S(1)} collective-permute-done((f32[3,16,2048]{2,1,0:T(8,128)S(1)}, f32[3,16,2048]{2,1,0:T(8,128)S(1)}, u32[]{:S(2)}, u32[]{:S(2)}) %collective-permute-start.3) | collective-permute-done | bytes 393248 | tf_op jit(solution)/shard_map/ppermute | solution.py:601
  24.8 2.2 %shard_map.41 = (f32[72,2304]{1,0:T(8,128)S(1)}, f32[72,2048]{1,0:T(8,128)S(1)}) custom-call(s32[5]{0:T(128)S(1)} %stack.31.place, f32[3,16,4096]{2,1,0:T(8,128)S(1)} %get-tuple-element.29.base, f32[3,16,4096]{2,1,0:T(8,128)S(1)} %copy-done, f32[3,24,4096]{2,1,0:T(8,128)S(1)} %get-tuple-element.25.fk, f32[3,24,4096]{2,1,0:T(8,128)S(1)} %get-tuple-element.30.ffk, ...), custom_call_target="tpu_custom_call" | custom-call | tf_op jit(solution)/shard_map/pallas_call | solution.py:539
  27.0 0.0 collective-permute-done.2.got
  27.0 2.8 %shard_map.42 = (f32[8,168,128]{2,1,0:T(8,128)}, f32[72,2304]{1,0:T(8,128)}, f32[72,2304]{1,0:T(8,128)}, f32[72,2048]{1,0:T(8,128)}, f32[72,2048]{1,0:T(8,128)}) custom-call(s32[5]{0:T(128)S(1)} %stack.31.place, f32[24,4096]{1,0:T(8,128)S(1)} %get-tuple-element.28.depth_ref.refs_4_.refs_5_, f32[72,2304]{1,0:T(8,128)S(1)} %collective-permute-done.2.got, ...), custom_call_target="tpu_custom_call" | custom-call | tf_op jit(solution)/shard_map/pallas_call | solution.py:539
  29.9 4.7 %all-to-all-start = ((f32[8,168,128]{2,1,0:T(8,128)}), f32[8,168,128]{2,1,0:T(8,128)S(1)}, u32[]{:S(2)}, u32[]{:S(2)}) async-start(f32[8,168,128]{2,1,0:T(8,128)} %get-tuple-element.37), calls=%async_computation | async-start | bytes 1376256 | tf_op jit(solution)/shard_map/all_to_all | solution.py:634
  34.6 1.9 %shard_map.46 = f32[2,2,18,1,2048]{4,3,2,1,0:T(1,128)} custom-call(f32[72,2304]{1,0:T(8,128)S(1)} %get-tuple-element.34.rest_0_.b_keep, f32[72,2304]{1,0:T(8,128)S(1)} %get-tuple-element.32.rest_1_.b_give, f32[72,2048]{1,0:T(8,128)} %get-tuple-element.41.v_keep.refs_2_, f32[72,2048]{1,0:T(8,128)} %get-tuple-element.42.v_give.refs_3_), custom_call_target="tpu_custom_call" | custom-call | tf_op jit(solution)/shard_map/pallas_call | solution.py:539
  36.5 1.5 %collective-permute-start.6 = (f32[2,2,18,1,2048]{4,3,2,1,0:T(1,128)}, f32[2,2,18,1,2048]{4,3,2,1,0:T(1,128)S(1)}, u32[]{:S(2)}, u32[]{:S(2)}) collective-permute-start(f32[2,2,18,1,2048]{4,3,2,1,0:T(1,128)} %shard_map.46), channel_id=1, source_target_pairs={{0,1},{1,0},{2,3},{3,2},{4,5},{5,4},{6,7},{7,6},{8,9},{9,8},{10,11... | collective-permute-start | bytes 1769480 | tf_op jit(solution)/shard_map/ppermute | solution.py:552
  38.0 1.6 %shard_map.43.ahead = f32[3,32,384]{2,1,0:T(8,128)S(1)} custom-call(s32[5]{0:T(128)S(1)} %stack.31.place, f32[192,128]{1,0:T(8,128)S(1)} %get-tuple-element.38.rest_0_, f32[384,128]{1,0:T(8,128)S(1)} %collective-permute-done.rest_0_.rest_1_), custom_call_target="tpu_custom_call" | custom-call | tf_op jit(solution)/shard_map/pallas_call | solution.py:539
  39.6 4.0 %all-to-all-done.recv = f32[8,168,128]{2,1,0:T(8,128)S(1)} async-done(((f32[8,168,128]{2,1,0:T(8,128)}), f32[8,168,128]{2,1,0:T(8,128)S(1)}, u32[]{:S(2)}, u32[]{:S(2)}) %all-to-all-start) | async-done | bytes 688160 | tf_op jit(solution)/shard_map/all_to_all | solution.py:634
  43.6 1.4 %shard_map.44 = f32[216,128]{1,0:T(8,128)S(1)} custom-call(s32[5]{0:T(128)S(1)} %stack.31.place, f32[8,168,128]{2,1,0:T(8,128)S(1)} %all-to-all-done.recv, f32[3,32,384]{2,1,0:T(8,128)S(1)} %shard_map.43.ahead, f32[192,128]{1,0:T(8,128)S(1)} %get-tuple-element.38.rest_0_, f32[384,128]{1,0:T(8,128)S(1)} %collective-permute-done.rest_0_.rest_1_), custom_call_target="tpu_custom_call" | custom-call | tf_op jit(solution)/shard_map/pallas_call | solution.py:539
  45.0 1.8 %collective-permute-start.4 = (f32[216,128]{1,0:T(8,128)S(1)}, f32[216,128]{1,0:T(8,128)S(1)}, u32[]{:S(2)}, u32[]{:S(2)}) collective-permute-start(f32[216,128]{1,0:T(8,128)S(1)} %shard_map.44), channel_id=1, source_target_pairs={{0,16},{1,17},{2,18},{3,19},{4,20},{5,21},{6,22},{7,23},{8,24},{9,... | collective-permute-start | bytes 331784 | tf_op jit(solution)/shard_map/ppermute | solution.py:656
  46.9 1.7 %collective-permute-done.4.carry = f32[216,128]{1,0:T(8,128)S(1)} collective-permute-done((f32[216,128]{1,0:T(8,128)S(1)}, f32[216,128]{1,0:T(8,128)S(1)}, u32[]{:S(2)}, u32[]{:S(2)}) %collective-permute-start.4) | collective-permute-done | bytes 110624 | tf_op jit(solution)/shard_map/ppermute | solution.py:656
  48.6 2.1 %shard_map.45 = f32[8,64,256]{2,1,0:T(8,128)} custom-call(s32[5]{0:T(128)S(1)} %stack.31.place, f32[8,168,128]{2,1,0:T(8,128)S(1)} %all-to-all-done.recv, f32[216,128]{1,0:T(8,128)S(1)} %collective-permute-done.4.carry, f32[192,128]{1,0:T(8,128)S(1)} %get-tuple-element.38.rest_0_, f32[384,128]{1,0:T(8,128)S(1)} %collective-permute-done.rest_0_.rest_1_), custom_call_target="tpu_custom_call" | custom-call | tf_op jit(solution)/shard_map/pallas_call | solution.py:539
  50.7 4.2 %all-to-all-start.1 = ((f32[8,64,256]{2,1,0:T(8,128)}), f32[8,64,256]{2,1,0:T(8,128)S(1)}, u32[]{:S(2)}, u32[]{:S(2)}) async-start(f32[8,64,256]{2,1,0:T(8,128)} %shard_map.45), calls=%async_computation.1 | async-start | bytes 1048576 | tf_op jit(solution)/shard_map/all_to_all | solution.py:665
  54.9 1.6 %collective-permute-done.6.refs_4_ = f32[2,2,18,1,2048]{4,3,2,1,0:T(1,128)S(1)} collective-permute-done((f32[2,2,18,1,2048]{4,3,2,1,0:T(1,128)}, f32[2,2,18,1,2048]{4,3,2,1,0:T(1,128)S(1)}, u32[]{:S(2)}, u32[]{:S(2)}) %collective-permute-start.6) | collective-permute-done | bytes 589856 | tf_op jit(solution)/shard_map/ppermute | solution.py:552
  56.6 2.8 %shard_map.47 = (f32[3,24,4096]{2,1,0:T(8,128)S(1)}, f32[3,16,4096]{2,1,0:T(8,128)}) custom-call(s32[5]{0:T(128)S(1)} %stack.31.place, f32[72,2304]{1,0:T(8,128)} %get-tuple-element.39.refs_0_, f32[72,2304]{1,0:T(8,128)} %get-tuple-element.40.refs_1_, f32[72,2048]{1,0:T(8,128)} %get-tuple-element.41.v_keep.refs_2_, ...), custom_call_target="tpu_custom_call" | custom-call | tf_op jit(solution)/shard_map/pallas_call | solution.py:539
  59.4 0.0 copy-start.1
  59.4 1.5 %collective-permute-start.7 = (f32[3,24,4096]{2,1,0:T(8,128)S(1)}, f32[3,24,4096]{2,1,0:T(8,128)S(1)}, u32[]{:S(2)}, u32[]{:S(2)}) collective-permute-start(f32[3,24,4096]{2,1,0:T(8,128)S(1)} %get-tuple-element.43.refs_1_.refs_2_), channel_id=1, source_target_pairs={{0,2},{1,3},{4,6},{5,7},{8,10},{9,11},{12,14},{13,15},{16,18},{17,... | collective-permute-start | bytes 3538952 | tf_op jit(solution)/shard_map/ppermute | solution.py:651
  60.9 0.6 all-to-all-done.1.refs_0_
  61.5 6.6 %collective-permute-start.5 = (f32[8,64,256]{2,1,0:T(8,128)S(1)}, f32[8,64,256]{2,1,0:T(8,128)S(1)}, u32[]{:S(2)}, u32[]{:S(2)}) collective-permute-start(f32[8,64,256]{2,1,0:T(8,128)S(1)} %all-to-all-done.1.refs_0_), channel_id=1, source_target_pairs={{0,2},{2,0},{1,3},{3,1},{4,6},{6,4},{5,7},{7,5},{8,10},{10,8},{9,1... | collective-permute-start | bytes 1572872 | tf_op jit(solution)/shard_map/ppermute | solution.py:668
  68.1 0.0 collective-permute-done.7.refs_2_.refs_3_
  68.1 0.0 copy-done.1
  68.1 3.2 %shard_map.48.refs_6_ = f32[3,3,16,4096]{3,2,1,0:T(8,128)} custom-call(s32[5]{0:T(128)S(1)} %stack.31.place, f32[8,64,256]{2,1,0:T(8,128)S(1)} %all-to-all-done.1.refs_0_, f32[3,24,4096]{2,1,0:T(8,128)} %copy-done.1, f32[3,24,4096]{2,1,0:T(8,128)S(1)} %collective-permute-done.7.refs_2_.refs_3_, f32[3,16,4096]{2,1,0:T(8,128)} %get-tuple-element.44.refs_3_.refs_4_, ...), custom_call_target="tpu_custom_call" | custom-call | tf_op jit(solution)/shard_map/pallas_call | solution.py:539
  71.3 0.0 collective-permute-done.5.refs_1_
  71.3 3.7 %shard_map.49 = f32[3,3,16,4096]{3,2,1,0:T(8,128)} custom-call(s32[5]{0:T(128)S(1)} %stack.31.place, f32[8,64,256]{2,1,0:T(8,128)S(1)} %all-to-all-done.1.refs_0_, f32[8,64,256]{2,1,0:T(8,128)S(1)} %collective-permute-done.5.refs_1_, f32[3,24,4096]{2,1,0:T(8,128)} %copy-done.1, ...), custom_call_target="tpu_custom_call", output_to_operand_aliasing={{}: (7, {})} | custom-call | tf_op jit(solution)/shard_map/pallas_call | solution.py:539
Async XLA Ops:
  2.3 11.1 %collective-permute-start.1 = (f32[3,16,2304]{2,1,0:T(8,128)S(1)}, f32[3,16,2304]{2,1,0:T(8,128)S(1)}, u32[]{:S(2)}, u32[]{:S(2)}) collective-permute-start(f32[3,16,2304]{2,1,0:T(8,128)S(1)} %get-tuple-element.31), channel_id=1, source_target_pairs={{0,2},{2,4},{4,6},{6,8},{8,10},{10,12},{12,14},{14,16},{16,18},{18... | collective-permute-start | bytes 1327112 | tf_op jit(solution)/shard_map/ppermute | solution.py:600
  6.8 5.4 %collective-permute-start = (f32[384,128]{1,0:T(8,128)S(1)}, f32[384,128]{1,0:T(8,128)S(1)}, u32[]{:S(2)}, u32[]{:S(2)}) collective-permute-start(f32[384,128]{1,0:T(8,128)S(1)} %get-tuple-element.27), channel_id=1, source_target_pairs={{0,1},{1,0},{2,3},{3,2},{4,5},{5,4},{6,7},{7,6},{8,9},{9,8},{10,11... | collective-permute-start | bytes 589832 | tf_op jit(solution)/shard_map/ppermute | solution.py:603
  10.6 2.8 %copy-start = (f32[3,16,4096]{2,1,0:T(8,128)S(1)}, f32[3,16,4096]{2,1,0:T(8,128)}, u32[]{:S(2)}) copy-start(f32[3,16,4096]{2,1,0:T(8,128)} %init.5) | copy-start | bytes 2359300
  15.7 11.3 %collective-permute-start.2 = (f32[72,2304]{1,0:T(8,128)S(1)}, f32[72,2304]{1,0:T(8,128)S(1)}, u32[]{:S(2)}, u32[]{:S(2)}) collective-permute-start(f32[72,2304]{1,0:T(8,128)S(1)} %get-tuple-element.32.rest_1_.b_give), channel_id=1, source_target_pairs={{0,2},{2,0},{1,3},{3,1},{4,6},{6,4},{5,7},{7,5},{8,10},{10,8},{9,1... | collective-permute-start | bytes 1990664 | tf_op jit(solution)/shard_map/ppermute | solution.py:624
  15.8 9.0 %collective-permute-start.3 = (f32[3,16,2048]{2,1,0:T(8,128)S(1)}, f32[3,16,2048]{2,1,0:T(8,128)S(1)}, u32[]{:S(2)}, u32[]{:S(2)}) collective-permute-start(f32[3,16,2048]{2,1,0:T(8,128)S(1)} %get-tuple-element.33), channel_id=1, source_target_pairs={{0,2},{2,4},{4,6},{6,8},{8,10},{10,12},{12,14},{14,16},{16,18},{18... | collective-permute-start | bytes 1179656 | tf_op jit(solution)/shard_map/ppermute | solution.py:601
  29.9 13.7 %all-to-all-start = ((f32[8,168,128]{2,1,0:T(8,128)}), f32[8,168,128]{2,1,0:T(8,128)S(1)}, u32[]{:S(2)}, u32[]{:S(2)}) async-start(f32[8,168,128]{2,1,0:T(8,128)} %get-tuple-element.37), calls=%async_computation | async-start | bytes 1376256 | tf_op jit(solution)/shard_map/all_to_all | solution.py:634
  36.5 20.1 %collective-permute-start.6 = (f32[2,2,18,1,2048]{4,3,2,1,0:T(1,128)}, f32[2,2,18,1,2048]{4,3,2,1,0:T(1,128)S(1)}, u32[]{:S(2)}, u32[]{:S(2)}) collective-permute-start(f32[2,2,18,1,2048]{4,3,2,1,0:T(1,128)} %shard_map.46), channel_id=1, source_target_pairs={{0,1},{1,0},{2,3},{3,2},{4,5},{5,4},{6,7},{7,6},{8,9},{9,8},{10,11... | collective-permute-start | bytes 1769480 | tf_op jit(solution)/shard_map/ppermute | solution.py:552
  45.0 3.6 %collective-permute-start.4 = (f32[216,128]{1,0:T(8,128)S(1)}, f32[216,128]{1,0:T(8,128)S(1)}, u32[]{:S(2)}, u32[]{:S(2)}) collective-permute-start(f32[216,128]{1,0:T(8,128)S(1)} %shard_map.44), channel_id=1, source_target_pairs={{0,16},{1,17},{2,18},{3,19},{4,20},{5,21},{6,22},{7,23},{8,24},{9,... | collective-permute-start | bytes 331784 | tf_op jit(solution)/shard_map/ppermute | solution.py:656
  50.7 10.7 %all-to-all-start.1 = ((f32[8,64,256]{2,1,0:T(8,128)}), f32[8,64,256]{2,1,0:T(8,128)S(1)}, u32[]{:S(2)}, u32[]{:S(2)}) async-start(f32[8,64,256]{2,1,0:T(8,128)} %shard_map.45), calls=%async_computation.1 | async-start | bytes 1048576 | tf_op jit(solution)/shard_map/all_to_all | solution.py:665
  59.4 8.7 %copy-start.1 = (f32[3,24,4096]{2,1,0:T(8,128)}, f32[3,24,4096]{2,1,0:T(8,128)S(1)}, u32[]{:S(2)}) copy-start(f32[3,24,4096]{2,1,0:T(8,128)S(1)} %get-tuple-element.43.refs_1_.refs_2_) | copy-start | bytes 3538948
  59.4 8.7 %collective-permute-start.7 = (f32[3,24,4096]{2,1,0:T(8,128)S(1)}, f32[3,24,4096]{2,1,0:T(8,128)S(1)}, u32[]{:S(2)}, u32[]{:S(2)}) collective-permute-start(f32[3,24,4096]{2,1,0:T(8,128)S(1)} %get-tuple-element.43.refs_1_.refs_2_), channel_id=1, source_target_pairs={{0,2},{1,3},{4,6},{5,7},{8,10},{9,11},{12,14},{13,15},{16,18},{17,... | collective-permute-start | bytes 3538952 | tf_op jit(solution)/shard_map/ppermute | solution.py:651
  61.5 9.9 %collective-permute-start.5 = (f32[8,64,256]{2,1,0:T(8,128)S(1)}, f32[8,64,256]{2,1,0:T(8,128)S(1)}, u32[]{:S(2)}, u32[]{:S(2)}) collective-permute-start(f32[8,64,256]{2,1,0:T(8,128)S(1)} %all-to-all-done.1.refs_0_), channel_id=1, source_target_pairs={{0,2},{2,0},{1,3},{3,1},{4,6},{6,4},{5,7},{7,5},{8,10},{10,8},{9,1... | collective-permute-start | bytes 1572872 | tf_op jit(solution)/shard_map/ppermute | solution.py:668

commit v8 on v7

--- a/solution.py
+++ b/solution.py
@@ -214,13 +214,17 @@
         b_out[at, :] = DT * (u[f] + (1.0 / 6.0) * (HALF * fu[f] + window(ffk, (f,), half)))
 
 
-def spill_body(b_keep, b_give, v_keep, v_give, spill_out, v_spread, sems):
+def spill_body(b_keep, b_give, v_keep, v_give, spill_out, keep_far, give_far, v_spread, sems):
     wide = b_keep.shape[0] // 3
     rows = wide - TILE
     copies = [
         pltpu.make_async_copy(v.at[pl.ds(f * wide + rows, TILE), :], v_spread.at[h, f], sems.at[3 * h + f])
         for h, v in enumerate((v_keep, v_give))
         for f in range(3)
+    ]
+    copies += [
+        pltpu.make_async_copy(b_keep, keep_far, sems.at[6]),
+        pltpu.make_async_copy(b_give, give_far, sems.at[7]),
     ]
     for copy in copies:
         copy.start()
@@ -232,13 +236,15 @@
                 for r in range(DEEP):
                     spill_out[side, h, DEEP * f + r] = b[top + spread + r : top + spread + r + 1, inside]
                 spill_out[side, h, 9 + f] = b[top + edge : top + edge + 1, inside]
-    for copy in copies:
+    for copy in copies[:6]:
         copy.wait()
     for h in range(2):
         for f in range(3):
             for side, spread in ((0, TILE - 2), (1, 0)):
                 for r in range(2):
                     spill_out[side, h, 12 + 2 * f + r] = v_spread[h, f, spread + r : spread + r + 1, :]
+    for copy in copies[6:]:
+        copy.wait()
 
 
 def mend_body(place, *refs):
@@ -280,14 +286,10 @@
     copy.wait()
 
 
-def pair_body(width, reach, count, place, depth_ref, got, *rest):
-    near, far = rest[:count], rest[count + 1 : 2 * count + 1]
-    msg_far, msg_out, sems = rest[count], rest[-2], rest[-1]
-    owners = msg_out.shape[0]
-    copies = [pltpu.make_async_copy(a, b, sems.at[owners + i]) for i, (a, b) in enumerate(zip(near, far))]
+def pair_body(width, reach, place, depth_ref, got, keep, v_keep, v_give, msg_far, vk_far, vg_far, msg_out, sems):
+    copies = [pltpu.make_async_copy(v_keep, vk_far, sems.at[1]), pltpu.make_async_copy(v_give, vg_far, sems.at[2])]
     for copy in copies:
         copy.start()
-    keep = near[0]
     wide = keep.shape[0] // 3
     even = place[2] == 0
     step_depth = DT * window(depth_ref, (), place[2])
@@ -296,7 +298,7 @@
     first = tuple(jnp.where(even, x, y) for x, y in zip(own, other))
     second = tuple(jnp.where(even, y, x) for x, y in zip(own, other))
     both = tuple(x + y for x, y in zip(second, stepped(first, step_depth)))
-    for j in range(owners):
+    for j in range(msg_out.shape[0]):
         for f in range(3):
             pack_block(both[f], f, j, width, reach, msg_out.at[j])
     copies.append(pltpu.make_async_copy(msg_out, msg_far, sems.at[0]))
@@ -625,17 +627,18 @@
     keep, v_keep = kernel(functools.partial(fine_body, True), fine_shapes, *fine_args, prev_late, scalars=1)
     tight = packed_rows(wide, width, reach)
     msg_shape = (owners, tight, LANES) if tight else (owners, 3 * wide, span)
-    parts = (keep, give, v_keep, v_give)
-    msgs, *far_parts = kernel(
-        functools.partial(pair_body, width, reach, len(parts)), [msg_shape] + [x.shape for x in parts],
-        place, depth, got, *parts, scalars=1, far_out=range(1 + len(parts)),
-        scratch_shapes=[pltpu.VMEM(msg_shape, jnp.float32), pltpu.SemaphoreType.DMA((owners + len(parts),))],
+    msgs, v_keep, v_give = kernel(
+        functools.partial(pair_body, width, reach), [msg_shape, v_keep.shape, v_give.shape],
+        place, depth, got, keep, v_keep, v_give, scalars=1, far_out=(0, 1, 2),
+        scratch_shapes=[pltpu.VMEM(msg_shape, jnp.float32), pltpu.SemaphoreType.DMA((3,))],
     )
     recv = lax.all_to_all(msgs, group, 0, 0, tiled=True)
-    spill = kernel(
-        spill_body, (2, 2, 18, 1, half), keep, give, *far_parts[2:], far=(2, 3),
-        scratch_shapes=[pltpu.VMEM((2, 3, TILE, half), jnp.float32), pltpu.SemaphoreType.DMA((6,))],
-    )
+    spill, keep, give = kernel(
+        spill_body, [(2, 2, 18, 1, half), keep.shape, give.shape], keep, give, v_keep, v_give,
+        far=(2, 3), far_out=(1, 2),
+        scratch_shapes=[pltpu.VMEM((2, 3, TILE, half), jnp.float32), pltpu.SemaphoreType.DMA((8,))],
+    )
+    far_parts = (keep, give, v_keep, v_give)
     ahead = kernel(
         functools.partial(ahead_body, inner, rows), (3, spaces * rows, span),
         place, *windows, scalars=1,

time: 75.7 us -> 75.3 us (level)
  transfers between devices with their start and end apart: 10 -> 10, of which waited for: 6 -> 6; matrix products, arithmetic and copies ran while one was open for 0% -> 0% of each run, Pallas kernels for 25% -> 26%
where the time goes in v8:
time: 75.3 us; the launch traced here: 74.8 us
  starting transfers between devices  30.4 us (40%)
  Pallas kernels  30.1 us (40%)
  waiting for transfers between devices  13.8 us (18%)
    pallas_call x13, Pallas kernels, kernel(): pl.pallas_call(body, out_shape=outs if many else outs[0], in_specs=[smem...  30.1 us
    ppermute x1, starting transfers between devices, per_device(): other = lax.ppermute(mine, 'core', swapped)  6.58 us
    ppermute x1, waiting for transfers between devices, per_device(): prev_late = lax.ppermute(late, ('outer', 'inner', 'core'), onward)  4.7 us
    all_to_all x1, starting transfers between devices, per_device(): recv = lax.all_to_all(msgs, group, 0, 0, tiled=True)  4.67 us
    ppermute x1, starting transfers between devices, per_device(): prev = lax.ppermute(soon, ('outer', 'inner', 'core'), onward)  4.5 us
    ppermute x1, starting transfers between devices, per_device(): prev_late = lax.ppermute(late, ('outer', 'inner', 'core'), onward)  4.29 us
    all_to_all x1, starting transfers between devices, per_device(): mine = lax.all_to_all(back, group, 0, 0, tiled=True)  4.19 us
    all_to_all x1, waiting for transfers between devices, per_device(): recv = lax.all_to_all(msgs, group, 0, 0, tiled=True)  3.53 us
  transfers between devices with their start and end apart: 10, of which 6 were waited for; matrix products, arithmetic and copies ran while one was open for 0% of the time, Pallas kernels for 26%

profile of v8, /device:TPU:1, one launch (start us, length us, event | category | flops | bytes accessed | tf_op | source)
XLA Modules:
  0.0 74.8 jit_solution(4292525977032306768)
XLA Ops:
  0.0 0.1 stack.31.place
  0.1 2.2 %shard_map.38 = (f32[3,16,2304]{2,1,0:T(8,128)S(1)}, f32[3,16,2048]{2,1,0:T(8,128)S(1)}, f32[192,128]{1,0:T(8,128)S(1)}, f32[384,128]{1,0:T(8,128)S(1)}) custom-call(s32[5]{0:T(128)S(1)} %stack.31.place, f32[3,3,16,4096]{3,2,1,0:T(8,128)} %bitcast.7, f32[16,4096]{1,0:T(8,128)} %depth_far.3, f32[3,16,4096]{2,1,0:T(8,128)} %init.5), custom_call_target="tpu_custom_call" | custom-call | tf_op jit(solution)/shard_map/pallas_call | solution.py:541
  2.3 4.5 %collective-permute-start.1 = (f32[3,16,2304]{2,1,0:T(8,128)S(1)}, f32[3,16,2304]{2,1,0:T(8,128)S(1)}, u32[]{:S(2)}, u32[]{:S(2)}) collective-permute-start(f32[3,16,2304]{2,1,0:T(8,128)S(1)} %get-tuple-element.32), channel_id=1, source_target_pairs={{0,2},{2,4},{4,6},{6,8},{8,10},{10,12},{12,14},{14,16},{16,18},{18... | collective-permute-start | bytes 1327112 | tf_op jit(solution)/shard_map/ppermute | solution.py:602
  6.8 1.3 %collective-permute-start = (f32[384,128]{1,0:T(8,128)S(1)}, f32[384,128]{1,0:T(8,128)S(1)}, u32[]{:S(2)}, u32[]{:S(2)}) collective-permute-start(f32[384,128]{1,0:T(8,128)S(1)} %get-tuple-element.28), channel_id=1, source_target_pairs={{0,1},{1,0},{2,3},{3,2},{4,5},{5,4},{6,7},{7,6},{8,9},{9,8},{10,11... | collective-permute-start | bytes 589832 | tf_op jit(solution)/shard_map/ppermute | solution.py:605
  8.1 2.5 %shard_map.37 = (f32[3,16,4096]{2,1,0:T(8,128)S(1)}, f32[3,24,4096]{2,1,0:T(8,128)S(1)}, f32[24,4096]{1,0:T(8,128)S(1)}) custom-call(f32[3,3,16,4096]{3,2,1,0:T(8,128)} %bitcast.8, f32[16,4096]{1,0:T(8,128)} %depth_far.3), custom_call_target="tpu_custom_call" | custom-call | tf_op jit(solution)/shard_map/pallas_call | solution.py:541
  10.6 0.0 copy-start
  10.6 1.6 %collective-permute-done.rest_0_.rest_1_ = f32[384,128]{1,0:T(8,128)S(1)} collective-permute-done((f32[384,128]{1,0:T(8,128)S(1)}, f32[384,128]{1,0:T(8,128)S(1)}, u32[]{:S(2)}, u32[]{:S(2)}) %collective-permute-start) | collective-permute-done | bytes 196640 | tf_op jit(solution)/shard_map/ppermute | solution.py:605
  12.2 1.2 %shard_map.39 = (f32[3,24,4096]{2,1,0:T(8,128)S(1)}, f32[24,4096]{1,0:T(8,128)S(1)}) custom-call(f32[3,24,4096]{2,1,0:T(8,128)S(1)} %get-tuple-element.26.fk, f32[24,4096]{1,0:T(8,128)S(1)} %get-tuple-element.27.bare, f32[384,128]{1,0:T(8,128)S(1)} %collective-permute-done.rest_0_.rest_1_), custom_call_target="tpu_custom_call" | custom-call | tf_op jit(solution)/shard_map/pallas_call | solution.py:541
  13.4 0.0 collective-permute-done.1.prev
  13.4 0.0 copy-done
  13.4 2.3 %shard_map.40 = (f32[72,2304]{1,0:T(8,128)S(1)}, f32[72,2048]{1,0:T(8,128)S(1)}) custom-call(s32[5]{0:T(128)S(1)} %stack.31.place, f32[3,16,4096]{2,1,0:T(8,128)S(1)} %get-tuple-element.30.base, f32[3,16,4096]{2,1,0:T(8,128)S(1)} %copy-done, f32[3,24,4096]{2,1,0:T(8,128)S(1)} %get-tuple-element.26.fk, f32[3,24,4096]{2,1,0:T(8,128)S(1)} %get-tuple-element.31.ffk, ...), custom_call_target="tpu_custom_call" | custom-call | tf_op jit(solution)/shard_map/pallas_call | solution.py:541
  15.7 0.1 collective-permute-start.2
  15.8 4.3 %collective-permute-start.3 = (f32[3,16,2048]{2,1,0:T(8,128)S(1)}, f32[3,16,2048]{2,1,0:T(8,128)S(1)}, u32[]{:S(2)}, u32[]{:S(2)}) collective-permute-start(f32[3,16,2048]{2,1,0:T(8,128)S(1)} %get-tuple-element.34), channel_id=1, source_target_pairs={{0,2},{2,4},{4,6},{6,8},{8,10},{10,12},{12,14},{14,16},{16,18},{18... | collective-permute-start | bytes 1179656 | tf_op jit(solution)/shard_map/ppermute | solution.py:603
  20.1 4.7 %collective-permute-done.3.rest_0_ = f32[3,16,2048]{2,1,0:T(8,128)S(1)} collective-permute-done((f32[3,16,2048]{2,1,0:T(8,128)S(1)}, f32[3,16,2048]{2,1,0:T(8,128)S(1)}, u32[]{:S(2)}, u32[]{:S(2)}) %collective-permute-start.3) | collective-permute-done | bytes 393248 | tf_op jit(solution)/shard_map/ppermute | solution.py:603
  24.8 2.2 %shard_map.41 = (f32[72,2304]{1,0:T(8,128)S(1)}, f32[72,2048]{1,0:T(8,128)S(1)}) custom-call(s32[5]{0:T(128)S(1)} %stack.31.place, f32[3,16,4096]{2,1,0:T(8,128)S(1)} %get-tuple-element.30.base, f32[3,16,4096]{2,1,0:T(8,128)S(1)} %copy-done, f32[3,24,4096]{2,1,0:T(8,128)S(1)} %get-tuple-element.26.fk, f32[3,24,4096]{2,1,0:T(8,128)S(1)} %get-tuple-element.31.ffk, ...), custom_call_target="tpu_custom_call" | custom-call | tf_op jit(solution)/shard_map/pallas_call | solution.py:541
  27.0 0.0 collective-permute-done.2.got
  27.0 2.5 %shard_map.42 = (f32[8,168,128]{2,1,0:T(8,128)}, f32[72,2048]{1,0:T(8,128)}, f32[72,2048]{1,0:T(8,128)}) custom-call(s32[5]{0:T(128)S(1)} %stack.31.place, f32[24,4096]{1,0:T(8,128)S(1)} %get-tuple-element.29.depth_ref.refs_4_.refs_5_, f32[72,2304]{1,0:T(8,128)S(1)} %collective-permute-done.2.got, f32[72,2304]{1,0:T(8,128)S(1)} %get-tuple-element.35.keep.b_keep, ...), custom_call_target="tpu_custom_call" | custom-call | tf_op jit(solution)/shard_map/pallas_call | solution.py:541
  29.6 4.7 %all-to-all-start = ((f32[8,168,128]{2,1,0:T(8,128)}), f32[8,168,128]{2,1,0:T(8,128)S(1)}, u32[]{:S(2)}, u32[]{:S(2)}) async-start(f32[8,168,128]{2,1,0:T(8,128)} %get-tuple-element.38), calls=%async_computation | async-start | bytes 1376256 | tf_op jit(solution)/shard_map/all_to_all | solution.py:635
  34.2 2.3 %shard_map.46 = (f32[2,2,18,1,2048]{4,3,2,1,0:T(1,128)}, f32[72,2304]{1,0:T(8,128)}, f32[72,2304]{1,0:T(8,128)}) custom-call(f32[72,2304]{1,0:T(8,128)S(1)} %get-tuple-element.35.keep.b_keep, f32[72,2304]{1,0:T(8,128)S(1)} %get-tuple-element.33.b_give, f32[72,2048]{1,0:T(8,128)} %get-tuple-element.40.v_keep.refs_2_, f32[72,2048]{1,0:T(8,128)} %get-tuple-element.41.v_give.refs_3_), custom_call_target="tpu_custom_call" | custom-call | tf_op jit(solution)/shard_map/pallas_call | solution.py:541
  36.6 1.5 %collective-permute-start.6 = (f32[2,2,18,1,2048]{4,3,2,1,0:T(1,128)}, f32[2,2,18,1,2048]{4,3,2,1,0:T(1,128)S(1)}, u32[]{:S(2)}, u32[]{:S(2)}) collective-permute-start(f32[2,2,18,1,2048]{4,3,2,1,0:T(1,128)} %get-tuple-element.44), channel_id=1, source_target_pairs={{0,1},{1,0},{2,3},{3,2},{4,5},{5,4},{6,7},{7,6},{8,9},{9,8},{10,11... | collective-permute-start | bytes 1769480 | tf_op jit(solution)/shard_map/ppermute | solution.py:554
  38.1 1.6 %shard_map.43.ahead = f32[3,32,384]{2,1,0:T(8,128)S(1)} custom-call(s32[5]{0:T(128)S(1)} %stack.31.place, f32[192,128]{1,0:T(8,128)S(1)} %get-tuple-element.39.rest_0_, f32[384,128]{1,0:T(8,128)S(1)} %collective-permute-done.rest_0_.rest_1_), custom_call_target="tpu_custom_call" | custom-call | tf_op jit(solution)/shard_map/pallas_call | solution.py:541
  39.7 3.5 %all-to-all-done.recv = f32[8,168,128]{2,1,0:T(8,128)S(1)} async-done(((f32[8,168,128]{2,1,0:T(8,128)}), f32[8,168,128]{2,1,0:T(8,128)S(1)}, u32[]{:S(2)}, u32[]{:S(2)}) %all-to-all-start) | async-done | bytes 688160 | tf_op jit(solution)/shard_map/all_to_all | solution.py:635
  43.3 1.4 %shard_map.44 = f32[216,128]{1,0:T(8,128)S(1)} custom-call(s32[5]{0:T(128)S(1)} %stack.31.place, f32[8,168,128]{2,1,0:T(8,128)S(1)} %all-to-all-done.recv, f32[3,32,384]{2,1,0:T(8,128)S(1)} %shard_map.43.ahead, f32[192,128]{1,0:T(8,128)S(1)} %get-tuple-element.39.rest_0_, f32[384,128]{1,0:T(8,128)S(1)} %collective-permute-done.rest_0_.rest_1_), custom_call_target="tpu_custom_call" | custom-call | tf_op jit(solution)/shard_map/pallas_call | solution.py:541
  44.7 1.8 %collective-permute-start.4 = (f32[216,128]{1,0:T(8,128)S(1)}, f32[216,128]{1,0:T(8,128)S(1)}, u32[]{:S(2)}, u32[]{:S(2)}) collective-permute-start(f32[216,128]{1,0:T(8,128)S(1)} %shard_map.44), channel_id=1, source_target_pairs={{0,16},{1,17},{2,18},{3,19},{4,20},{5,21},{6,22},{7,23},{8,24},{9,... | collective-permute-start | bytes 331784 | tf_op jit(solution)/shard_map/ppermute | solution.py:659
  46.5 1.7 %collective-permute-done.4.carry = f32[216,128]{1,0:T(8,128)S(1)} collective-permute-done((f32[216,128]{1,0:T(8,128)S(1)}, f32[216,128]{1,0:T(8,128)S(1)}, u32[]{:S(2)}, u32[]{:S(2)}) %collective-permute-start.4) | collective-permute-done | bytes 110624 | tf_op jit(solution)/shard_map/ppermute | solution.py:659
  48.3 2.1 %shard_map.45 = f32[8,64,256]{2,1,0:T(8,128)} custom-call(s32[5]{0:T(128)S(1)} %stack.31.place, f32[8,168,128]{2,1,0:T(8,128)S(1)} %all-to-all-done.recv, f32[216,128]{1,0:T(8,128)S(1)} %collective-permute-done.4.carry, f32[192,128]{1,0:T(8,128)S(1)} %get-tuple-element.39.rest_0_, f32[384,128]{1,0:T(8,128)S(1)} %collective-permute-done.rest_0_.rest_1_), custom_call_target="tpu_custom_call" | custom-call | tf_op jit(solution)/shard_map/pallas_call | solution.py:541
  50.4 4.2 %all-to-all-start.1 = ((f32[8,64,256]{2,1,0:T(8,128)}), f32[8,64,256]{2,1,0:T(8,128)S(1)}, u32[]{:S(2)}, u32[]{:S(2)}) async-start(f32[8,64,256]{2,1,0:T(8,128)} %shard_map.45), calls=%async_computation.1 | async-start | bytes 1048576 | tf_op jit(solution)/shard_map/all_to_all | solution.py:668
  54.6 1.7 %collective-permute-done.6.refs_4_ = f32[2,2,18,1,2048]{4,3,2,1,0:T(1,128)S(1)} collective-permute-done((f32[2,2,18,1,2048]{4,3,2,1,0:T(1,128)}, f32[2,2,18,1,2048]{4,3,2,1,0:T(1,128)S(1)}, u32[]{:S(2)}, u32[]{:S(2)}) %collective-permute-start.6) | collective-permute-done | bytes 589856 | tf_op jit(solution)/shard_map/ppermute | solution.py:554
  56.3 2.8 %shard_map.47 = (f32[3,24,4096]{2,1,0:T(8,128)S(1)}, f32[3,16,4096]{2,1,0:T(8,128)}) custom-call(s32[5]{0:T(128)S(1)} %stack.31.place, f32[72,2304]{1,0:T(8,128)} %get-tuple-element.42.refs_0_, f32[72,2304]{1,0:T(8,128)} %get-tuple-element.43.refs_1_, f32[72,2048]{1,0:T(8,128)} %get-tuple-element.40.v_keep.refs_2_, ...), custom_call_target="tpu_custom_call" | custom-call | tf_op jit(solution)/shard_map/pallas_call | solution.py:541
  59.1 0.0 copy-start.1
  59.1 1.5 %collective-permute-start.7 = (f32[3,24,4096]{2,1,0:T(8,128)S(1)}, f32[3,24,4096]{2,1,0:T(8,128)S(1)}, u32[]{:S(2)}, u32[]{:S(2)}) collective-permute-start(f32[3,24,4096]{2,1,0:T(8,128)S(1)} %get-tuple-element.45.refs_1_.refs_2_), channel_id=1, source_target_pairs={{0,2},{1,3},{4,6},{5,7},{8,10},{9,11},{12,14},{13,15},{16,18},{17,... | collective-permute-start | bytes 3538952 | tf_op jit(solution)/shard_map/ppermute | solution.py:654
  60.6 0.5 all-to-all-done.1.refs_0_
  61.1 6.6 %collective-permute-start.5 = (f32[8,64,256]{2,1,0:T(8,128)S(1)}, f32[8,64,256]{2,1,0:T(8,128)S(1)}, u32[]{:S(2)}, u32[]{:S(2)}) collective-permute-start(f32[8,64,256]{2,1,0:T(8,128)S(1)} %all-to-all-done.1.refs_0_), channel_id=1, source_target_pairs={{0,2},{2,0},{1,3},{3,1},{4,6},{6,4},{5,7},{7,5},{8,10},{10,8},{9,1... | collective-permute-start | bytes 1572872 | tf_op jit(solution)/shard_map/ppermute | solution.py:671
  67.7 0.0 collective-permute-done.7.refs_2_.refs_3_
  67.7 0.0 copy-done.1
  67.7 3.2 %shard_map.48.refs_6_ = f32[3,3,16,4096]{3,2,1,0:T(8,128)} custom-call(s32[5]{0:T(128)S(1)} %stack.31.place, f32[8,64,256]{2,1,0:T(8,128)S(1)} %all-to-all-done.1.refs_0_, f32[3,24,4096]{2,1,0:T(8,128)} %copy-done.1, f32[3,24,4096]{2,1,0:T(8,128)S(1)} %collective-permute-done.7.refs_2_.refs_3_, f32[3,16,4096]{2,1,0:T(8,128)} %get-tuple-element.46.refs_3_.refs_4_, ...), custom_call_target="tpu_custom_call" | custom-call | tf_op jit(solution)/shard_map/pallas_call | solution.py:541
  70.9 0.0 collective-permute-done.5.refs_1_
  71.0 3.7 %shard_map.49 = f32[3,3,16,4096]{3,2,1,0:T(8,128)} custom-call(s32[5]{0:T(128)S(1)} %stack.31.place, f32[8,64,256]{2,1,0:T(8,128)S(1)} %all-to-all-done.1.refs_0_, f32[8,64,256]{2,1,0:T(8,128)S(1)} %collective-permute-done.5.refs_1_, f32[3,24,4096]{2,1,0:T(8,128)} %copy-done.1, ...), custom_call_target="tpu_custom_call", output_to_operand_aliasing={{}: (7, {})} | custom-call | tf_op jit(solution)/shard_map/pallas_call | solution.py:541
Async XLA Ops:
  2.3 11.1 %collective-permute-start.1 = (f32[3,16,2304]{2,1,0:T(8,128)S(1)}, f32[3,16,2304]{2,1,0:T(8,128)S(1)}, u32[]{:S(2)}, u32[]{:S(2)}) collective-permute-start(f32[3,16,2304]{2,1,0:T(8,128)S(1)} %get-tuple-element.32), channel_id=1, source_target_pairs={{0,2},{2,4},{4,6},{6,8},{8,10},{10,12},{12,14},{14,16},{16,18},{18... | collective-permute-start | bytes 1327112 | tf_op jit(solution)/shard_map/ppermute | solution.py:602
  6.8 5.4 %collective-permute-start = (f32[384,128]{1,0:T(8,128)S(1)}, f32[384,128]{1,0:T(8,128)S(1)}, u32[]{:S(2)}, u32[]{:S(2)}) collective-permute-start(f32[384,128]{1,0:T(8,128)S(1)} %get-tuple-element.28), channel_id=1, source_target_pairs={{0,1},{1,0},{2,3},{3,2},{4,5},{5,4},{6,7},{7,6},{8,9},{9,8},{10,11... | collective-permute-start | bytes 589832 | tf_op jit(solution)/shard_map/ppermute | solution.py:605
  10.6 2.8 %copy-start = (f32[3,16,4096]{2,1,0:T(8,128)S(1)}, f32[3,16,4096]{2,1,0:T(8,128)}, u32[]{:S(2)}) copy-start(f32[3,16,4096]{2,1,0:T(8,128)} %init.5) | copy-start | bytes 2359300
  15.7 11.3 %collective-permute-start.2 = (f32[72,2304]{1,0:T(8,128)S(1)}, f32[72,2304]{1,0:T(8,128)S(1)}, u32[]{:S(2)}, u32[]{:S(2)}) collective-permute-start(f32[72,2304]{1,0:T(8,128)S(1)} %get-tuple-element.33.b_give), channel_id=1, source_target_pairs={{0,2},{2,0},{1,3},{3,1},{4,6},{6,4},{5,7},{7,5},{8,10},{10,8},{9,1... | collective-permute-start | bytes 1990664 | tf_op jit(solution)/shard_map/ppermute | solution.py:626
  15.8 9.0 %collective-permute-start.3 = (f32[3,16,2048]{2,1,0:T(8,128)S(1)}, f32[3,16,2048]{2,1,0:T(8,128)S(1)}, u32[]{:S(2)}, u32[]{:S(2)}) collective-permute-start(f32[3,16,2048]{2,1,0:T(8,128)S(1)} %get-tuple-element.34), channel_id=1, source_target_pairs={{0,2},{2,4},{4,6},{6,8},{8,10},{10,12},{12,14},{14,16},{16,18},{18... | collective-permute-start | bytes 1179656 | tf_op jit(solution)/shard_map/ppermute | solution.py:603
  29.6 13.7 %all-to-all-start = ((f32[8,168,128]{2,1,0:T(8,128)}), f32[8,168,128]{2,1,0:T(8,128)S(1)}, u32[]{:S(2)}, u32[]{:S(2)}) async-start(f32[8,168,128]{2,1,0:T(8,128)} %get-tuple-element.38), calls=%async_computation | async-start | bytes 1376256 | tf_op jit(solution)/shard_map/all_to_all | solution.py:635
  36.6 19.7 %collective-permute-start.6 = (f32[2,2,18,1,2048]{4,3,2,1,0:T(1,128)}, f32[2,2,18,1,2048]{4,3,2,1,0:T(1,128)S(1)}, u32[]{:S(2)}, u32[]{:S(2)}) collective-permute-start(f32[2,2,18,1,2048]{4,3,2,1,0:T(1,128)} %get-tuple-element.44), channel_id=1, source_target_pairs={{0,1},{1,0},{2,3},{3,2},{4,5},{5,4},{6,7},{7,6},{8,9},{9,8},{10,11... | collective-permute-start | bytes 1769480 | tf_op jit(solution)/shard_map/ppermute | solution.py:554
  44.7 3.6 %collective-permute-start.4 = (f32[216,128]{1,0:T(8,128)S(1)}, f32[216,128]{1,0:T(8,128)S(1)}, u32[]{:S(2)}, u32[]{:S(2)}) collective-permute-start(f32[216,128]{1,0:T(8,128)S(1)} %shard_map.44), channel_id=1, source_target_pairs={{0,16},{1,17},{2,18},{3,19},{4,20},{5,21},{6,22},{7,23},{8,24},{9,... | collective-permute-start | bytes 331784 | tf_op jit(solution)/shard_map/ppermute | solution.py:659
  50.4 10.7 %all-to-all-start.1 = ((f32[8,64,256]{2,1,0:T(8,128)}), f32[8,64,256]{2,1,0:T(8,128)S(1)}, u32[]{:S(2)}, u32[]{:S(2)}) async-start(f32[8,64,256]{2,1,0:T(8,128)} %shard_map.45), calls=%async_computation.1 | async-start | bytes 1048576 | tf_op jit(solution)/shard_map/all_to_all | solution.py:668
  59.1 8.6 %copy-start.1 = (f32[3,24,4096]{2,1,0:T(8,128)}, f32[3,24,4096]{2,1,0:T(8,128)S(1)}, u32[]{:S(2)}) copy-start(f32[3,24,4096]{2,1,0:T(8,128)S(1)} %get-tuple-element.45.refs_1_.refs_2_) | copy-start | bytes 3538948
  59.1 8.6 %collective-permute-start.7 = (f32[3,24,4096]{2,1,0:T(8,128)S(1)}, f32[3,24,4096]{2,1,0:T(8,128)S(1)}, u32[]{:S(2)}, u32[]{:S(2)}) collective-permute-start(f32[3,24,4096]{2,1,0:T(8,128)S(1)} %get-tuple-element.45.refs_1_.refs_2_), channel_id=1, source_target_pairs={{0,2},{1,3},{4,6},{5,7},{8,10},{9,11},{12,14},{13,15},{16,18},{17,... | collective-permute-start | bytes 3538952 | tf_op jit(solution)/shard_map/ppermute | solution.py:654
  61.1 9.8 %collective-permute-start.5 = (f32[8,64,256]{2,1,0:T(8,128)S(1)}, f32[8,64,256]{2,1,0:T(8,128)S(1)}, u32[]{:S(2)}, u32[]{:S(2)}) collective-permute-start(f32[8,64,256]{2,1,0:T(8,128)S(1)} %all-to-all-done.1.refs_0_), channel_id=1, source_target_pairs={{0,2},{2,0},{1,3},{3,1},{4,6},{6,4},{5,7},{7,5},{8,10},{10,8},{9,1... | collective-permute-start | bytes 1572872 | tf_op jit(solution)/shard_map/ppermute | solution.py:671
